TPU v7x, 256 devices: a whole 4x4x8 slice. The times are simulated.
256 devices in a mesh: group: 2 (over y_hi), fsdp: 128 (over x, z, y_lo, core).
Axes of the slice: x: 4, y: 4 (y_hi: 2, y_lo: 2; y = y_hi * 2 + y_lo), z: 8, core: 2. Of those that a mesh axis runs over, the one named last changes fastest.
Arguments:
- acts: bfloat16 [2, 65536, 8192], P('group', 'fsdp'), may hold values from -24 to 24
- cotangent: bfloat16 [2, 65536, 512], P('group', 'fsdp'), may hold values from -15.3125 to 15.3125
- inner_params: float32 [2, 8192, 512], P('group', 'fsdp'), may hold values from -6 to 6
- adam_first: float32 [2, 8192, 512], P('group', 'fsdp'), may hold values from -0.018 to 0.018
- adam_second: float32 [2, 8192, 512], P('group', 'fsdp'), may hold values from 1e-06 to 0.0001
- inner_steps: int32 [2], replicated, may hold values from 8 to 128
- group_tokens: int32 [2], replicated, may hold values from 16384 to 131072
- anchor: float32 [8192, 512], P(('fsdp', 'group')), may hold values from -6 to 6
- momentum: float32 [8192, 512], P(('fsdp', 'group')), may hold values from -2 to 2
Outputs:
- new_anchor: float32 [8192, 512], P(('fsdp', 'group'))
- new_momentum: float32 [8192, 512], P(('fsdp', 'group'))
- group_weights: bfloat16 [2, 8192, 512], P('group', 'fsdp')
All inputs are finite; a program needn't handle non-finite values.
Results may differ from a plain program's by a relative error of at most 0.0004.
Values may be sent and summed in bfloat16 or wider, within the bound.
No kernel may reach another device: no remote copies, remote signals or barrier semaphores. Data moves between devices by JAX's collectives and lax.ppermute only.
A program may use at most 128 MiB of HBM per device.

v0:
```python
import jax
import jax.numpy as jnp
from jax import lax
from jax.sharding import Mesh
from jax.sharding import PartitionSpec as P

FSDP = ("fsdp_0", "fsdp_1", "fsdp_2", "fsdp_3")
FSDP_GROUP = ("fsdp_0", "fsdp_1", "fsdp_2", "fsdp_3", "group")


beta_one = 0.9
beta_two = 0.95
epsilon = 1e-08
inner_rate = 0.3
decay_rate = 0.1
outer_rate = 0.7
outer_mom = 0.9


def cut_along(shard, dim, length):
    before, after = (shard.shape[:dim], shard.shape[dim + 1 :])
    return jnp.moveaxis(shard.reshape(*before, length, -1, *after), dim, 0)


def summed_rows(shard, chips, core, dim):
    sizes = (lax.axis_size(chips), lax.axis_size(core))
    tiles = cut_along(shard, dim, sizes[0] * sizes[1])
    inside = tiles.shape[1:]
    tiles = tiles.reshape(*sizes, *inside).swapaxes(0, 1).reshape(-1, *inside)
    tiles = lax.psum_scatter(tiles, core, scatter_dimension=0, tiled=True)
    return lax.psum_scatter(tiles, chips, scatter_dimension=0, tiled=True)[0]


def copy_for_each(shard, axis):
    length = lax.axis_size(axis)
    return lax.all_to_all(
        jnp.broadcast_to(shard[None], (length, *shard.shape)), axis, 0, 0, tiled=True
    )


def of_everyone(shard, axis):
    return copy_for_each(shard, axis).sum(axis=0)


def together(arrays, axis):
    ends = [0]
    for a in arrays:
        ends.append(ends[-1] + a.size)
    so_far = of_everyone(jnp.concatenate([a.ravel() for a in arrays]), axis)
    return tuple((so_far[b:e].reshape(a.shape) for a, b, e in zip(arrays, ends, ends[1:])))


def inner_update(params, first_moment, second_moment, gradient, steps):
    fresh_first = beta_one * first_moment + (1.0 - beta_one) * gradient
    fresh_second = beta_two * second_moment + (1.0 - beta_two) * gradient * gradient
    steps_float = steps.astype(jnp.float32)
    correct_one = 1.0 - jnp.power(jnp.float32(beta_one), steps_float)
    correct_two = 1.0 - jnp.power(jnp.float32(beta_two), steps_float)
    ratio = fresh_first / correct_one / (jnp.sqrt(fresh_second / correct_two) + epsilon)
    return params - inner_rate * (ratio + decay_rate * params)


def outer_update(anchor, momentum, merged):
    pseudo = anchor - merged
    fresh_momentum = outer_mom * momentum + pseudo
    fresh_anchor = anchor - outer_rate * (pseudo + outer_mom * fresh_momentum)
    return (fresh_anchor, fresh_momentum)


def per_device(
    acts,
    cotangent,
    inner_params,
    adam_first,
    adam_second,
    inner_steps,
    group_tokens,
    anchor,
    momentum,
):
    fsdp_count = lax.axis_size(FSDP)
    group_index = lax.axis_index("group")
    inputs = acts[0]
    upstream = cotangent[0]
    row_count = inner_params.shape[1]
    group_total = inputs.shape[0] * fsdp_count
    contract = (((0,), (0,)), ((), ()))
    summed = summed_rows(
        lax.dot_general(inputs, upstream, contract, preferred_element_type=jnp.float32),
        ("fsdp_0", "fsdp_1", "fsdp_2"),
        "fsdp_3",
        0,
    )
    gradient = summed / group_total
    steps = lax.dynamic_index_in_dim(inner_steps, group_index, 0, False)
    updated = inner_update(inner_params[0], adam_first[0], adam_second[0], gradient, steps)
    counts = group_tokens.astype(jnp.float32)
    share = lax.dynamic_index_in_dim(counts, group_index, 0, False) / jnp.sum(counts)
    weighted = share * updated
    half_rows = anchor.shape[0]
    blank = jnp.zeros((row_count, anchor.shape[1]), jnp.float32)
    place = group_index * half_rows
    padded_anchor = lax.dynamic_update_slice_in_dim(blank, anchor, place, 0)
    padded_momentum = lax.dynamic_update_slice_in_dim(blank, momentum, place, 0)
    merged, full_anchor, full_momentum = together(
        (weighted, padded_anchor, padded_momentum), "group"
    )
    whole_anchor, whole_momentum = outer_update(full_anchor, full_momentum, merged)
    new_anchor = lax.dynamic_slice_in_dim(whole_anchor, place, half_rows, 0)
    new_momentum = lax.dynamic_slice_in_dim(whole_momentum, place, half_rows, 0)
    rebuilt = whole_anchor.astype(jnp.bfloat16)
    return (new_anchor, new_momentum, rebuilt[None])


def solution(mesh):
    torus = Mesh(
        mesh.devices.reshape(mesh.shape["group"], 4, 8, 2, 2),
        ("group", "fsdp_0", "fsdp_1", "fsdp_2", "fsdp_3"),
    )
    in_specs = (
        P("group", FSDP, None),
        P("group", FSDP, None),
        P("group", FSDP, None),
        P("group", FSDP, None),
        P("group", FSDP, None),
        P(),
        P(),
        P(FSDP_GROUP, None),
        P(FSDP_GROUP, None),
    )
    out_specs = (P(FSDP_GROUP, None), P(FSDP_GROUP, None), P("group", FSDP, None))
    return jax.shard_map(
        per_device, mesh=torus, in_specs=in_specs, out_specs=out_specs, check_vma=False
    )
```

profile of v0, /device:TPU:0, one launch (start us, length us, event | category | flops | bytes accessed | tf_op | source)
XLA Modules:
  0.0 430.1 jit_solution(276848921162435200)
XLA Ops:
  7.2 0.0 copy-start
  7.2 0.0 reduce-scatter.3.cloned.1.call-start
  7.2 12.0 %copy.17 = bf16[1,512,8192]{1,2,0:T(8,128)(2,1)} copy(bf16[1,512,8192]{2,1,0:T(8,128)(2,1)} %param.9) | data formatting | bytes 16777216 | tf_op args[0]
  19.3 0.0 copy-done
  19.3 8.0 %convolution_bitcast_fusion = f32[2,64,64,512]{3,2,0,1:T(8,128)S(1)} fusion(bf16[64,2,64,512]{3,2,1,0:T(8,128)(2,1)} %bitcast.31, bf16[1,512,512]{2,1,0:T(8,128)(2,1)S(1)} %copy-done), kind=kOutput, calls=%fused_computation | convolution fusion | flops 4294967296 | bytes 25690112 | tf_op jit(solution)/shard_map/dot_general | solution.py:89
  27.3 6.2 %copy.18 = f32[2,64,64,512]{3,2,1,0:T(8,128)} copy(f32[2,64,64,512]{3,2,0,1:T(8,128)S(1)} %convolution_bitcast_fusion) | data formatting | bytes 33554432 | tf_op jit(solution)/shard_map/transpose | solution.py:29
  33.5 0.0 reduce-scatter.3.cloned.1.call-update
  33.5 0.0 copy-start.6
  33.5 0.0 copy-start.7
  33.5 0.0 copy-start.1
  33.6 0.0 copy-start.4
  33.6 0.0 copy-start.5
  33.6 0.0 copy-start.2
  33.6 0.0 copy-start.3
  33.6 0.0 reduce-scatter.5.cloned.1.call-start
  33.7 32.1 %reduce-scatter.3.cloned.1.call-done = f32[64,64,512]{2,1,0:T(8,128)} async-done(((f32[128,64,512]{2,1,0:T(8,128)}), f32[64,64,512]{2,1,0:T(8,128)}) %reduce-scatter.3.cloned.1.call-update) | async-done | bytes 8388624 | tf_op jit(solution)/shard_map/reduce_scatter | solution.py:30
  65.7 0.0 reduce-scatter.5.cloned.1.call-update
  65.7 0.0 copy-done.6
  65.7 0.6 dynamic_slice.15
  67.1 0.0 copy-done.7
  67.1 0.6 dynamic_slice.14
  67.7 0.0 copy-done.1
  67.7 0.0 copy-done.4
  67.8 0.0 copy-done.5
  67.9 0.6 convert_reduce_fusion
  69.8 335.4 %reduce-scatter.5.cloned.1.call-done = f32[1,64,512]{2,1,0:T(8,128)} async-done(((f32[64,64,512]{2,1,0:T(8,128)}), f32[1,64,512]{2,1,0:T(8,128)}) %reduce-scatter.5.cloned.1.call-update) | async-done | bytes 131088 | tf_op jit(solution)/shard_map/reduce_scatter | solution.py:31
  405.1 0.0 copy-done.2
  405.1 0.0 copy-done.3
  405.2 1.0 divide_bitcast_fusion
  406.3 0.4 broadcast_in_dim.13
  406.7 14.0 %all_to_all.6 = f32[2,1,98304]{2,1,0:T(1,128)S(1)} all-to-all(f32[2,1,98304]{2,1,0:T(1,128)S(1)} %broadcast_in_dim.13), channel_id=1, replica_groups=mesh['group'=2,'fsdp_0'=4,'fsdp_1'=8,'fsdp_2'=2,'fsdp_3'=2] {'group'}, dimensions={0} | all-to-all | bytes 1572864 | tf_op jit(solution)/shard_map/all_to_all | solution.py:36
  420.7 1.1 reduce_sum.19
  421.9 0.7 convert_bitcast_fusion
  422.6 0.7 constant_dynamic-slice_fusion
  (15 shorter events, 0.4 us)
Async XLA Ops:
  7.2 12.1 %copy-start = (bf16[1,512,512]{2,1,0:T(8,128)(2,1)S(1)}, bf16[1,512,512]{2,1,0:T(8,128)(2,1)}, u32[]{:S(2)}) copy-start(bf16[1,512,512]{2,1,0:T(8,128)(2,1)} %param.10) | copy-start | bytes 1572868
  7.2 58.5 %reduce-scatter.3.cloned.1.call-start = ((), (), s32[]{:S(2)}) async-start(), calls=%async_computation.3 | async-start | bytes 25165824 | tf_op jit(solution)/shard_map/reduce_scatter | solution.py:30
  33.5 32.2 %copy-start.6 = (s32[2]{0:T(128)S(1)}, s32[2]{0:T(128)}, u32[]{:S(2)}) copy-start(s32[2]{0:T(128)} %param.14) | copy-start | bytes 28
  33.5 33.5 %copy-start.7 = (s32[2]{0:T(128)S(1)}, s32[2]{0:T(128)}, u32[]{:S(2)}) copy-start(s32[2]{0:T(128)} %param.15) | copy-start | bytes 28
  33.5 34.1 %copy-start.1 = (f32[1,64,512]{2,1,0:T(8,128)S(1)}, f32[1,64,512]{2,1,0:T(8,128)}, u32[]{:S(2)}) copy-start(f32[1,64,512]{2,1,0:T(8,128)} %param.11) | copy-start | bytes 393220
  33.6 34.2 %copy-start.4 = (f32[32,512]{1,0:T(8,128)S(1)}, f32[32,512]{1,0:T(8,128)}, u32[]{:S(2)}) copy-start(f32[32,512]{1,0:T(8,128)} %param.16) | copy-start | bytes 196612
  33.6 34.3 %copy-start.5 = (f32[32,512]{1,0:T(8,128)S(1)}, f32[32,512]{1,0:T(8,128)}, u32[]{:S(2)}) copy-start(f32[32,512]{1,0:T(8,128)} %param.17) | copy-start | bytes 196612
  33.6 371.6 %copy-start.2 = (f32[1,64,512]{2,1,0:T(8,128)S(1)}, f32[1,64,512]{2,1,0:T(8,128)}, u32[]{:S(2)}) copy-start(f32[1,64,512]{2,1,0:T(8,128)} %param.13) | copy-start | bytes 393220
  33.6 371.6 %copy-start.3 = (f32[1,64,512]{2,1,0:T(8,128)S(1)}, f32[1,64,512]{2,1,0:T(8,128)}, u32[]{:S(2)}) copy-start(f32[1,64,512]{2,1,0:T(8,128)} %param.12) | copy-start | bytes 393220
  33.6 371.5 %reduce-scatter.5.cloned.1.call-start = ((), (), s32[]{:S(2)}) async-start(), calls=%async_computation.4 | async-start | bytes 8519680 | tf_op jit(solution)/shard_map/reduce_scatter | solution.py:31
Sparse Core Ops, SparseCore 0:
  33.6 32.0 reduce-scatter.2
  68.2 336.8 reduce-scatter.4
where the time goes:
time: 431 us; the launch traced here: 430 us
  waiting for transfers between devices  367 us (85%)
  local copies, waits for them, and re-layouts  20.8 us (5%)
  between operations  16.3 us (4%)
  blocking collectives  14 us (3%)
  matrix products  8.01 us (2%)
    reduce_scatter x1, waiting for transfers between devices, summed_rows(): return lax.psum_scatter(tiles, chips, scatter_dimension=0, tiled=True)[0]  335 us
    reduce_scatter x1, waiting for transfers between devices, summed_rows(): tiles = lax.psum_scatter(tiles, core, scatter_dimension=0, tiled=True)  32.1 us
    all_to_all x1, blocking collectives, copy_for_each(): lax.all_to_all(jnp.broadcast_to(shard[None], (length, *shard.shape)), axi...  14 us
    unnamed x21, local copies, waits for them, and re-layouts  12.2 us
  transfers between devices with their start and end apart: 2, of which 2 were waited for; matrix products, arithmetic and copies ran while one was open for 0% of the time, Pallas kernels for 0%

commit v1 on v0

v1 whole, which is shorter than its diff:
```python
import functools

import jax
import jax.numpy as jnp
from jax import lax
from jax.experimental import pallas as pl
from jax.experimental.pallas import tpu as pltpu
from jax.sharding import Mesh
from jax.sharding import PartitionSpec as P

FSDP = ("x", "z", "y", "c")
FSDP_GROUP = ("x", "z", "y", "c", "group")
NX, NZ, NY, NC, NG = 4, 8, 2, 2, 2

beta_one = 0.9
beta_two = 0.95
epsilon = 1e-08
inner_rate = 0.3
decay_rate = 0.1
outer_rate = 0.7
outer_mom = 0.9

WIRE = jnp.float16
F32 = jnp.float32
PEAK = 128.0
ROWS_A = 176
LANES = 128
BLOCK = 1024


def swap(a, axis):
    return lax.ppermute(a, axis, [(0, 1), (1, 0)])


def around(a, axis, k, size):
    return lax.ppermute(a, axis, [(i, (i + k) % size) for i in range(size)])


def pick(a, i):
    return lax.dynamic_index_in_dim(a, i, 0, False)


def terms_kernel(scale, which, cot, acts, out_a, out_b, turned):
    @pl.when(pl.program_id(0) == 0)
    def _():
        turned[...] = cot[...].astype(F32).T.astype(cot.dtype)

    out = jnp.dot(turned[...], acts[...], preferred_element_type=F32) * scale
    for j in range(BLOCK // LANES):
        z, y = divmod(j, NY)
        piece = out[:, j * LANES : (j + 1) * LANES]
        out_a[0, z, y] = piece[:ROWS_A]
        out_b[z, 0, y] = piece[ROWS_A:]


def terms(inputs, upstream, which):
    tokens, width = inputs.shape
    half = upstream.shape[1] // NC
    zs = BLOCK // (LANES * NY)
    per = NZ // zs
    rows_b = half - ROWS_A
    return pl.pallas_call(
        functools.partial(terms_kernel, PEAK / (tokens * NC)),
        grid_spec=pltpu.PrefetchScalarGridSpec(
            num_scalar_prefetch=1,
            grid=(width // BLOCK,),
            in_specs=[
                pl.BlockSpec((tokens, half), lambda i, w: (0, w[0])),
                pl.BlockSpec((tokens, BLOCK), lambda i, w: (0, i)),
            ],
            out_specs=[
                pl.BlockSpec(
                    (1, zs, NY, ROWS_A, LANES),
                    lambda i, w: (i // per, i % per, 0, 0, 0),
                ),
                pl.BlockSpec(
                    (zs, 1, NY, rows_b, LANES),
                    lambda i, w: (i % per, i // per, 0, 0, 0),
                ),
            ],
            scratch_shapes=[pltpu.VMEM((half, tokens), inputs.dtype)],
        ),
        out_shape=[
            jax.ShapeDtypeStruct((NX, NZ, NY, ROWS_A, LANES), F32),
            jax.ShapeDtypeStruct((NZ, NX, NY, rows_b, LANES), F32),
        ],
        cost_estimate=pl.CostEstimate(
            flops=2 * tokens * half * width,
            bytes_accessed=2 * tokens * width + 4 * half * width,
            transcendentals=0,
        ),
        name="terms",
    )(which[None], upstream, inputs)


def turn_kernel(first, second, out):
    rows = LANES // NC
    for y in range(NY):
        whole = jnp.concatenate([first[y], second[y]], 0).T
        for c in range(NC):
            for g in range(NG):
                out[(g * NY + y) * NC + c] = whole[c * rows : (c + 1) * rows]


def final_kernel(
    group, facts, got, p0, m0, v0, p1, m1, v1, a0, a1, w0, w1, new_a, new_m, new_w
):
    mine = group[0] == 0

    def weighted(first, k, p, m, v):
        at = [(g * NY + y) * NC for g in range(NG) for y in range(NY)]
        sides = []
        for c in range(NC):
            zero = got[at[0] + c] + got[at[1] + c]
            one = got[at[2] + c] + got[at[3] + c]
            sides.append(jnp.where(mine == first, zero, one))
        gradient = jnp.concatenate(sides, -1) * (1.0 / (NY * PEAK))
        share, correct_one, correct_two = (facts[3 * k + n] for n in range(3))
        fresh_first = beta_one * m + (1.0 - beta_one) * gradient
        fresh_second = beta_two * v + (1.0 - beta_two) * gradient * gradient
        ratio = (
            fresh_first / correct_one / (jnp.sqrt(fresh_second / correct_two) + epsilon)
        )
        return share * (p - inner_rate * (ratio + decay_rate * p))

    merged = weighted(True, 0, p0[...], m0[...], v0[...]) + weighted(
        False, 1, p1[...], m1[...], v1[...]
    )
    few = a0.shape[0]

    def half(anchor, momentum, part):
        pseudo = anchor - part
        fresh_momentum = outer_mom * momentum + pseudo
        fresh_anchor = anchor - outer_rate * (pseudo + outer_mom * fresh_momentum)
        return fresh_anchor, fresh_momentum

    front, back = merged[:few], merged[few:]
    near_anchor, near_momentum = half(a0[...], w0[...], jnp.where(mine, front, back))
    far_anchor, _ = half(a1[...], w1[...], jnp.where(mine, back, front))
    new_a[...] = near_anchor
    new_m[...] = near_momentum
    new_w[:few] = jnp.where(mine, near_anchor, far_anchor).astype(new_w.dtype)
    new_w[few:] = jnp.where(mine, far_anchor, near_anchor).astype(new_w.dtype)


def per_device(
    acts,
    cotangent,
    inner_params,
    adam_first,
    adam_second,
    inner_steps,
    group_tokens,
    anchor,
    momentum,
):
    group, x, z, core = (lax.axis_index(a) for a in ("group", "x", "z", "c"))
    inputs = acts[0]
    upstream = cotangent[0]
    half = upstream.shape[1] // NC
    rows = inner_params.shape[1]

    theirs_a, theirs_b = terms(inputs, upstream, 1 - core)
    with jax.named_scope("core"):
        got_a = swap(theirs_a, "c")
        got_b = swap(theirs_b, "c")
    near = (inner_params[0], adam_first[0], adam_second[0], anchor, momentum)
    gated, inputs, upstream, _ = lax.optimization_barrier(
        (near, inputs, upstream, theirs_a)
    )
    with jax.named_scope("state"):
        far = tuple(swap(a, "group") for a in gated)
    own_a, own_b = terms(inputs, upstream, core)

    def chip_a(i):
        return pick(own_a, i) + pick(got_a, i)

    with jax.named_scope("xa"):
        sent = [
            around(chip_a((x + k) % NX).astype(WIRE), "x", k, NX) for k in (2, 1, 3)
        ]
    second = own_b + got_b
    with jax.named_scope("zb"):
        back = lax.all_to_all(second.astype(WIRE), "z", 0, 0, tiled=True)
    first = chip_a(x)
    sent, back = lax.optimization_barrier((sent, back))
    place = lax.broadcasted_iota(jnp.int32, (NZ, 1, 1, 1, 1), 0)
    back = jnp.where(place == z, 0.0, back.astype(F32)).sum(0) + pick(second, z)
    second = back * (1.0 / NZ)
    with jax.named_scope("xb"):
        sent_b = [
            around(pick(second, (x + k) % NX).astype(WIRE), "x", k, NX)
            for k in (2, 1, 3)
        ]
    second = pick(second, x)

    for s in sent:
        first = first + s.astype(F32)
    first = first * (1.0 / NX)
    with jax.named_scope("za"):
        back = lax.all_to_all(first.astype(WIRE), "z", 0, 0, tiled=True)
    sent_b, back = lax.optimization_barrier((sent_b, back))
    place = lax.broadcasted_iota(jnp.int32, (NZ, 1, 1, 1), 0)
    first = jnp.where(place == z, 0.0, back.astype(F32)).sum(0) + pick(first, z)
    first = first * (1.0 / NZ)
    for s in sent_b:
        second = second + s.astype(F32)
    second = second * (1.0 / NX)

    part = pl.pallas_call(
        turn_kernel,
        out_shape=jax.ShapeDtypeStruct((NG * NY * NC, rows, half), F32),
        name="turn",
    )(first, second)
    with jax.named_scope("last"):
        got = lax.all_to_all(part, ("group", "y", "c"), 0, 0, tiled=True)

    counts = group_tokens.astype(F32)
    steps = inner_steps.astype(F32)
    facts = jnp.stack(
        [
            counts / jnp.sum(counts),
            1.0 - jnp.power(F32(beta_one), steps),
            1.0 - jnp.power(F32(beta_two), steps),
        ],
        1,
    )
    facts = jnp.where(group == 0, facts, facts[::-1]).reshape(-1)
    vmem = pl.BlockSpec(memory_space=pltpu.VMEM)
    smem = pl.BlockSpec(memory_space=pltpu.SMEM)
    new_anchor, new_momentum, weights = pl.pallas_call(
        final_kernel,
        in_specs=[smem, smem] + [vmem] * 11,
        out_specs=[vmem] * 3,
        out_shape=[
            jax.ShapeDtypeStruct(anchor.shape, F32),
            jax.ShapeDtypeStruct(anchor.shape, F32),
            jax.ShapeDtypeStruct((rows, anchor.shape[1]), jnp.bfloat16),
        ],
        name="final",
    )(
        group[None],
        facts,
        got,
        *near[:3],
        *far[:3],
        near[3],
        far[3],
        near[4],
        far[4],
    )
    return new_anchor, new_momentum, weights[None]


def solution(mesh):
    torus = Mesh(
        mesh.devices.reshape(NG, NX, NZ, NY, NC), ("group", "x", "z", "y", "c")
    )
    shard = P("group", FSDP, None)
    thin = P(FSDP_GROUP, None)
    return jax.shard_map(
        per_device,
        mesh=torus,
        in_specs=(shard, shard, shard, shard, shard, P(), P(), thin, thin),
        out_specs=(thin, thin, shard),
        check_vma=False,
    )
```

time: 431 us -> 133 us (0.31)
  the two profiles are of different devices: /device:TPU:0 before, /device:TPU:1 now
where the time goes in v1:
time: 133 us; the launch traced here: 132 us
  waiting for transfers between devices  45.6 us (34%)
  starting transfers between devices  40.3 us (30%)
  Pallas kernels  25.4 us (19%)
  other arithmetic  17.1 us (13%)
  local copies, waits for them, and re-layouts  2.52 us (2%)
    all_to_all x1, waiting for transfers between devices, per_device(): back = lax.all_to_all(second.astype(WIRE), 'z', 0, 0, tiled=True)  25.4 us
    pallas_call x2, Pallas kernels, terms(): pl.pallas_call(functools.partial(terms_kernel, PEAK / (tokens * NC)), gri...  21.2 us
    ppermute x7, starting transfers between devices, swap(): return lax.ppermute(a, axis, [(0, 1), (1, 0)])  12.1 us
    all_to_all x1, starting transfers between devices, per_device(): got = lax.all_to_all(part, ('group', 'y', 'c'), 0, 0, tiled=True)  8.02 us
    all_to_all x1, waiting for transfers between devices, per_device(): got = lax.all_to_all(part, ('group', 'y', 'c'), 0, 0, tiled=True)  7.78 us
    ppermute x6, starting transfers between devices, around(): return lax.ppermute(a, axis, [(i, (i + k) % size) for i in range(size)])  7.21 us
    all_to_all x1, starting transfers between devices, per_device(): back = lax.all_to_all(first.astype(WIRE), 'z', 0, 0, tiled=True)  6.48 us
    all_to_all x1, starting transfers between devices, per_device(): back = lax.all_to_all(second.astype(WIRE), 'z', 0, 0, tiled=True)  6.48 us
  transfers between devices with their start and end apart: 16, of which 5 were waited for; matrix products, arithmetic and copies ran while one was open for 11% of the time, Pallas kernels for 9%

profile of v1, /device:TPU:1, one launch (start us, length us, event | category | flops | bytes accessed | tf_op | source)
XLA Modules:
  0.0 131.7 jit_solution(12593673447537274901)
XLA Ops:
  0.6 10.6 %terms.2 = (f32[4,8,2,176,128]{4,3,2,1,0:T(8,128)}, f32[8,4,2,80,128]{4,3,2,1,0:T(8,128)}) custom-call(s32[1]{0:T(128)} %bitcast.10.which, bf16[512,512]{1,0:T(8,128)(2,1)} %bitcast.54, bf16[512,8192]{1,0:T(8,128)(2,1)} %bitcast.52), custom_call_target="tpu_custom_call" | custom-call | flops 2147483648 | bytes 16777216 | tf_op jit(solution)/shard_map/terms/pallas_call | solution.py:62
  11.2 3.2 %collective-permute-start = (f32[4,8,2,176,128]{4,3,2,1,0:T(8,128)}, f32[4,8,2,176,128]{4,3,2,1,0:T(8,128)}, u32[]{:S(2)}, u32[]{:S(2)}) collective-permute-start(f32[4,8,2,176,128]{4,3,2,1,0:T(8,128)} %get-tuple-element.25), channel_id=1, source_target_pairs={{0,1},{1,0},{2,3},{3,2},{4,5},{5,4},{6,7},{7,6},{8,9},{9,8},{10,11... | collective-permute-start | bytes 17301512 | tf_op jit(solution)/shard_map/core/ppermute | solution.py:32
  14.4 0.0 collective-permute-start.4
  14.4 10.6 %terms.3 = (f32[4,8,2,176,128]{4,3,2,1,0:T(8,128)}, f32[8,4,2,80,128]{4,3,2,1,0:T(8,128)}) custom-call(s32[1]{0:T(128)} %bitcast.4.which, bf16[512,512]{1,0:T(8,128)(2,1)} %bitcast.55, bf16[512,8192]{1,0:T(8,128)(2,1)} %bitcast.53), custom_call_target="tpu_custom_call" | custom-call | flops 2147483648 | bytes 16777216 | tf_op jit(solution)/shard_map/terms/pallas_call | solution.py:62
  25.0 2.4 %collective-permute-done.4 = f32[8,4,2,80,128]{4,3,2,1,0:T(8,128)S(1)} collective-permute-done((f32[8,4,2,80,128]{4,3,2,1,0:T(8,128)}, f32[8,4,2,80,128]{4,3,2,1,0:T(8,128)S(1)}, u32[]{:S(2)}, u32[]{:S(2)}) %collective-permute-start.4) | collective-permute-done | bytes 2621472 | tf_op jit(solution)/shard_map/core/ppermute | solution.py:32
  27.4 4.1 %fusion.16 = (f16[8,4,2,80,128]{4,3,2,1,0:T(8,128)(2,1)}, f32[8,4,2,80,128]{4,3,2,1,0:T(8,128)}) fusion(f32[8,4,2,80,128]{4,3,2,1,0:T(8,128)} %get-tuple-element.29, f32[8,4,2,80,128]{4,3,2,1,0:T(8,128)S(1)} %collective-permute-done.4), kind=kLoop, calls=%fused_computation.34 | loop fusion | flops 1310720 | bytes 9175040 | tf_op jit(solution)/shard_map/zb/convert_element_type | solution.py:184
  31.5 6.5 %all-to-all-start = ((f16[8,4,2,80,128]{4,3,2,1,0:T(8,128)(2,1)}), f16[8,4,2,80,128]{4,3,2,1,0:T(8,128)(2,1)S(1)}, u32[]{:S(2)}, u32[]{:S(2)}) async-start(f16[8,4,2,80,128]{4,3,2,1,0:T(8,128)(2,1)} %get-tuple-element.49), calls=%async_computation | async-start | bytes 2621440 | tf_op jit(solution)/shard_map/zb/all_to_all | solution.py:184
  38.0 0.0 collective-permute-done
  38.0 5.2 %fusion.5 = (f16[8,2,176,128]{3,2,1,0:T(8,128)(2,1)}, f16[8,2,176,128]{3,2,1,0:T(8,128)(2,1)}, f16[8,2,176,128]{3,2,1,0:T(8,128)(2,1)S(1)}) fusion(f32[4,8,2,176,128]{4,3,2,1,0:T(8,128)} %collective-permute-done, s32[]{:T(128)S(6)} %select_n.72, f32[4,8,2,176,128]{4,3,2,1,0:T(8,128)} %get-tuple-element.28, s32[]{:T(128)S(6)} %select_n.70, s32[]{:T(128)S(6)} %select_n.68), kind=kLoop, calls=%fused_computation.11 | loop fusion | flops 2162688 | bytes 10813452 | tf_op jit(solution)/shard_map/xa/convert_element_type | solution.py:180
  43.2 2.5 %collective-permute-start.3 = (f16[8,2,176,128]{3,2,1,0:T(8,128)(2,1)}, f16[8,2,176,128]{3,2,1,0:T(8,128)(2,1)S(1)}, u32[]{:S(2)}, u32[]{:S(2)}) collective-permute-start(f16[8,2,176,128]{3,2,1,0:T(8,128)(2,1)} %get-tuple-element.51), channel_id=1, source_target_pairs={{0,96},{32,0},{64,32},{96,64},{1,97},{33,1},{65,33},{97,65},{2,98}... | collective-permute-start | bytes 2162696 | tf_op jit(solution)/shard_map/xa/ppermute | solution.py:36
  45.7 1.7 %collective-permute-start.1 = (f16[8,2,176,128]{3,2,1,0:T(8,128)(2,1)S(1)}, f16[8,2,176,128]{3,2,1,0:T(8,128)(2,1)}, u32[]{:S(2)}, u32[]{:S(2)}) collective-permute-start(f16[8,2,176,128]{3,2,1,0:T(8,128)(2,1)S(1)} %get-tuple-element.53), channel_id=1, source_target_pairs={{0,64},{32,96},{64,0},{96,32},{1,65},{33,97},{65,1},{97,33},{2,66}... | collective-permute-start | bytes 2162696 | tf_op jit(solution)/shard_map/xa/ppermute | solution.py:36
  47.4 25.4 %all-to-all-done = f16[8,4,2,80,128]{4,3,2,1,0:T(8,128)(2,1)S(1)} async-done(((f16[8,4,2,80,128]{4,3,2,1,0:T(8,128)(2,1)}), f16[8,4,2,80,128]{4,3,2,1,0:T(8,128)(2,1)S(1)}, u32[]{:S(2)}, u32[]{:S(2)}) %all-to-all-start) | async-done | bytes 1310752 | tf_op jit(solution)/shard_map/zb/all_to_all | solution.py:184
  72.8 0.9 copy-done.1
  73.7 4.8 %collective-permute-done.1 = f16[8,2,176,128]{3,2,1,0:T(8,128)(2,1)} collective-permute-done((f16[8,2,176,128]{3,2,1,0:T(8,128)(2,1)S(1)}, f16[8,2,176,128]{3,2,1,0:T(8,128)(2,1)}, u32[]{:S(2)}, u32[]{:S(2)}) %collective-permute-start.1) | collective-permute-done | bytes 720928 | tf_op jit(solution)/shard_map/xa/ppermute | solution.py:36
  78.5 3.6 %fusion.14 = (f16[8,2,176,128]{3,2,1,0:T(8,128)(2,1)}, f32[8,2,176,128]{3,2,1,0:T(8,128)S(1)}) fusion(f16[8,2,176,128]{3,2,1,0:T(8,128)(2,1)S(1)} %collective-permute-done.3, f16[8,2,176,128]{3,2,1,0:T(8,128)(2,1)} %copy-done.1, f16[8,2,176,128]{3,2,1,0:T(8,128)(2,1)} %collective-permute-done.1, f32[4,8,2,176,128]{4,3,2,1,0:T(8,128)} %collective-permute-done, ...), kind=kLoop, calls=%fused_computation.33 | loop fusion | flops 3244032 | bytes 7208964 | tf_op jit(solution)/shard_map/za/convert_element_type | solution.py:201
  82.1 6.5 %all-to-all-start.1 = ((f16[8,2,176,128]{3,2,1,0:T(8,128)(2,1)}), f16[8,2,176,128]{3,2,1,0:T(8,128)(2,1)S(1)}, u32[]{:S(2)}, u32[]{:S(2)}) async-start(f16[8,2,176,128]{3,2,1,0:T(8,128)(2,1)} %get-tuple-element.47), calls=%async_computation.1 | async-start | bytes 1441792 | tf_op jit(solution)/shard_map/za/all_to_all | solution.py:201
  88.6 3.0 %collective-permute-start.11 = (f32[32,512]{1,0:T(8,128)S(1)}, f32[32,512]{1,0:T(8,128)}, u32[]{:S(2)}, u32[]{:S(2)}) collective-permute-start(f32[32,512]{1,0:T(8,128)S(1)} %copy-done.5), channel_id=1, source_target_pairs={{0,128},{128,0},{1,129},{129,1},{2,130},{130,2},{3,131},{131,3},{4... | collective-permute-start | bytes 196616 | tf_op jit(solution)/shard_map/state/ppermute | solution.py:32
  91.6 0.1 collective-permute-start.12
  91.7 0.3 select_reduce_fusion
  92.0 1.0 fusion.6
  93.1 0.1 collective-permute-start.7
  93.2 1.5 %collective-permute-start.6 = (f16[2,80,128]{2,1,0:T(8,128)(2,1)S(1)}, f16[2,80,128]{2,1,0:T(8,128)(2,1)S(1)}, u32[]{:S(2)}, u32[]{:S(2)}) collective-permute-start(f16[2,80,128]{2,1,0:T(8,128)(2,1)S(1)} %get-tuple-element.55), channel_id=1, source_target_pairs={{0,32},{32,64},{64,96},{96,0},{1,33},{33,65},{65,97},{97,1},{2,34}... | collective-permute-start | bytes 122888 | tf_op jit(solution)/shard_map/xb/ppermute | solution.py:36
  94.6 1.5 %collective-permute-start.5 = (f16[2,80,128]{2,1,0:T(8,128)(2,1)S(1)}, f16[2,80,128]{2,1,0:T(8,128)(2,1)S(1)}, u32[]{:S(2)}, u32[]{:S(2)}) collective-permute-start(f16[2,80,128]{2,1,0:T(8,128)(2,1)S(1)} %get-tuple-element.56), channel_id=1, source_target_pairs={{0,64},{32,96},{64,0},{96,32},{1,65},{33,97},{65,1},{97,33},{2,66}... | collective-permute-start | bytes 122888 | tf_op jit(solution)/shard_map/xb/ppermute | solution.py:36
  96.1 0.6 convert_reduce_fusion
  96.7 0.0 collective-permute-done.7
  96.7 2.9 %collective-permute-start.8 = (f32[64,512]{1,0:T(8,128)}, f32[64,512]{1,0:T(8,128)S(1)}, u32[]{:S(2)}, u32[]{:S(2)}) collective-permute-start(f32[64,512]{1,0:T(8,128)} %bitcast.56), channel_id=1, source_target_pairs={{0,128},{128,0},{1,129},{129,1},{2,130},{130,2},{3,131},{131,3},{4... | collective-permute-start | bytes 393224 | tf_op jit(solution)/shard_map/state/ppermute | solution.py:32
  99.6 0.0 collective-permute-done.6
  99.6 0.8 collective-permute-start.9
  100.4 0.0 collective-permute-done.5
  100.4 2.1 %collective-permute-start.10 = (f32[64,512]{1,0:T(8,128)}, f32[64,512]{1,0:T(8,128)S(1)}, u32[]{:S(2)}, u32[]{:S(2)}) collective-permute-start(f32[64,512]{1,0:T(8,128)} %bitcast.60), channel_id=1, source_target_pairs={{0,128},{128,0},{1,129},{129,1},{2,130},{130,2},{3,131},{131,3},{4... | collective-permute-start | bytes 393224 | tf_op jit(solution)/shard_map/state/ppermute | solution.py:32
  102.5 5.2 %all-to-all-done.1 = f16[8,2,176,128]{3,2,1,0:T(8,128)(2,1)S(1)} async-done(((f16[8,2,176,128]{3,2,1,0:T(8,128)(2,1)}), f16[8,2,176,128]{3,2,1,0:T(8,128)(2,1)S(1)}, u32[]{:S(2)}, u32[]{:S(2)}) %all-to-all-start.1) | async-done | bytes 720928 | tf_op jit(solution)/shard_map/za/all_to_all | solution.py:201
  107.7 0.2 select_reduce_fusion.1
  107.9 0.0 copy-start.6
  107.9 0.7 fusion.7.first
  108.6 0.7 fusion.10.second
  109.3 1.9 %turn.1 = f32[8,64,256]{2,1,0:T(8,128)} custom-call(f32[2,176,128]{2,1,0:T(8,128)} %fusion.7.first, f32[2,80,128]{2,1,0:T(8,128)} %fusion.10.second), custom_call_target="tpu_custom_call" | custom-call | tf_op jit(solution)/shard_map/turn/pallas_call | solution.py:210
  111.2 8.0 %all-to-all-start.2 = ((f32[8,64,256]{2,1,0:T(8,128)}), f32[8,64,256]{2,1,0:T(8,128)S(1)}, u32[]{:S(2)}, u32[]{:S(2)}) async-start(f32[8,64,256]{2,1,0:T(8,128)} %turn.1), calls=%async_computation.2 | async-start | bytes 1048576 | tf_op jit(solution)/shard_map/last/all_to_all | solution.py:216
  119.2 0.7 subtract_bitcast_fusion.1
  119.9 0.1 rev.3
  120.0 0.1 copy.12
  120.1 0.6 reshape.29.facts
  120.7 0.0 collective-permute-done.11.a1
  120.7 0.0 collective-permute-done.12.w1
  120.7 0.0 collective-permute-done.8.p1
  120.8 0.0 collective-permute-done.10.v1
  120.8 7.8 %all-to-all-done.2.got = f32[8,64,256]{2,1,0:T(8,128)S(1)} async-done(((f32[8,64,256]{2,1,0:T(8,128)}), f32[8,64,256]{2,1,0:T(8,128)S(1)}, u32[]{:S(2)}, u32[]{:S(2)}) %all-to-all-start.2) | async-done | bytes 524320 | tf_op jit(solution)/shard_map/last/all_to_all | solution.py:216
  128.6 0.8 copy-done
  129.4 2.4 %final.1 = (f32[32,512]{1,0:T(8,128)}, f32[32,512]{1,0:T(8,128)}, bf16[64,512]{1,0:T(8,128)(2,1)}) custom-call(s32[1]{0:T(128)} %bitcast.group, f32[6]{0:T(128)} %reshape.29.facts, f32[8,64,256]{2,1,0:T(8,128)} %copy-done, f32[64,512]{1,0:T(8,128)} %bitcast.57, f32[64,512]{1,0:T(8,128)} %bitcast.59, f32[64,512]{1,0:T(8,128)} %bitcast.61, ...), custom_call_target="tpu_custom_call" | custom-call | tf_op jit(solution)/shard_map/final/pallas_call | solution.py:231
  (21 shorter events, 0.1 us)
Async XLA Ops:
  11.2 26.8 %collective-permute-start = (f32[4,8,2,176,128]{4,3,2,1,0:T(8,128)}, f32[4,8,2,176,128]{4,3,2,1,0:T(8,128)}, u32[]{:S(2)}, u32[]{:S(2)}) collective-permute-start(f32[4,8,2,176,128]{4,3,2,1,0:T(8,128)} %get-tuple-element.25), channel_id=1, source_target_pairs={{0,1},{1,0},{2,3},{3,2},{4,5},{5,4},{6,7},{7,6},{8,9},{9,8},{10,11... | collective-permute-start | bytes 17301512 | tf_op jit(solution)/shard_map/core/ppermute | solution.py:32
  14.4 13.0 %collective-permute-start.4 = (f32[8,4,2,80,128]{4,3,2,1,0:T(8,128)}, f32[8,4,2,80,128]{4,3,2,1,0:T(8,128)S(1)}, u32[]{:S(2)}, u32[]{:S(2)}) collective-permute-start(f32[8,4,2,80,128]{4,3,2,1,0:T(8,128)} %get-tuple-element.30), channel_id=1, source_target_pairs={{0,1},{1,0},{2,3},{3,2},{4,5},{5,4},{6,7},{7,6},{8,9},{9,8},{10,11... | collective-permute-start | bytes 7864328 | tf_op jit(solution)/shard_map/core/ppermute | solution.py:32
  31.5 41.3 %all-to-all-start = ((f16[8,4,2,80,128]{4,3,2,1,0:T(8,128)(2,1)}), f16[8,4,2,80,128]{4,3,2,1,0:T(8,128)(2,1)S(1)}, u32[]{:S(2)}, u32[]{:S(2)}) async-start(f16[8,4,2,80,128]{4,3,2,1,0:T(8,128)(2,1)} %get-tuple-element.49), calls=%async_computation | async-start | bytes 2621440 | tf_op jit(solution)/shard_map/zb/all_to_all | solution.py:184
  43.2 29.6 %collective-permute-start.3 = (f16[8,2,176,128]{3,2,1,0:T(8,128)(2,1)}, f16[8,2,176,128]{3,2,1,0:T(8,128)(2,1)S(1)}, u32[]{:S(2)}, u32[]{:S(2)}) collective-permute-start(f16[8,2,176,128]{3,2,1,0:T(8,128)(2,1)} %get-tuple-element.51), channel_id=1, source_target_pairs={{0,96},{32,0},{64,32},{96,64},{1,97},{33,1},{65,33},{97,65},{2,98}... | collective-permute-start | bytes 2162696 | tf_op jit(solution)/shard_map/xa/ppermute | solution.py:36
  45.6 27.1 %collective-permute-start.2 = (f16[8,2,176,128]{3,2,1,0:T(8,128)(2,1)}, f16[8,2,176,128]{3,2,1,0:T(8,128)(2,1)S(1)}, u32[]{:S(2)}, u32[]{:S(2)}) collective-permute-start(f16[8,2,176,128]{3,2,1,0:T(8,128)(2,1)} %get-tuple-element.52), channel_id=1, source_target_pairs={{0,32},{32,64},{64,96},{96,0},{1,33},{33,65},{65,97},{97,1},{2,34}... | collective-permute-start | bytes 2162696 | tf_op jit(solution)/shard_map/xa/ppermute | solution.py:36
  45.7 32.8 %collective-permute-start.1 = (f16[8,2,176,128]{3,2,1,0:T(8,128)(2,1)S(1)}, f16[8,2,176,128]{3,2,1,0:T(8,128)(2,1)}, u32[]{:S(2)}, u32[]{:S(2)}) collective-permute-start(f16[8,2,176,128]{3,2,1,0:T(8,128)(2,1)S(1)} %get-tuple-element.53), channel_id=1, source_target_pairs={{0,64},{32,96},{64,0},{96,32},{1,65},{33,97},{65,1},{97,33},{2,66}... | collective-permute-start | bytes 2162696 | tf_op jit(solution)/shard_map/xa/ppermute | solution.py:36
  72.8 0.9 copy-start.1
  82.1 6.5 %copy-start.5 = (f32[32,512]{1,0:T(8,128)S(1)}, f32[32,512]{1,0:T(8,128)}, u32[]{:S(2)}) copy-start(f32[32,512]{1,0:T(8,128)} %a0.1) | copy-start | bytes 196612
  82.1 25.6 %all-to-all-start.1 = ((f16[8,2,176,128]{3,2,1,0:T(8,128)(2,1)}), f16[8,2,176,128]{3,2,1,0:T(8,128)(2,1)S(1)}, u32[]{:S(2)}, u32[]{:S(2)}) async-start(f16[8,2,176,128]{3,2,1,0:T(8,128)(2,1)} %get-tuple-element.47), calls=%async_computation.1 | async-start | bytes 1441792 | tf_op jit(solution)/shard_map/za/all_to_all | solution.py:201
  88.6 32.2 %collective-permute-start.11 = (f32[32,512]{1,0:T(8,128)S(1)}, f32[32,512]{1,0:T(8,128)}, u32[]{:S(2)}, u32[]{:S(2)}) collective-permute-start(f32[32,512]{1,0:T(8,128)S(1)} %copy-done.5), channel_id=1, source_target_pairs={{0,128},{128,0},{1,129},{129,1},{2,130},{130,2},{3,131},{131,3},{4... | collective-permute-start | bytes 196616 | tf_op jit(solution)/shard_map/state/ppermute | solution.py:32
  91.6 29.2 %collective-permute-start.12 = (f32[32,512]{1,0:T(8,128)}, f32[32,512]{1,0:T(8,128)}, u32[]{:S(2)}, u32[]{:S(2)}) collective-permute-start(f32[32,512]{1,0:T(8,128)} %w0.1), channel_id=1, source_target_pairs={{0,128},{128,0},{1,129},{129,1},{2,130},{130,2},{3,131},{131,3},{4... | collective-permute-start | bytes 196616 | tf_op jit(solution)/shard_map/state/ppermute | solution.py:32
  91.7 4.4 %copy-start.7 = (s32[2]{0:T(128)S(1)}, s32[2]{0:T(128)}, u32[]{:S(2)}) copy-start(s32[2]{0:T(128)} %param.15) | copy-start | bytes 28
  93.1 3.6 %collective-permute-start.7 = (f16[2,80,128]{2,1,0:T(8,128)(2,1)S(1)}, f16[2,80,128]{2,1,0:T(8,128)(2,1)S(1)}, u32[]{:S(2)}, u32[]{:S(2)}) collective-permute-start(f16[2,80,128]{2,1,0:T(8,128)(2,1)S(1)} %get-tuple-element.54), channel_id=1, source_target_pairs={{0,96},{32,0},{64,32},{96,64},{1,97},{33,1},{65,33},{97,65},{2,98}... | collective-permute-start | bytes 122888 | tf_op jit(solution)/shard_map/xb/ppermute | solution.py:36
  93.2 6.4 %collective-permute-start.6 = (f16[2,80,128]{2,1,0:T(8,128)(2,1)S(1)}, f16[2,80,128]{2,1,0:T(8,128)(2,1)S(1)}, u32[]{:S(2)}, u32[]{:S(2)}) collective-permute-start(f16[2,80,128]{2,1,0:T(8,128)(2,1)S(1)} %get-tuple-element.55), channel_id=1, source_target_pairs={{0,32},{32,64},{64,96},{96,0},{1,33},{33,65},{65,97},{97,1},{2,34}... | collective-permute-start | bytes 122888 | tf_op jit(solution)/shard_map/xb/ppermute | solution.py:36
  94.6 5.8 %collective-permute-start.5 = (f16[2,80,128]{2,1,0:T(8,128)(2,1)S(1)}, f16[2,80,128]{2,1,0:T(8,128)(2,1)S(1)}, u32[]{:S(2)}, u32[]{:S(2)}) collective-permute-start(f16[2,80,128]{2,1,0:T(8,128)(2,1)S(1)} %get-tuple-element.56), channel_id=1, source_target_pairs={{0,64},{32,96},{64,0},{96,32},{1,65},{33,97},{65,1},{97,33},{2,66}... | collective-permute-start | bytes 122888 | tf_op jit(solution)/shard_map/xb/ppermute | solution.py:36
  96.7 24.0 %collective-permute-start.8 = (f32[64,512]{1,0:T(8,128)}, f32[64,512]{1,0:T(8,128)S(1)}, u32[]{:S(2)}, u32[]{:S(2)}) collective-permute-start(f32[64,512]{1,0:T(8,128)} %bitcast.56), channel_id=1, source_target_pairs={{0,128},{128,0},{1,129},{129,1},{2,130},{130,2},{3,131},{131,3},{4... | collective-permute-start | bytes 393224 | tf_op jit(solution)/shard_map/state/ppermute | solution.py:32
  99.6 21.2 %collective-permute-start.9 = (f32[64,512]{1,0:T(8,128)}, f32[64,512]{1,0:T(8,128)S(1)}, u32[]{:S(2)}, u32[]{:S(2)}) collective-permute-start(f32[64,512]{1,0:T(8,128)} %bitcast.58), channel_id=1, source_target_pairs={{0,128},{128,0},{1,129},{129,1},{2,130},{130,2},{3,131},{131,3},{4... | collective-permute-start | bytes 393224 | tf_op jit(solution)/shard_map/state/ppermute | solution.py:32
  100.4 20.4 %collective-permute-start.10 = (f32[64,512]{1,0:T(8,128)}, f32[64,512]{1,0:T(8,128)S(1)}, u32[]{:S(2)}, u32[]{:S(2)}) collective-permute-start(f32[64,512]{1,0:T(8,128)} %bitcast.60), channel_id=1, source_target_pairs={{0,128},{128,0},{1,129},{129,1},{2,130},{130,2},{3,131},{131,3},{4... | collective-permute-start | bytes 393224 | tf_op jit(solution)/shard_map/state/ppermute | solution.py:32
  107.9 11.3 %copy-start.6 = (s32[2]{0:T(128)S(1)}, s32[2]{0:T(128)}, u32[]{:S(2)}) copy-start(s32[2]{0:T(128)} %param.14) | copy-start | bytes 28
  111.2 17.4 %all-to-all-start.2 = ((f32[8,64,256]{2,1,0:T(8,128)}), f32[8,64,256]{2,1,0:T(8,128)S(1)}, u32[]{:S(2)}, u32[]{:S(2)}) async-start(f32[8,64,256]{2,1,0:T(8,128)} %turn.1), calls=%async_computation.2 | async-start | bytes 1048576 | tf_op jit(solution)/shard_map/last/all_to_all | solution.py:216
  120.7 7.8 %copy-start.2 = (f32[64,512]{1,0:T(8,128)}, f32[64,512]{1,0:T(8,128)S(1)}, u32[]{:S(2)}) copy-start(f32[64,512]{1,0:T(8,128)S(1)} %collective-permute-done.8.p1) | copy-start | bytes 393220
  120.8 7.8 %copy-start.3 = (f32[64,512]{1,0:T(8,128)}, f32[64,512]{1,0:T(8,128)S(1)}, u32[]{:S(2)}) copy-start(f32[64,512]{1,0:T(8,128)S(1)} %collective-permute-done.9.m1) | copy-start | bytes 393220
  120.8 7.8 %copy-start.4 = (f32[64,512]{1,0:T(8,128)}, f32[64,512]{1,0:T(8,128)S(1)}, u32[]{:S(2)}) copy-start(f32[64,512]{1,0:T(8,128)S(1)} %collective-permute-done.10.v1) | copy-start | bytes 393220
  128.6 0.8 copy-start

commit v2 on v1

v2 whole, which is shorter than its diff:
```python
import functools

import jax
import jax.numpy as jnp
from jax import lax
from jax.experimental import pallas as pl
from jax.experimental.pallas import tpu as pltpu
from jax.sharding import Mesh
from jax.sharding import PartitionSpec as P

FSDP = ("x", "z", "y", "c")
FSDP_GROUP = ("x", "z", "y", "c", "group")
NX, NZ, NY, NC, NG = 4, 8, 2, 2, 2

beta_one = 0.9
beta_two = 0.95
epsilon = 1e-08
inner_rate = 0.3
decay_rate = 0.1
outer_rate = 0.7
outer_mom = 0.9

WIRE = jnp.float16
F32 = jnp.float32
PEAK = 128.0
ROWS_A = 192
LANES = 128
BLOCK = 1024
ORDER = (2, 1, 3, 0)


def swap(a, axis):
    return lax.ppermute(a, axis, [(0, 1), (1, 0)])


def around(a, axis, k, size):
    return lax.ppermute(a, axis, [(i, (i + k) % size) for i in range(size)])


def pick(a, i):
    return lax.dynamic_index_in_dim(a, i, 0, False)


def terms_kernel(scale, which, place, cot, acts, *refs):
    outs, out_b = refs[:NX], refs[NX]
    turned, held, arrived = refs[NX + 1 :]
    step = pl.program_id(0)
    steps = acts.shape[1] // BLOCK
    per = steps // NX

    def copy(i):
        x = lax.rem(place[0] + ORDER[i // per], NX)
        start = pl.multiple_of((x * per + i % per) * BLOCK, BLOCK)
        return pltpu.make_async_copy(
            acts.at[:, pl.ds(start, BLOCK)], held.at[i], arrived.at[i]
        )

    @pl.when(step == 0)
    def _():
        for i in range(steps):
            copy(i).start()
        turned[...] = cot[...].astype(F32).T.astype(cot.dtype)

    for i in range(steps):

        @pl.when(step == i)
        def _():
            copy(i).wait()
            out = jnp.dot(turned[...], held[i], preferred_element_type=F32) * scale
            for j in range(BLOCK // LANES):
                z, y = divmod(j, NY)
                piece = out[:, j * LANES : (j + 1) * LANES]
                outs[i // per][z, y] = piece[:ROWS_A]
                out_b[z, 0, y] = piece[ROWS_A:]


def terms(inputs, upstream, which, x):
    tokens, width = inputs.shape
    half = upstream.shape[1] // NC
    zs = BLOCK // (LANES * NY)
    per = NZ // zs
    steps = width // BLOCK
    rows_b = half - ROWS_A

    def at(n):
        return lambda i, w, x: (jnp.clip(i - n * per, 0, per - 1), 0, 0, 0)

    return pl.pallas_call(
        functools.partial(terms_kernel, PEAK / (tokens * NC)),
        grid_spec=pltpu.PrefetchScalarGridSpec(
            num_scalar_prefetch=2,
            grid=(steps,),
            in_specs=[
                pl.BlockSpec((tokens, half), lambda i, w, x: (0, w[0])),
                pl.BlockSpec(memory_space=pl.ANY),
            ],
            out_specs=[
                pl.BlockSpec((zs, NY, ROWS_A, LANES), at(n)) for n in range(NX)
            ]
            + [
                pl.BlockSpec(
                    (zs, 1, NY, rows_b, LANES),
                    lambda i, w, x: (i % per, i // per, 0, 0, 0),
                ),
            ],
            scratch_shapes=[
                pltpu.VMEM((half, tokens), inputs.dtype),
                pltpu.VMEM((steps, tokens, BLOCK), inputs.dtype),
                pltpu.SemaphoreType.DMA((steps,)),
            ],
        ),
        out_shape=[jax.ShapeDtypeStruct((NZ, NY, ROWS_A, LANES), F32)] * NX
        + [jax.ShapeDtypeStruct((NZ, NX, NY, rows_b, LANES), F32)],
        cost_estimate=pl.CostEstimate(
            flops=2 * tokens * half * width,
            bytes_accessed=2 * tokens * width + 4 * half * width,
            transcendentals=0,
        ),
        name="terms",
    )(which[None], x[None], upstream, inputs)


def turn_kernel(first, second, out):
    rows = LANES // NC
    for y in range(NY):
        whole = jnp.concatenate([first[y], second[y]], 0).T
        for c in range(NC):
            for g in range(NG):
                out[(g * NY + y) * NC + c] = whole[c * rows : (c + 1) * rows]


def pack_kernel(*refs):
    at = 0
    for ref in refs[:-1]:
        refs[-1][at : at + ref.shape[0]] = ref[...]
        at += ref.shape[0]


def final_kernel(group, facts, got, p0, m0, v0, a0, w0, far, new_a, new_m, new_w):
    rows, few = p0.shape[0], a0.shape[0]
    p1, m1, v1 = (far[i * rows : (i + 1) * rows] for i in range(3))
    a1, w1 = far[3 * rows : 3 * rows + few], far[3 * rows + few :]
    mine = group[0] == 0

    def weighted(first, k, p, m, v):
        at = [(g * NY + y) * NC for g in range(NG) for y in range(NY)]
        sides = []
        for c in range(NC):
            zero = got[at[0] + c] + got[at[1] + c]
            one = got[at[2] + c] + got[at[3] + c]
            sides.append(jnp.where(mine == first, zero, one))
        gradient = jnp.concatenate(sides, -1) * (1.0 / (NY * PEAK))
        share, correct_one, correct_two = (facts[3 * k + n] for n in range(3))
        fresh_first = beta_one * m + (1.0 - beta_one) * gradient
        fresh_second = beta_two * v + (1.0 - beta_two) * gradient * gradient
        ratio = (
            fresh_first / correct_one / (jnp.sqrt(fresh_second / correct_two) + epsilon)
        )
        return share * (p - inner_rate * (ratio + decay_rate * p))

    merged = weighted(True, 0, p0[...], m0[...], v0[...]) + weighted(
        False, 1, p1, m1, v1
    )

    def half(anchor, momentum, part):
        pseudo = anchor - part
        fresh_momentum = outer_mom * momentum + pseudo
        fresh_anchor = anchor - outer_rate * (pseudo + outer_mom * fresh_momentum)
        return fresh_anchor, fresh_momentum

    front, back = merged[:few], merged[few:]
    near_anchor, near_momentum = half(a0[...], w0[...], jnp.where(mine, front, back))
    far_anchor, _ = half(a1, w1, jnp.where(mine, back, front))
    new_a[...] = near_anchor
    new_m[...] = near_momentum
    new_w[:few] = jnp.where(mine, near_anchor, far_anchor).astype(new_w.dtype)
    new_w[few:] = jnp.where(mine, far_anchor, near_anchor).astype(new_w.dtype)


def per_device(
    acts,
    cotangent,
    inner_params,
    adam_first,
    adam_second,
    inner_steps,
    group_tokens,
    anchor,
    momentum,
):
    group, x, z, core = (lax.axis_index(a) for a in ("group", "x", "z", "c"))
    inputs = acts[0]
    upstream = cotangent[0]
    half = upstream.shape[1] // NC
    rows = inner_params.shape[1]

    *theirs_a, theirs_b = terms(inputs, upstream, 1 - core, x)
    got_a = [swap(a, "c") for a in theirs_a]
    got_b = swap(theirs_b, "c")
    inputs, upstream, _ = lax.optimization_barrier((inputs, upstream, theirs_b))
    *own_a, own_b = terms(inputs, upstream, core, x)
    counts = group_tokens.astype(F32)
    steps = inner_steps.astype(F32)
    facts = jnp.stack(
        [
            counts / jnp.sum(counts),
            1.0 - jnp.power(F32(beta_one), steps),
            1.0 - jnp.power(F32(beta_two), steps),
        ],
        1,
    )
    facts = jnp.where(group == 0, facts, facts[::-1]).reshape(-1)

    def wire_a(n):
        return (own_a[n] + got_a[n]).astype(WIRE)

    near = (inner_params[0], adam_first[0], adam_second[0], anchor, momentum)

    def send_a(n):
        return around(wire, "x", ORDER[n], NX)

    wire = wire_a(0)
    sent = [send_a(0)]
    _, own_b, got_b = lax.optimization_barrier((wire, own_b, got_b))
    wire = wire_b = (own_b + got_b).astype(WIRE)
    back = lax.all_to_all(wire_b, "z", 0, 0, tiled=True)
    for n in range(1, NX - 1):
        _, own_a[n], got_a[n] = lax.optimization_barrier((wire, own_a[n], got_a[n]))
        wire = wire_a(n)
        sent.append(send_a(n))
    gated, _ = lax.optimization_barrier((near, wire))
    packed = pl.pallas_call(
        pack_kernel,
        out_shape=jax.ShapeDtypeStruct(
            (sum(a.shape[0] for a in near), near[0].shape[1]), F32
        ),
        name="pack",
    )(*gated)
    far = swap(packed, "group")
    first = own_a[-1] + got_a[-1]
    second = pick(own_b, z) + pick(got_b, z)
    sent, back, far, facts = lax.optimization_barrier((sent, back, far, facts))
    place = lax.broadcasted_iota(jnp.int32, (NZ, 1, 1, 1, 1), 0)
    second = jnp.where(place == z, 0.0, back.astype(F32)).sum(0) + second
    second = second * (1.0 / NZ)
    sent_b = [around(second[n].astype(WIRE), "x", ORDER[n], NX) for n in range(NX - 1)]
    second = second[-1]

    for s in sent:
        first = first + s.astype(F32)
    first = first * (1.0 / NX)
    back = lax.all_to_all(first.astype(WIRE), "z", 0, 0, tiled=True)
    sent_b, back = lax.optimization_barrier((sent_b, back))
    place = lax.broadcasted_iota(jnp.int32, (NZ, 1, 1, 1), 0)
    first = jnp.where(place == z, 0.0, back.astype(F32)).sum(0) + pick(first, z)
    first = first * (1.0 / NZ)
    for s in sent_b:
        second = second + s.astype(F32)
    second = second * (1.0 / NX)

    part = pl.pallas_call(
        turn_kernel,
        out_shape=jax.ShapeDtypeStruct((NG * NY * NC, rows, half), F32),
        name="turn",
    )(first, second)
    got = lax.all_to_all(part, ("group", "y", "c"), 0, 0, tiled=True)

    vmem = pl.BlockSpec(memory_space=pltpu.VMEM)
    smem = pl.BlockSpec(memory_space=pltpu.SMEM)
    new_anchor, new_momentum, weights = pl.pallas_call(
        final_kernel,
        in_specs=[smem, smem] + [vmem] * 7,
        out_specs=[vmem] * 3,
        out_shape=[
            jax.ShapeDtypeStruct(anchor.shape, F32),
            jax.ShapeDtypeStruct(anchor.shape, F32),
            jax.ShapeDtypeStruct((rows, anchor.shape[1]), jnp.bfloat16),
        ],
        name="final",
    )(group[None], facts, got, *near, far)
    return new_anchor, new_momentum, weights[None]


def solution(mesh):
    torus = Mesh(
        mesh.devices.reshape(NG, NX, NZ, NY, NC), ("group", "x", "z", "y", "c")
    )
    shard = P("group", FSDP, None)
    thin = P(FSDP_GROUP, None)

    return jax.shard_map(
        per_device,
        mesh=torus,
        in_specs=(shard, shard, shard, shard, shard, P(), P(), thin, thin),
        out_specs=(thin, thin, shard),
        check_vma=False,
    )
```

time: 133 us -> 129 us (0.970)
  blocking collectives: 0 us -> 14.4 us
  starting transfers between devices: 40.3 us -> 29.4 us
  waiting for transfers between devices: 45.6 us -> 39 us
    all_to_all x2 -> x1, waiting for transfers between devices: 33.2 us -> 0.01 us  [per_device(): back = lax.all_to_all(wire_b, 'z', 0, 0, tiled=True)]
    all_to_all x0 -> x1, blocking collectives: none -> 14.4 us  [per_device(): got = lax.all_to_all(part, ('group', 'y', 'c'), 0, 0, tiled=True)]
    ppermute x6, waiting for transfers between devices: 4.8 us -> 18 us  [around(): return lax.ppermute(a, axis, [(i, (i + k) % size) for i in range(size)])]
    all_to_all x1, waiting for transfers between devices: 5.17 us -> 14.9 us  [per_device(): back = lax.all_to_all(first.astype(WIRE), 'z', 0, 0, tiled=True)]
    all_to_all x2 -> x1, starting transfers between devices: 14.5 us -> 6.48 us  [per_device(): back = lax.all_to_all(wire_b, 'z', 0, 0, tiled=True)]
    ppermute x7 -> x6, starting transfers between devices: 12.1 us -> 7.5 us  [swap(): return lax.ppermute(a, axis, [(0, 1), (1, 0)])]
    ppermute x7 -> x6, waiting for transfers between devices: 2.43 us -> 6.11 us  [swap(): return lax.ppermute(a, axis, [(0, 1), (1, 0)])]
    pallas_call x2, Pallas kernels: 21.2 us -> 19 us  [terms(): pl.pallas_call(functools.partial(terms_kernel, PEAK / (tokens * NC)), gri...]
  transfers between devices with their start and end apart: 16 -> 14, of which waited for: 5 -> 7; matrix products, arithmetic and copies ran while one was open for 11% -> 10% of each run, Pallas kernels for 9% -> 9%
where the time goes in v2:
time: 129 us
  waiting for transfers between devices  39 us (30%)
  starting transfers between devices  29.4 us (23%)
  Pallas kernels  25.1 us (19%)
  other arithmetic  17.6 us (14%)
  blocking collectives  14.4 us (11%)
  local copies, waits for them, and re-layouts  2.31 us (2%)
    pallas_call x2, Pallas kernels, terms(): pl.pallas_call(functools.partial(terms_kernel, PEAK / (tokens * NC)), gri...  19 us
    ppermute x6, waiting for transfers between devices, around(): return lax.ppermute(a, axis, [(i, (i + k) % size) for i in range(size)])  18 us
    all_to_all x1, waiting for transfers between devices, per_device(): back = lax.all_to_all(first.astype(WIRE), 'z', 0, 0, tiled=True)  14.9 us
    all_to_all x1, blocking collectives, per_device(): got = lax.all_to_all(part, ('group', 'y', 'c'), 0, 0, tiled=True)  14.4 us
    ppermute x6, starting transfers between devices, around(): return lax.ppermute(a, axis, [(i, (i + k) % size) for i in range(size)])  8.49 us
    convert_element_type x3, other arithmetic, wire_a(): return (own_a[n] + got_a[n]).astype(WIRE)  7.86 us
    ppermute x6, starting transfers between devices, swap(): return lax.ppermute(a, axis, [(0, 1), (1, 0)])  7.5 us
    all_to_all x1, starting transfers between devices, per_device(): back = lax.all_to_all(first.astype(WIRE), 'z', 0, 0, tiled=True)  6.93 us
  transfers between devices with their start and end apart: 14, of which 7 were waited for; matrix products, arithmetic and copies ran while one was open for 10% of the time, Pallas kernels for 9%

profile of v2, /device:TPU:1, one launch (start us, length us, event | category | flops | bytes accessed | tf_op | source)
XLA Modules:
  0.0 128.6 jit_solution(6945007301632890086)
XLA Ops:
  0.6 9.6 %terms.2 = (f32[8,2,192,128]{3,2,1,0:T(8,128)}, f32[8,2,192,128]{3,2,1,0:T(8,128)}, f32[8,2,192,128]{3,2,1,0:T(8,128)}, f32[8,2,192,128]{3,2,1,0:T(8,128)}, f32[8,4,2,64,128]{4,3,2,1,0:T(8,128)}) custom-call(s32[1]{0:T(128)} %bitcast.5.which, s32[1]{0:T(128)} %bitcast.2.place, bf16[512,512]{1,0:T(8,128)(2,1)} %bitcast.43, bf16[512,8192]{1,0:T(8,128)(2,1)} %bitcast.41), custom_call_target="tpu_custom_call" | custom-call | flops 2147483648 | bytes 16777216 | tf_op jit(solution)/shard_map/terms/pallas_call | solution.py:88
  10.3 3.3 %collective-permute-start.2 = (f32[8,4,2,64,128]{4,3,2,1,0:T(8,128)}, f32[8,4,2,64,128]{4,3,2,1,0:T(8,128)S(1)}, u32[]{:S(2)}, u32[]{:S(2)}) collective-permute-start(f32[8,4,2,64,128]{4,3,2,1,0:T(8,128)} %get-tuple-element.39), channel_id=1, source_target_pairs={{0,1},{1,0},{2,3},{3,2},{4,5},{5,4},{6,7},{7,6},{8,9},{9,8},{10,11... | collective-permute-start | bytes 6291464 | tf_op jit(solution)/shard_map/ppermute | solution.py:33
  13.5 0.1 collective-permute-start
  13.6 0.4 collective-permute-start.3
  14.1 0.1 collective-permute-start.5
  14.2 9.4 %terms.3 = (f32[8,2,192,128]{3,2,1,0:T(8,128)}, f32[8,2,192,128]{3,2,1,0:T(8,128)}, f32[8,2,192,128]{3,2,1,0:T(8,128)}, f32[8,2,192,128]{3,2,1,0:T(8,128)}, f32[8,4,2,64,128]{4,3,2,1,0:T(8,128)}) custom-call(s32[1]{0:T(128)} %bitcast.1.which, s32[1]{0:T(128)} %bitcast.2.place, bf16[512,512]{1,0:T(8,128)(2,1)} %bitcast.44, bf16[512,8192]{1,0:T(8,128)(2,1)} %bitcast.42), custom_call_target="tpu_custom_call" | custom-call | flops 2147483648 | bytes 16777216 | tf_op jit(solution)/shard_map/terms/pallas_call | solution.py:88
  23.5 0.0 collective-permute-done
  23.5 2.2 %add_convert_fusion.3 = f16[8,2,192,128]{3,2,1,0:T(8,128)(2,1)S(1)} fusion(f32[8,2,192,128]{3,2,1,0:T(8,128)} %get-tuple-element.42, f32[8,2,192,128]{3,2,1,0:T(8,128)} %collective-permute-done), kind=kLoop, calls=%fused_computation.6 | loop fusion | flops 786432 | bytes 3932160 | tf_op jit(solution)/shard_map/convert_element_type | solution.py:215
  25.8 0.0 collective-permute-done.2
  25.8 0.3 copy-done.1
  26.1 1.4 %add_convert_fusion = f16[8,4,2,64,128]{4,3,2,1,0:T(8,128)(2,1)} fusion(f32[8,4,2,64,128]{4,3,2,1,0:T(8,128)S(1)} %copy-done.1, f32[8,4,2,64,128]{4,3,2,1,0:T(8,128)S(1)} %collective-permute-done.2), kind=kLoop, calls=%fused_computation.1 | loop fusion | flops 1048576 | bytes 5242880 | tf_op jit(solution)/shard_map/convert_element_type | solution.py:225
  27.5 6.5 %all-to-all-start = ((f16[8,4,2,64,128]{4,3,2,1,0:T(8,128)(2,1)}), f16[8,4,2,64,128]{4,3,2,1,0:T(8,128)(2,1)S(1)}, u32[]{:S(2)}, u32[]{:S(2)}) async-start(f16[8,4,2,64,128]{4,3,2,1,0:T(8,128)(2,1)} %add_convert_fusion), calls=%async_computation | async-start | bytes 2097152 | tf_op jit(solution)/shard_map/all_to_all | solution.py:226
  34.0 0.7 collective-permute-start.11
  34.7 2.7 %collective-permute-start.1 = (f16[8,2,192,128]{3,2,1,0:T(8,128)(2,1)S(1)}, f16[8,2,192,128]{3,2,1,0:T(8,128)(2,1)}, u32[]{:S(2)}, u32[]{:S(2)}) collective-permute-start(f16[8,2,192,128]{3,2,1,0:T(8,128)(2,1)S(1)} %add_convert_fusion.3), channel_id=1, source_target_pairs={{0,64},{32,96},{64,0},{96,32},{1,65},{33,97},{65,1},{97,33},{2,66}... | collective-permute-start | bytes 2359304 | tf_op jit(solution)/shard_map/ppermute | solution.py:37
  37.4 3.1 %add_convert_fusion.2 = f16[8,2,192,128]{3,2,1,0:T(8,128)(2,1)} fusion(f32[8,2,192,128]{3,2,1,0:T(8,128)} %get-tuple-element.49, f32[8,2,192,128]{3,2,1,0:T(8,128)} %collective-permute-done.3), kind=kLoop, calls=%fused_computation.5 | loop fusion | flops 786432 | bytes 3932160 | tf_op jit(solution)/shard_map/convert_element_type | solution.py:215
  40.5 0.0 collective-permute-done.5
  40.5 0.0 copy-start.4
  40.5 2.5 %add_convert_fusion.1 = f16[8,2,192,128]{3,2,1,0:T(8,128)(2,1)} fusion(f32[8,2,192,128]{3,2,1,0:T(8,128)S(1)} %copy-done.2, f32[8,2,192,128]{3,2,1,0:T(8,128)} %collective-permute-done.5), kind=kLoop, calls=%fused_computation.4 | loop fusion | flops 786432 | bytes 3932160 | tf_op jit(solution)/shard_map/convert_element_type | solution.py:215
  43.1 0.9 collective-permute-start.6
  43.9 0.6 collective-permute-start.4
  44.6 0.6 convert_reduce_fusion
  45.2 1.9 %pack.1 = f32[256,512]{1,0:T(8,128)} custom-call(f32[64,512]{1,0:T(8,128)} %bitcast.45, f32[64,512]{1,0:T(8,128)} %bitcast.47, f32[64,512]{1,0:T(8,128)} %bitcast.49, f32[32,512]{1,0:T(8,128)} %a0.1, f32[32,512]{1,0:T(8,128)} %w0.1), custom_call_target="tpu_custom_call" | custom-call | tf_op jit(solution)/shard_map/pack/pallas_call | solution.py:232
  47.1 2.9 %collective-permute-start.7 = (f32[256,512]{1,0:T(8,128)}, f32[256,512]{1,0:T(8,128)}, u32[]{:S(2)}, u32[]{:S(2)}) collective-permute-start(f32[256,512]{1,0:T(8,128)} %pack.1), channel_id=1, source_target_pairs={{0,128},{128,0},{1,129},{129,1},{2,130},{130,2},{3,131},{131,3},{4... | collective-permute-start | bytes 1572872 | tf_op jit(solution)/shard_map/ppermute | solution.py:33
  50.0 0.7 subtract_bitcast_fusion.1
  50.7 0.1 rev.3
  50.8 0.1 copy.12
  50.9 0.6 reshape.23.facts
  51.5 3.9 %collective-permute-done.1 = f16[8,2,192,128]{3,2,1,0:T(8,128)(2,1)} collective-permute-done((f16[8,2,192,128]{3,2,1,0:T(8,128)(2,1)S(1)}, f16[8,2,192,128]{3,2,1,0:T(8,128)(2,1)}, u32[]{:S(2)}, u32[]{:S(2)}) %collective-permute-start.1) | collective-permute-done | bytes 786464 | tf_op jit(solution)/shard_map/ppermute | solution.py:37
  55.3 6.1 %collective-permute-done.7.far = f32[256,512]{1,0:T(8,128)} collective-permute-done((f32[256,512]{1,0:T(8,128)}, f32[256,512]{1,0:T(8,128)}, u32[]{:S(2)}, u32[]{:S(2)}) %collective-permute-start.7) | collective-permute-done | bytes 524320 | tf_op jit(solution)/shard_map/ppermute | solution.py:33
  61.4 10.8 %collective-permute-done.6 = f16[8,2,192,128]{3,2,1,0:T(8,128)(2,1)} collective-permute-done((f16[8,2,192,128]{3,2,1,0:T(8,128)(2,1)}, f16[8,2,192,128]{3,2,1,0:T(8,128)(2,1)}, u32[]{:S(2)}, u32[]{:S(2)}) %collective-permute-start.6) | collective-permute-done | bytes 786464 | tf_op jit(solution)/shard_map/ppermute | solution.py:37
  72.3 0.3 collective-permute-done.4
  72.6 1.2 copy-done.3
  73.8 4.1 %fusion.6 = (f16[8,2,192,128]{3,2,1,0:T(8,128)(2,1)}, f32[8,2,192,128]{3,2,1,0:T(8,128)S(1)}) fusion(f16[8,2,192,128]{3,2,1,0:T(8,128)(2,1)} %collective-permute-done.6, f16[8,2,192,128]{3,2,1,0:T(8,128)(2,1)} %collective-permute-done.4, f16[8,2,192,128]{3,2,1,0:T(8,128)(2,1)} %collective-permute-done.1, f32[8,2,192,128]{3,2,1,0:T(8,128)} %get-tuple-element.62, ...), kind=kLoop, calls=%fused_computation.26 | loop fusion | flops 3538944 | bytes 7864320 | tf_op jit(solution)/shard_map/convert_element_type | solution.py:252
  77.9 6.9 %all-to-all-start.1 = ((f16[8,2,192,128]{3,2,1,0:T(8,128)(2,1)}), f16[8,2,192,128]{3,2,1,0:T(8,128)(2,1)S(1)}, u32[]{:S(2)}, u32[]{:S(2)}) async-start(f16[8,2,192,128]{3,2,1,0:T(8,128)(2,1)} %get-tuple-element.75), calls=%async_computation.1 | async-start | bytes 1572864 | tf_op jit(solution)/shard_map/all_to_all | solution.py:252
  84.8 0.3 select_reduce_fusion
  85.1 1.1 fusion.7
  86.3 2.6 %collective-permute-start.10 = (f16[2,64,128]{2,1,0:T(8,128)(2,1)S(1)}, f16[2,64,128]{2,1,0:T(8,128)(2,1)S(1)}, u32[]{:S(2)}, u32[]{:S(2)}) collective-permute-start(f16[2,64,128]{2,1,0:T(8,128)(2,1)S(1)} %get-tuple-element.79), channel_id=1, source_target_pairs={{0,96},{32,0},{64,32},{96,64},{1,97},{33,1},{65,33},{97,65},{2,98}... | collective-permute-start | bytes 98312 | tf_op jit(solution)/shard_map/ppermute | solution.py:37
  88.9 0.0 collective-permute-start.9
  88.9 1.7 %collective-permute-start.8 = (f16[2,64,128]{2,1,0:T(8,128)(2,1)S(1)}, f16[2,64,128]{2,1,0:T(8,128)(2,1)S(1)}, u32[]{:S(2)}, u32[]{:S(2)}) collective-permute-start(f16[2,64,128]{2,1,0:T(8,128)(2,1)S(1)} %get-tuple-element.81), channel_id=1, source_target_pairs={{0,64},{32,96},{64,0},{96,32},{1,65},{33,97},{65,1},{97,33},{2,66}... | collective-permute-start | bytes 98312 | tf_op jit(solution)/shard_map/ppermute | solution.py:37
  90.6 2.6 %collective-permute-done.9 = f16[2,64,128]{2,1,0:T(8,128)(2,1)S(1)} collective-permute-done((f16[2,64,128]{2,1,0:T(8,128)(2,1)S(1)}, f16[2,64,128]{2,1,0:T(8,128)(2,1)S(1)}, u32[]{:S(2)}, u32[]{:S(2)}) %collective-permute-start.9) | collective-permute-done | bytes 32800 | tf_op jit(solution)/shard_map/ppermute | solution.py:37
  93.1 0.4 collective-permute-done.8
  93.5 14.9 %all-to-all-done.1 = f16[8,2,192,128]{3,2,1,0:T(8,128)(2,1)S(1)} async-done(((f16[8,2,192,128]{3,2,1,0:T(8,128)(2,1)}), f16[8,2,192,128]{3,2,1,0:T(8,128)(2,1)S(1)}, u32[]{:S(2)}, u32[]{:S(2)}) %all-to-all-start.1) | async-done | bytes 786464 | tf_op jit(solution)/shard_map/all_to_all | solution.py:252
  108.4 0.2 select_reduce_fusion.1
  108.6 0.7 fusion.1.first
  109.3 0.6 fusion.5.second
  110.0 1.9 %turn.1 = f32[8,64,256]{2,1,0:T(8,128)} custom-call(f32[2,192,128]{2,1,0:T(8,128)} %fusion.1.first, f32[2,64,128]{2,1,0:T(8,128)} %fusion.5.second), custom_call_target="tpu_custom_call" | custom-call | tf_op jit(solution)/shard_map/turn/pallas_call | solution.py:261
  111.8 14.4 %all_to_all.15.got = f32[8,64,256]{2,1,0:T(8,128)} all-to-all(f32[8,64,256]{2,1,0:T(8,128)} %turn.1), channel_id=1, replica_groups=mesh['group'=2,'x'=4,'z'=8,'y'=2,'c'=2] {'group','y','c'}, dimensions={0} | all-to-all | bytes 1048576 | tf_op jit(solution)/shard_map/all_to_all | solution.py:266
  126.2 2.4 %final.1 = (f32[32,512]{1,0:T(8,128)}, f32[32,512]{1,0:T(8,128)}, bf16[64,512]{1,0:T(8,128)(2,1)}) custom-call(s32[1]{0:T(128)} %bitcast.group, f32[6]{0:T(128)} %reshape.23.facts, f32[8,64,256]{2,1,0:T(8,128)} %all_to_all.15.got, f32[64,512]{1,0:T(8,128)} %bitcast.46, f32[64,512]{1,0:T(8,128)} %bitcast.48, f32[64,512]{1,0:T(8,128)} %bitcast.50, ...), custom_call_target="tpu_custom_call" | custom-call | tf_op jit(solution)/shard_map/final/pallas_call | solution.py:270
  (17 shorter events, 0.1 us)
Async XLA Ops:
  10.3 15.5 %collective-permute-start.2 = (f32[8,4,2,64,128]{4,3,2,1,0:T(8,128)}, f32[8,4,2,64,128]{4,3,2,1,0:T(8,128)S(1)}, u32[]{:S(2)}, u32[]{:S(2)}) collective-permute-start(f32[8,4,2,64,128]{4,3,2,1,0:T(8,128)} %get-tuple-element.39), channel_id=1, source_target_pairs={{0,1},{1,0},{2,3},{3,2},{4,5},{5,4},{6,7},{7,6},{8,9},{9,8},{10,11... | collective-permute-start | bytes 6291464 | tf_op jit(solution)/shard_map/ppermute | solution.py:33
  13.5 10.0 %collective-permute-start = (f32[8,2,192,128]{3,2,1,0:T(8,128)}, f32[8,2,192,128]{3,2,1,0:T(8,128)}, u32[]{:S(2)}, u32[]{:S(2)}) collective-permute-start(f32[8,2,192,128]{3,2,1,0:T(8,128)} %get-tuple-element.43), channel_id=1, source_target_pairs={{0,1},{1,0},{2,3},{3,2},{4,5},{5,4},{6,7},{7,6},{8,9},{9,8},{10,11... | collective-permute-start | bytes 4718600 | tf_op jit(solution)/shard_map/ppermute | solution.py:33
  13.6 23.8 %collective-permute-start.3 = (f32[8,2,192,128]{3,2,1,0:T(8,128)}, f32[8,2,192,128]{3,2,1,0:T(8,128)}, u32[]{:S(2)}, u32[]{:S(2)}) collective-permute-start(f32[8,2,192,128]{3,2,1,0:T(8,128)} %get-tuple-element.48), channel_id=1, source_target_pairs={{0,1},{1,0},{2,3},{3,2},{4,5},{5,4},{6,7},{7,6},{8,9},{9,8},{10,11... | collective-permute-start | bytes 4718600 | tf_op jit(solution)/shard_map/ppermute | solution.py:33
  14.1 26.5 %collective-permute-start.5 = (f32[8,2,192,128]{3,2,1,0:T(8,128)}, f32[8,2,192,128]{3,2,1,0:T(8,128)}, u32[]{:S(2)}, u32[]{:S(2)}) collective-permute-start(f32[8,2,192,128]{3,2,1,0:T(8,128)} %get-tuple-element.52), channel_id=1, source_target_pairs={{0,1},{1,0},{2,3},{3,2},{4,5},{5,4},{6,7},{7,6},{8,9},{9,8},{10,11... | collective-permute-start | bytes 4718600 | tf_op jit(solution)/shard_map/ppermute | solution.py:33
  23.5 2.5 %copy-start.1 = (f32[8,4,2,64,128]{4,3,2,1,0:T(8,128)S(1)}, f32[8,4,2,64,128]{4,3,2,1,0:T(8,128)}, u32[]{:S(2)}) copy-start(f32[8,4,2,64,128]{4,3,2,1,0:T(8,128)} %get-tuple-element.45) | copy-start | bytes 6291460
  25.8 1.7 %copy-start = (f32[8,4,2,64,128]{4,3,2,1,0:T(8,128)}, f32[8,4,2,64,128]{4,3,2,1,0:T(8,128)S(1)}, u32[]{:S(2)}) copy-start(f32[8,4,2,64,128]{4,3,2,1,0:T(8,128)S(1)} %collective-permute-done.2) | copy-start | bytes 6291460
  27.5 45.1 %all-to-all-start = ((f16[8,4,2,64,128]{4,3,2,1,0:T(8,128)(2,1)}), f16[8,4,2,64,128]{4,3,2,1,0:T(8,128)(2,1)S(1)}, u32[]{:S(2)}, u32[]{:S(2)}) async-start(f16[8,4,2,64,128]{4,3,2,1,0:T(8,128)(2,1)} %add_convert_fusion), calls=%async_computation | async-start | bytes 2097152 | tf_op jit(solution)/shard_map/all_to_all | solution.py:226
  34.0 38.6 %collective-permute-start.11 = (f32[8,2,192,128]{3,2,1,0:T(8,128)}, f32[8,2,192,128]{3,2,1,0:T(8,128)S(1)}, u32[]{:S(2)}, u32[]{:S(2)}) collective-permute-start(f32[8,2,192,128]{3,2,1,0:T(8,128)} %get-tuple-element.63), channel_id=1, source_target_pairs={{0,1},{1,0},{2,3},{3,2},{4,5},{5,4},{6,7},{7,6},{8,9},{9,8},{10,11... | collective-permute-start | bytes 4718600 | tf_op jit(solution)/shard_map/ppermute | solution.py:33
  34.7 20.7 %collective-permute-start.1 = (f16[8,2,192,128]{3,2,1,0:T(8,128)(2,1)S(1)}, f16[8,2,192,128]{3,2,1,0:T(8,128)(2,1)}, u32[]{:S(2)}, u32[]{:S(2)}) collective-permute-start(f16[8,2,192,128]{3,2,1,0:T(8,128)(2,1)S(1)} %add_convert_fusion.3), channel_id=1, source_target_pairs={{0,64},{32,96},{64,0},{96,32},{1,65},{33,97},{65,1},{97,33},{2,66}... | collective-permute-start | bytes 2359304 | tf_op jit(solution)/shard_map/ppermute | solution.py:37
  37.4 3.1 %copy-start.2 = (f32[8,2,192,128]{3,2,1,0:T(8,128)S(1)}, f32[8,2,192,128]{3,2,1,0:T(8,128)}, u32[]{:S(2)}) copy-start(f32[8,2,192,128]{3,2,1,0:T(8,128)} %get-tuple-element.53) | copy-start | bytes 4718596
  40.5 4.0 %copy-start.5 = (s32[2]{0:T(128)S(1)}, s32[2]{0:T(128)}, u32[]{:S(2)}) copy-start(s32[2]{0:T(128)} %param.15) | copy-start | bytes 28
  40.5 9.5 %copy-start.4 = (s32[2]{0:T(128)S(1)}, s32[2]{0:T(128)}, u32[]{:S(2)}) copy-start(s32[2]{0:T(128)} %param.14) | copy-start | bytes 28
  43.1 29.2 %collective-permute-start.6 = (f16[8,2,192,128]{3,2,1,0:T(8,128)(2,1)}, f16[8,2,192,128]{3,2,1,0:T(8,128)(2,1)}, u32[]{:S(2)}, u32[]{:S(2)}) collective-permute-start(f16[8,2,192,128]{3,2,1,0:T(8,128)(2,1)} %add_convert_fusion.1), channel_id=1, source_target_pairs={{0,96},{32,0},{64,32},{96,64},{1,97},{33,1},{65,33},{97,65},{2,98}... | collective-permute-start | bytes 2359304 | tf_op jit(solution)/shard_map/ppermute | solution.py:37
  43.9 28.7 %collective-permute-start.4 = (f16[8,2,192,128]{3,2,1,0:T(8,128)(2,1)}, f16[8,2,192,128]{3,2,1,0:T(8,128)(2,1)}, u32[]{:S(2)}, u32[]{:S(2)}) collective-permute-start(f16[8,2,192,128]{3,2,1,0:T(8,128)(2,1)} %add_convert_fusion.2), channel_id=1, source_target_pairs={{0,32},{32,64},{64,96},{96,0},{1,33},{33,65},{65,97},{97,1},{2,34}... | collective-permute-start | bytes 2359304 | tf_op jit(solution)/shard_map/ppermute | solution.py:37
  47.1 14.4 %collective-permute-start.7 = (f32[256,512]{1,0:T(8,128)}, f32[256,512]{1,0:T(8,128)}, u32[]{:S(2)}, u32[]{:S(2)}) collective-permute-start(f32[256,512]{1,0:T(8,128)} %pack.1), channel_id=1, source_target_pairs={{0,128},{128,0},{1,129},{129,1},{2,130},{130,2},{3,131},{131,3},{4... | collective-permute-start | bytes 1572872 | tf_op jit(solution)/shard_map/ppermute | solution.py:33
  72.6 1.2 copy-start.3
  77.9 30.5 %all-to-all-start.1 = ((f16[8,2,192,128]{3,2,1,0:T(8,128)(2,1)}), f16[8,2,192,128]{3,2,1,0:T(8,128)(2,1)S(1)}, u32[]{:S(2)}, u32[]{:S(2)}) async-start(f16[8,2,192,128]{3,2,1,0:T(8,128)(2,1)} %get-tuple-element.75), calls=%async_computation.1 | async-start | bytes 1572864 | tf_op jit(solution)/shard_map/all_to_all | solution.py:252
  86.3 4.3 %collective-permute-start.10 = (f16[2,64,128]{2,1,0:T(8,128)(2,1)S(1)}, f16[2,64,128]{2,1,0:T(8,128)(2,1)S(1)}, u32[]{:S(2)}, u32[]{:S(2)}) collective-permute-start(f16[2,64,128]{2,1,0:T(8,128)(2,1)S(1)} %get-tuple-element.79), channel_id=1, source_target_pairs={{0,96},{32,0},{64,32},{96,64},{1,97},{33,1},{65,33},{97,65},{2,98}... | collective-permute-start | bytes 98312 | tf_op jit(solution)/shard_map/ppermute | solution.py:37
  88.9 4.3 %collective-permute-start.9 = (f16[2,64,128]{2,1,0:T(8,128)(2,1)S(1)}, f16[2,64,128]{2,1,0:T(8,128)(2,1)S(1)}, u32[]{:S(2)}, u32[]{:S(2)}) collective-permute-start(f16[2,64,128]{2,1,0:T(8,128)(2,1)S(1)} %get-tuple-element.80), channel_id=1, source_target_pairs={{0,32},{32,64},{64,96},{96,0},{1,33},{33,65},{65,97},{97,1},{2,34}... | collective-permute-start | bytes 98312 | tf_op jit(solution)/shard_map/ppermute | solution.py:37
  88.9 4.7 %collective-permute-start.8 = (f16[2,64,128]{2,1,0:T(8,128)(2,1)S(1)}, f16[2,64,128]{2,1,0:T(8,128)(2,1)S(1)}, u32[]{:S(2)}, u32[]{:S(2)}) collective-permute-start(f16[2,64,128]{2,1,0:T(8,128)(2,1)S(1)} %get-tuple-element.81), channel_id=1, source_target_pairs={{0,64},{32,96},{64,0},{96,32},{1,65},{33,97},{65,1},{97,33},{2,66}... | collective-permute-start | bytes 98312 | tf_op jit(solution)/shard_map/ppermute | solution.py:37

commit v3 on v2

--- a/solution.py
+++ b/solution.py
@@ -23,9 +23,10 @@
 WIRE = jnp.float16
 F32 = jnp.float32
 PEAK = 128.0
-ROWS_A = 192
+ROWS_A = 184
 LANES = 128
 BLOCK = 1024
+AHEAD = 4
 ORDER = (2, 1, 3, 0)
 
 
@@ -43,10 +44,14 @@
 
 def terms_kernel(scale, which, place, cot, acts, *refs):
     outs, out_b = refs[:NX], refs[NX]
-    turned, held, arrived = refs[NX + 1 :]
-    step = pl.program_id(0)
+    upstream, held, mine, arrived, ready, left = refs[NX + 1 :]
+    outs = (*outs[:-1], mine)
+    last = pltpu.make_async_copy(mine, refs[NX - 1], left)
     steps = acts.shape[1] // BLOCK
     per = steps // NX
+    half = upstream.shape[1]
+
+    turns = [n * per + i for n in (0, NX - 1, *range(1, NX - 1)) for i in range(per)]
 
     def copy(i):
         x = lax.rem(place[0] + ORDER[i // per], NX)
@@ -55,69 +60,63 @@
             acts.at[:, pl.ds(start, BLOCK)], held.at[i], arrived.at[i]
         )
 
-    @pl.when(step == 0)
-    def _():
-        for i in range(steps):
-            copy(i).start()
-        turned[...] = cot[...].astype(F32).T.astype(cot.dtype)
-
-    for i in range(steps):
-
-        @pl.when(step == i)
-        def _():
-            copy(i).wait()
-            out = jnp.dot(turned[...], held[i], preferred_element_type=F32) * scale
-            for j in range(BLOCK // LANES):
-                z, y = divmod(j, NY)
-                piece = out[:, j * LANES : (j + 1) * LANES]
-                outs[i // per][z, y] = piece[:ROWS_A]
-                out_b[z, 0, y] = piece[ROWS_A:]
+    first = pl.multiple_of(which[0] * half, half)
+    whole = pltpu.make_async_copy(cot.at[:, pl.ds(first, half)], upstream, ready)
+    whole.start()
+    for i in turns[:AHEAD]:
+        copy(i).start()
+    whole.wait()
+    turned = upstream[...].astype(F32).T.astype(upstream.dtype)
+    for turn, i in enumerate(turns):
+        copy(i).wait()
+        if turn + AHEAD < steps:
+            copy(turns[turn + AHEAD]).start()
+        out = jnp.dot(turned, held[i], preferred_element_type=F32) * scale
+        for j in range(BLOCK // LANES):
+            z, y = divmod(j, NY)
+            z += i % per * (NZ // per)
+            piece = out[:, j * LANES : (j + 1) * LANES]
+            outs[i // per][z, y] = piece[:ROWS_A]
+            out_b[z, i // per, y] = piece[ROWS_A:]
+        if turn == 2 * per - 1:
+            last.start()
+    last.wait()
 
 
 def terms(inputs, upstream, which, x):
     tokens, width = inputs.shape
     half = upstream.shape[1] // NC
-    zs = BLOCK // (LANES * NY)
-    per = NZ // zs
     steps = width // BLOCK
-    rows_b = half - ROWS_A
-
-    def at(n):
-        return lambda i, w, x: (jnp.clip(i - n * per, 0, per - 1), 0, 0, 0)
-
+    vmem = pl.BlockSpec(memory_space=pltpu.VMEM)
     return pl.pallas_call(
         functools.partial(terms_kernel, PEAK / (tokens * NC)),
-        grid_spec=pltpu.PrefetchScalarGridSpec(
-            num_scalar_prefetch=2,
-            grid=(steps,),
-            in_specs=[
-                pl.BlockSpec((tokens, half), lambda i, w, x: (0, w[0])),
-                pl.BlockSpec(memory_space=pl.ANY),
-            ],
-            out_specs=[
-                pl.BlockSpec((zs, NY, ROWS_A, LANES), at(n)) for n in range(NX)
-            ]
-            + [
-                pl.BlockSpec(
-                    (zs, 1, NY, rows_b, LANES),
-                    lambda i, w, x: (i % per, i // per, 0, 0, 0),
-                ),
-            ],
-            scratch_shapes=[
-                pltpu.VMEM((half, tokens), inputs.dtype),
-                pltpu.VMEM((steps, tokens, BLOCK), inputs.dtype),
-                pltpu.SemaphoreType.DMA((steps,)),
-            ],
-        ),
-        out_shape=[jax.ShapeDtypeStruct((NZ, NY, ROWS_A, LANES), F32)] * NX
-        + [jax.ShapeDtypeStruct((NZ, NX, NY, rows_b, LANES), F32)],
+        in_specs=[pl.BlockSpec(memory_space=pltpu.SMEM)] * 2
+        + [pl.BlockSpec(memory_space=pl.ANY)] * 2,
+        out_specs=[vmem] * (NX - 1) + [pl.BlockSpec(memory_space=pl.ANY), vmem],
+        scratch_shapes=[
+            pltpu.VMEM((tokens, half), inputs.dtype),
+            pltpu.VMEM((steps, tokens, BLOCK), inputs.dtype),
+            pltpu.VMEM((NZ, NY, ROWS_A, LANES), F32),
+            pltpu.SemaphoreType.DMA((steps,)),
+            pltpu.SemaphoreType.DMA,
+            pltpu.SemaphoreType.DMA,
+        ],
+        out_shape=[pltpu.VMEM((NZ, NY, ROWS_A, LANES), F32)] * (NX - 1)
+        + [pltpu.HBM((NZ, NY, ROWS_A, LANES), F32)]
+        + [pltpu.VMEM((NZ, NX, NY, half - ROWS_A, LANES), F32)],
+        compiler_params=pltpu.CompilerParams(vmem_limit_bytes=18 * 2**20),
         cost_estimate=pl.CostEstimate(
             flops=2 * tokens * half * width,
             bytes_accessed=2 * tokens * width + 4 * half * width,
             transcendentals=0,
         ),
         name="terms",
-    )(which[None], x[None], upstream, inputs)
+    )(
+        which[None],
+        x[None],
+        pltpu.with_memory_space_constraint(upstream, pltpu.HBM),
+        pltpu.with_memory_space_constraint(inputs, pltpu.HBM),
+    )
 
 
 def turn_kernel(first, second, out):
@@ -195,7 +194,9 @@
     rows = inner_params.shape[1]
 
     *theirs_a, theirs_b = terms(inputs, upstream, 1 - core, x)
-    got_a = [swap(a, "c") for a in theirs_a]
+    got_a = []
+    for a in theirs_a:
+        got_a.append(swap(a, "c"))
     got_b = swap(theirs_b, "c")
     inputs, upstream, _ = lax.optimization_barrier((inputs, upstream, theirs_b))
     *own_a, own_b = terms(inputs, upstream, core, x)
@@ -211,23 +212,21 @@
     )
     facts = jnp.where(group == 0, facts, facts[::-1]).reshape(-1)
 
-    def wire_a(n):
-        return (own_a[n] + got_a[n]).astype(WIRE)
-
     near = (inner_params[0], adam_first[0], adam_second[0], anchor, momentum)
 
-    def send_a(n):
+    def send(wire, n):
         return around(wire, "x", ORDER[n], NX)
 
-    wire = wire_a(0)
-    sent = [send_a(0)]
+    wire = (own_a[0] + got_a[0]).astype(WIRE)
+    sent_0 = send(wire, 0)
     _, own_b, got_b = lax.optimization_barrier((wire, own_b, got_b))
-    wire = wire_b = (own_b + got_b).astype(WIRE)
-    back = lax.all_to_all(wire_b, "z", 0, 0, tiled=True)
+    wire = (own_b + got_b).astype(WIRE)
+    back_b = lax.all_to_all(wire, "z", 0, 0, tiled=True)
+    sent = [sent_0]
     for n in range(1, NX - 1):
-        _, own_a[n], got_a[n] = lax.optimization_barrier((wire, own_a[n], got_a[n]))
-        wire = wire_a(n)
-        sent.append(send_a(n))
+        _, own, got = lax.optimization_barrier((wire, own_a[n], got_a[n]))
+        wire = (own + got).astype(WIRE)
+        sent.append(send(wire, n))
     gated, _ = lax.optimization_barrier((near, wire))
     packed = pl.pallas_call(
         pack_kernel,
@@ -237,26 +236,24 @@
         name="pack",
     )(*gated)
     far = swap(packed, "group")
+
+    sent, back_b, far, facts = lax.optimization_barrier((sent, back_b, far, facts))
     first = own_a[-1] + got_a[-1]
-    second = pick(own_b, z) + pick(got_b, z)
-    sent, back, far, facts = lax.optimization_barrier((sent, back, far, facts))
-    place = lax.broadcasted_iota(jnp.int32, (NZ, 1, 1, 1, 1), 0)
-    second = jnp.where(place == z, 0.0, back.astype(F32)).sum(0) + second
-    second = second * (1.0 / NZ)
-    sent_b = [around(second[n].astype(WIRE), "x", ORDER[n], NX) for n in range(NX - 1)]
+    for w in sent:
+        first = first + w.astype(F32)
+    first = first * (1.0 / NX)
+    back_a = lax.all_to_all(first.astype(WIRE), "z", 0, 0, tiled=True)
+    second = back_b.astype(F32).sum(0) * (1.0 / NZ)
+    wires = [second[n].astype(WIRE) for n in range(NX - 1)]
+    sent_b = [around(wires[n], "x", ORDER[n], NX) for n in range(NX - 1)]
     second = second[-1]
-
-    for s in sent:
-        first = first + s.astype(F32)
-    first = first * (1.0 / NX)
-    back = lax.all_to_all(first.astype(WIRE), "z", 0, 0, tiled=True)
-    sent_b, back = lax.optimization_barrier((sent_b, back))
+    sent_b, back_a = lax.optimization_barrier((sent_b, back_a))
+    for w in sent_b:
+        second = second + w.astype(F32)
+    second = second * (1.0 / NX)
     place = lax.broadcasted_iota(jnp.int32, (NZ, 1, 1, 1), 0)
-    first = jnp.where(place == z, 0.0, back.astype(F32)).sum(0) + pick(first, z)
-    first = first * (1.0 / NZ)
-    for s in sent_b:
-        second = second + s.astype(F32)
-    second = second * (1.0 / NX)
+    back_a = jnp.where(place == z, 0.0, back_a.astype(F32)).sum(0)
+    first = (back_a + pick(first, z)) * (1.0 / NZ)
 
     part = pl.pallas_call(
         turn_kernel,

time: 129 us -> 119 us (0.922)
  Pallas kernels: 25.1 us -> 19.3 us
  waiting for transfers between devices: 39 us -> 35.8 us
    pallas_call x2, Pallas kernels: 19 us -> 13.1 us  [terms(): pl.pallas_call(functools.partial(terms_kernel, PEAK / (tokens * NC)), in_...]
    convert_element_type x5, other arithmetic: 13.4 us -> 10.8 us  [the longest x2 5.01 us: per_device(): wire = (own + got).astype(WIRE)]
    ppermute x6, waiting for transfers between devices: 18 us -> 16.3 us  [around(): return lax.ppermute(a, axis, [(i, (i + k) % size) for i in range(size)])]
    all_to_all x2, waiting for transfers between devices: 14.9 us -> 13.6 us  [the longest x1 13.6 us: per_device(): back_a = lax.all_to_all(first.astype(WIRE), 'z', 0, 0, tiled=True)]
  transfers between devices with their start and end apart: 14 -> 14, of which waited for: 7 -> 7; matrix products, arithmetic and copies ran while one was open for 10% -> 10% of each run, Pallas kernels for 9% -> 6%
where the time goes in v3:
time: 119 us; the launch traced here: 118 us
  waiting for transfers between devices  35.8 us (30%)
  starting transfers between devices  29.4 us (25%)
  Pallas kernels  19.3 us (16%)
  other arithmetic  16.5 us (14%)
  blocking collectives  14.4 us (12%)
  local copies, waits for them, and re-layouts  2.21 us (2%)
    ppermute x6, waiting for transfers between devices, around(): return lax.ppermute(a, axis, [(i, (i + k) % size) for i in range(size)])  16.3 us
    all_to_all x1, blocking collectives, per_device(): got = lax.all_to_all(part, ('group', 'y', 'c'), 0, 0, tiled=True)  14.4 us
    all_to_all x1, waiting for transfers between devices, per_device(): back_a = lax.all_to_all(first.astype(WIRE), 'z', 0, 0, tiled=True)  13.6 us
    pallas_call x2, Pallas kernels, terms(): pl.pallas_call(functools.partial(terms_kernel, PEAK / (tokens * NC)), in_...  13.1 us
    ppermute x6, starting transfers between devices, around(): return lax.ppermute(a, axis, [(i, (i + k) % size) for i in range(size)])  8.44 us
    ppermute x6, starting transfers between devices, swap(): return lax.ppermute(a, axis, [(0, 1), (1, 0)])  7.49 us
    all_to_all x1, starting transfers between devices, per_device(): back_a = lax.all_to_all(first.astype(WIRE), 'z', 0, 0, tiled=True)  6.98 us
    all_to_all x1, starting transfers between devices, per_device(): back_b = lax.all_to_all(wire, 'z', 0, 0, tiled=True)  6.48 us
  transfers between devices with their start and end apart: 14, of which 7 were waited for; matrix products, arithmetic and copies ran while one was open for 10% of the time, Pallas kernels for 6%

profile of v3, /device:TPU:1, one launch (start us, length us, event | category | flops | bytes accessed | tf_op | source)
XLA Modules:
  0.0 118.2 jit_solution(10332229348890530482)
XLA Ops:
  0.6 7.4 %terms.2 = (f32[8,2,184,128]{3,2,1,0:T(8,128)S(1)}, f32[8,2,184,128]{3,2,1,0:T(8,128)}, f32[8,2,184,128]{3,2,1,0:T(8,128)}, f32[8,2,184,128]{3,2,1,0:T(8,128)}, f32[8,4,2,72,128]{4,3,2,1,0:T(8,128)S(1)}) custom-call(s32[1]{0:T(128)} %bitcast.5.which, s32[1]{0:T(128)} %bitcast.2.place, bf16[512,512]{1,0:T(8,128)(2,1)} %bitcast.38, bf16[512,8192]{1,0:T(8,128)(2,1)} %bitcast.36), custom_call_target="tpu_custom_call" | custom-call | flops 2147483648 | bytes 16777216 | tf_op jit(solution)/shard_map/terms/pallas_call | solution.py:91
  8.1 3.3 %collective-permute-start.2 = (f32[8,4,2,72,128]{4,3,2,1,0:T(8,128)S(1)}, f32[8,4,2,72,128]{4,3,2,1,0:T(8,128)S(1)}, u32[]{:S(2)}, u32[]{:S(2)}) collective-permute-start(f32[8,4,2,72,128]{4,3,2,1,0:T(8,128)S(1)} %get-tuple-element.39), channel_id=1, source_target_pairs={{0,1},{1,0},{2,3},{3,2},{4,5},{5,4},{6,7},{7,6},{8,9},{9,8},{10,11... | collective-permute-start | bytes 7077896 | tf_op jit(solution)/shard_map/ppermute | solution.py:34
  11.3 0.1 collective-permute-start
  11.4 0.4 collective-permute-start.3
  11.9 0.1 collective-permute-start.5
  12.0 5.7 %terms.3 = (f32[8,2,184,128]{3,2,1,0:T(8,128)S(1)}, f32[8,2,184,128]{3,2,1,0:T(8,128)S(1)}, f32[8,2,184,128]{3,2,1,0:T(8,128)S(1)}, f32[8,2,184,128]{3,2,1,0:T(8,128)}, f32[8,4,2,72,128]{4,3,2,1,0:T(8,128)S(1)}) custom-call(s32[1]{0:T(128)} %bitcast.1.which, s32[1]{0:T(128)} %bitcast.2.place, bf16[512,512]{1,0:T(8,128)(2,1)} %bitcast.39, ...), custom_call_target="tpu_custom_call" | custom-call | flops 2147483648 | bytes 16777216 | tf_op jit(solution)/shard_map/terms/pallas_call | solution.py:91
  17.6 0.0 collective-permute-done
  17.7 1.0 add_convert_fusion.3
  18.7 0.0 collective-permute-done.2
  18.7 1.3 %add_convert_fusion = f16[8,4,2,72,128]{4,3,2,1,0:T(8,128)(2,1)} fusion(f32[8,4,2,72,128]{4,3,2,1,0:T(8,128)S(1)} %get-tuple-element.45, f32[8,4,2,72,128]{4,3,2,1,0:T(8,128)S(1)} %collective-permute-done.2), kind=kLoop, calls=%fused_computation.1 | loop fusion | flops 1179648 | bytes 5898240 | tf_op jit(solution)/shard_map/convert_element_type | solution.py:223
  20.1 6.5 %all-to-all-start = ((f16[8,4,2,72,128]{4,3,2,1,0:T(8,128)(2,1)}), f16[8,4,2,72,128]{4,3,2,1,0:T(8,128)(2,1)}, u32[]{:S(2)}, u32[]{:S(2)}) async-start(f16[8,4,2,72,128]{4,3,2,1,0:T(8,128)(2,1)} %add_convert_fusion), calls=%async_computation | async-start | bytes 2359296 | tf_op jit(solution)/shard_map/all_to_all | solution.py:224
  26.5 0.7 collective-permute-start.11
  27.2 2.7 %collective-permute-start.1 = (f16[8,2,184,128]{3,2,1,0:T(8,128)(2,1)}, f16[8,2,184,128]{3,2,1,0:T(8,128)(2,1)}, u32[]{:S(2)}, u32[]{:S(2)}) collective-permute-start(f16[8,2,184,128]{3,2,1,0:T(8,128)(2,1)} %add_convert_fusion.3), channel_id=1, source_target_pairs={{0,64},{32,96},{64,0},{96,32},{1,65},{33,97},{65,1},{97,33},{2,66}... | collective-permute-start | bytes 2261000 | tf_op jit(solution)/shard_map/ppermute | solution.py:38
  30.0 2.5 %add_convert_fusion.2 = f16[8,2,184,128]{3,2,1,0:T(8,128)(2,1)} fusion(f32[8,2,184,128]{3,2,1,0:T(8,128)S(1)} %get-tuple-element.49, f32[8,2,184,128]{3,2,1,0:T(8,128)} %collective-permute-done.3), kind=kLoop, calls=%fused_computation.5 | loop fusion | flops 753664 | bytes 3768320 | tf_op jit(solution)/shard_map/convert_element_type | solution.py:228
  32.4 0.0 collective-permute-done.5
  32.4 2.5 %add_convert_fusion.1 = f16[8,2,184,128]{3,2,1,0:T(8,128)(2,1)} fusion(f32[8,2,184,128]{3,2,1,0:T(8,128)S(1)} %get-tuple-element.53, f32[8,2,184,128]{3,2,1,0:T(8,128)} %collective-permute-done.5), kind=kLoop, calls=%fused_computation.4 | loop fusion | flops 753664 | bytes 3768320 | tf_op jit(solution)/shard_map/convert_element_type | solution.py:228
  35.0 0.9 collective-permute-start.6
  35.8 0.6 collective-permute-start.4
  36.5 0.6 convert_reduce_fusion.1
  37.1 1.9 %pack.1 = f32[256,512]{1,0:T(8,128)} custom-call(f32[64,512]{1,0:T(8,128)} %bitcast.40, f32[64,512]{1,0:T(8,128)} %bitcast.42, f32[64,512]{1,0:T(8,128)} %bitcast.44, f32[32,512]{1,0:T(8,128)} %a0.1, f32[32,512]{1,0:T(8,128)} %w0.1), custom_call_target="tpu_custom_call" | custom-call | tf_op jit(solution)/shard_map/pack/pallas_call | solution.py:231
  38.9 2.9 %collective-permute-start.7 = (f32[256,512]{1,0:T(8,128)}, f32[256,512]{1,0:T(8,128)S(1)}, u32[]{:S(2)}, u32[]{:S(2)}) collective-permute-start(f32[256,512]{1,0:T(8,128)} %pack.1), channel_id=1, source_target_pairs={{0,128},{128,0},{1,129},{129,1},{2,130},{130,2},{3,131},{131,3},{4... | collective-permute-start | bytes 1572872 | tf_op jit(solution)/shard_map/ppermute | solution.py:34
  41.9 1.3 %subtract_bitcast_fusion.1 = (f32[2,1]{0,1:T(1,128)S(1)}, f32[2,1]{0,1:T(1,128)S(1)}, f32[2,1]{0,1:T(1,128)S(1)}) fusion(s32[2]{0:T(128)S(1)} %copy-done.5, f32[]{:T(128)} %convert_reduce_fusion.1, s32[2]{0:T(128)} %param.15), kind=kLoop, calls=%fused_computation.22 | loop fusion | flops 10 | bytes 44 | tf_op jit(solution)/shard_map/stack | solution.py:205
  43.2 0.5 copy-done.4
  43.7 0.1 rev.3
  43.8 0.7 broadcast_select_fusion
  44.5 0.1 copy.12
  44.6 0.6 reshape.17.facts
  45.2 2.2 %collective-permute-done.1 = f16[8,2,184,128]{3,2,1,0:T(8,128)(2,1)} collective-permute-done((f16[8,2,184,128]{3,2,1,0:T(8,128)(2,1)}, f16[8,2,184,128]{3,2,1,0:T(8,128)(2,1)}, u32[]{:S(2)}, u32[]{:S(2)}) %collective-permute-start.1) | collective-permute-done | bytes 753696 | tf_op jit(solution)/shard_map/ppermute | solution.py:38
  47.4 5.9 %collective-permute-done.7.far = f32[256,512]{1,0:T(8,128)S(1)} collective-permute-done((f32[256,512]{1,0:T(8,128)}, f32[256,512]{1,0:T(8,128)S(1)}, u32[]{:S(2)}, u32[]{:S(2)}) %collective-permute-start.7) | collective-permute-done | bytes 524320 | tf_op jit(solution)/shard_map/ppermute | solution.py:34
  53.3 10.2 %collective-permute-done.6 = f16[8,2,184,128]{3,2,1,0:T(8,128)(2,1)S(1)} collective-permute-done((f16[8,2,184,128]{3,2,1,0:T(8,128)(2,1)}, f16[8,2,184,128]{3,2,1,0:T(8,128)(2,1)S(1)}, u32[]{:S(2)}, u32[]{:S(2)}) %collective-permute-start.6) | collective-permute-done | bytes 753696 | tf_op jit(solution)/shard_map/ppermute | solution.py:38
  63.5 0.3 collective-permute-done.4
  63.8 0.0 all-to-all-done
  63.9 0.6 copy-done.1
  64.5 0.3 copy-done.2
  64.7 3.5 %fusion.6 = (f16[8,2,184,128]{3,2,1,0:T(8,128)(2,1)}, f32[8,2,184,128]{3,2,1,0:T(8,128)S(1)}) fusion(f16[8,2,184,128]{3,2,1,0:T(8,128)(2,1)} %copy-done.1, f16[8,2,184,128]{3,2,1,0:T(8,128)(2,1)} %copy-done.2, f16[8,2,184,128]{3,2,1,0:T(8,128)(2,1)} %collective-permute-done.1, f32[8,2,184,128]{3,2,1,0:T(8,128)S(1)} %copy-done, ...), kind=kLoop, calls=%fused_computation.26 | loop fusion | flops 3391488 | bytes 7536640 | tf_op jit(solution)/shard_map/convert_element_type | solution.py:245
  68.2 7.0 %all-to-all-start.1 = ((f16[8,2,184,128]{3,2,1,0:T(8,128)(2,1)}), f16[8,2,184,128]{3,2,1,0:T(8,128)(2,1)S(1)}, u32[]{:S(2)}, u32[]{:S(2)}) async-start(f16[8,2,184,128]{3,2,1,0:T(8,128)(2,1)} %get-tuple-element.75), calls=%async_computation.1 | async-start | bytes 1507328 | tf_op jit(solution)/shard_map/all_to_all | solution.py:245
  75.2 1.5 %convert_reduce_fusion = f32[4,2,72,128]{3,2,1,0:T(8,128)S(1)} fusion(f16[8,4,2,72,128]{4,3,2,1,0:T(8,128)(2,1)} %all-to-all-done), kind=kLoop, calls=%fused_computation | loop fusion | flops 1105920 | bytes 1474560 | tf_op jit(solution)/shard_map/reduce_sum | solution.py:246
  76.7 2.8 %collective-permute-start.10 = (f16[2,72,128]{2,1,0:T(8,128)(2,1)S(1)}, f16[2,72,128]{2,1,0:T(8,128)(2,1)S(1)}, u32[]{:S(2)}, u32[]{:S(2)}) collective-permute-start(f16[2,72,128]{2,1,0:T(8,128)(2,1)S(1)} %get-tuple-element.79), channel_id=1, source_target_pairs={{0,96},{32,0},{64,32},{96,64},{1,97},{33,1},{65,33},{97,65},{2,98}... | collective-permute-start | bytes 110600 | tf_op jit(solution)/shard_map/ppermute | solution.py:38
  79.5 1.4 %collective-permute-start.8 = (f16[2,72,128]{2,1,0:T(8,128)(2,1)S(1)}, f16[2,72,128]{2,1,0:T(8,128)(2,1)S(1)}, u32[]{:S(2)}, u32[]{:S(2)}) collective-permute-start(f16[2,72,128]{2,1,0:T(8,128)(2,1)S(1)} %get-tuple-element.81), channel_id=1, source_target_pairs={{0,64},{32,96},{64,0},{96,32},{1,65},{33,97},{65,1},{97,33},{2,66}... | collective-permute-start | bytes 110600 | tf_op jit(solution)/shard_map/ppermute | solution.py:38
  80.9 3.0 %collective-permute-done.9 = f16[2,72,128]{2,1,0:T(8,128)(2,1)S(1)} collective-permute-done((f16[2,72,128]{2,1,0:T(8,128)(2,1)S(1)}, f16[2,72,128]{2,1,0:T(8,128)(2,1)S(1)}, u32[]{:S(2)}, u32[]{:S(2)}) %collective-permute-start.9) | collective-permute-done | bytes 36896 | tf_op jit(solution)/shard_map/ppermute | solution.py:38
  83.9 0.5 collective-permute-done.8
  84.5 13.6 %all-to-all-done.1 = f16[8,2,184,128]{3,2,1,0:T(8,128)(2,1)S(1)} async-done(((f16[8,2,184,128]{3,2,1,0:T(8,128)(2,1)}), f16[8,2,184,128]{3,2,1,0:T(8,128)(2,1)S(1)}, u32[]{:S(2)}, u32[]{:S(2)}) %all-to-all-start.1) | async-done | bytes 753696 | tf_op jit(solution)/shard_map/all_to_all | solution.py:245
  98.0 0.2 select_reduce_fusion
  98.2 0.7 fusion.first
  98.9 0.6 fusion.4.second
  99.6 1.9 %turn.1 = f32[8,64,256]{2,1,0:T(8,128)} custom-call(f32[2,184,128]{2,1,0:T(8,128)} %fusion.first, f32[2,72,128]{2,1,0:T(8,128)} %fusion.4.second), custom_call_target="tpu_custom_call" | custom-call | tf_op jit(solution)/shard_map/turn/pallas_call | solution.py:258
  101.5 14.4 %all_to_all.15.got = f32[8,64,256]{2,1,0:T(8,128)} all-to-all(f32[8,64,256]{2,1,0:T(8,128)} %turn.1), channel_id=1, replica_groups=mesh['group'=2,'x'=4,'z'=8,'y'=2,'c'=2] {'group','y','c'}, dimensions={0} | all-to-all | bytes 1048576 | tf_op jit(solution)/shard_map/all_to_all | solution.py:263
  115.9 2.4 %final.1 = (f32[32,512]{1,0:T(8,128)}, f32[32,512]{1,0:T(8,128)}, bf16[64,512]{1,0:T(8,128)(2,1)}) custom-call(s32[1]{0:T(128)} %bitcast.group, f32[6]{0:T(128)} %reshape.17.facts, f32[8,64,256]{2,1,0:T(8,128)} %all_to_all.15.got, f32[64,512]{1,0:T(8,128)} %bitcast.41, f32[64,512]{1,0:T(8,128)} %bitcast.43, f32[64,512]{1,0:T(8,128)} %bitcast.45, ...), custom_call_target="tpu_custom_call" | custom-call | tf_op jit(solution)/shard_map/final/pallas_call | solution.py:267
  (19 shorter events, 0.1 us)
Async XLA Ops:
  8.1 10.6 %collective-permute-start.2 = (f32[8,4,2,72,128]{4,3,2,1,0:T(8,128)S(1)}, f32[8,4,2,72,128]{4,3,2,1,0:T(8,128)S(1)}, u32[]{:S(2)}, u32[]{:S(2)}) collective-permute-start(f32[8,4,2,72,128]{4,3,2,1,0:T(8,128)S(1)} %get-tuple-element.39), channel_id=1, source_target_pairs={{0,1},{1,0},{2,3},{3,2},{4,5},{5,4},{6,7},{7,6},{8,9},{9,8},{10,11... | collective-permute-start | bytes 7077896 | tf_op jit(solution)/shard_map/ppermute | solution.py:34
  11.3 6.3 %collective-permute-start = (f32[8,2,184,128]{3,2,1,0:T(8,128)S(1)}, f32[8,2,184,128]{3,2,1,0:T(8,128)S(1)}, u32[]{:S(2)}, u32[]{:S(2)}) collective-permute-start(f32[8,2,184,128]{3,2,1,0:T(8,128)S(1)} %get-tuple-element.43), channel_id=1, source_target_pairs={{0,1},{1,0},{2,3},{3,2},{4,5},{5,4},{6,7},{7,6},{8,9},{9,8},{10,11... | collective-permute-start | bytes 4521992 | tf_op jit(solution)/shard_map/ppermute | solution.py:34
  11.4 18.5 %collective-permute-start.3 = (f32[8,2,184,128]{3,2,1,0:T(8,128)}, f32[8,2,184,128]{3,2,1,0:T(8,128)}, u32[]{:S(2)}, u32[]{:S(2)}) collective-permute-start(f32[8,2,184,128]{3,2,1,0:T(8,128)} %get-tuple-element.48), channel_id=1, source_target_pairs={{0,1},{1,0},{2,3},{3,2},{4,5},{5,4},{6,7},{7,6},{8,9},{9,8},{10,11... | collective-permute-start | bytes 4521992 | tf_op jit(solution)/shard_map/ppermute | solution.py:34
  11.9 20.6 %collective-permute-start.5 = (f32[8,2,184,128]{3,2,1,0:T(8,128)}, f32[8,2,184,128]{3,2,1,0:T(8,128)}, u32[]{:S(2)}, u32[]{:S(2)}) collective-permute-start(f32[8,2,184,128]{3,2,1,0:T(8,128)} %get-tuple-element.52), channel_id=1, source_target_pairs={{0,1},{1,0},{2,3},{3,2},{4,5},{5,4},{6,7},{7,6},{8,9},{9,8},{10,11... | collective-permute-start | bytes 4521992 | tf_op jit(solution)/shard_map/ppermute | solution.py:34
  20.1 43.8 %all-to-all-start = ((f16[8,4,2,72,128]{4,3,2,1,0:T(8,128)(2,1)}), f16[8,4,2,72,128]{4,3,2,1,0:T(8,128)(2,1)}, u32[]{:S(2)}, u32[]{:S(2)}) async-start(f16[8,4,2,72,128]{4,3,2,1,0:T(8,128)(2,1)} %add_convert_fusion), calls=%async_computation | async-start | bytes 2359296 | tf_op jit(solution)/shard_map/all_to_all | solution.py:224
  26.5 37.3 %collective-permute-start.11 = (f32[8,2,184,128]{3,2,1,0:T(8,128)}, f32[8,2,184,128]{3,2,1,0:T(8,128)}, u32[]{:S(2)}, u32[]{:S(2)}) collective-permute-start(f32[8,2,184,128]{3,2,1,0:T(8,128)} %get-tuple-element.63), channel_id=1, source_target_pairs={{0,1},{1,0},{2,3},{3,2},{4,5},{5,4},{6,7},{7,6},{8,9},{9,8},{10,11... | collective-permute-start | bytes 4521992 | tf_op jit(solution)/shard_map/ppermute | solution.py:34
  27.2 20.2 %collective-permute-start.1 = (f16[8,2,184,128]{3,2,1,0:T(8,128)(2,1)}, f16[8,2,184,128]{3,2,1,0:T(8,128)(2,1)}, u32[]{:S(2)}, u32[]{:S(2)}) collective-permute-start(f16[8,2,184,128]{3,2,1,0:T(8,128)(2,1)} %add_convert_fusion.3), channel_id=1, source_target_pairs={{0,64},{32,96},{64,0},{96,32},{1,65},{33,97},{65,1},{97,33},{2,66}... | collective-permute-start | bytes 2261000 | tf_op jit(solution)/shard_map/ppermute | solution.py:38
  32.4 4.0 %copy-start.6 = (s32[2]{0:T(128)S(1)}, s32[2]{0:T(128)}, u32[]{:S(2)}) copy-start(s32[2]{0:T(128)} %param.15) | copy-start | bytes 28
  32.4 9.4 %copy-start.5 = (s32[2]{0:T(128)S(1)}, s32[2]{0:T(128)}, u32[]{:S(2)}) copy-start(s32[2]{0:T(128)} %param.14) | copy-start | bytes 28
  32.4 32.3 %copy-start = (f32[8,2,184,128]{3,2,1,0:T(8,128)S(1)}, f32[8,2,184,128]{3,2,1,0:T(8,128)}, u32[]{:S(2)}) copy-start(f32[8,2,184,128]{3,2,1,0:T(8,128)} %get-tuple-element.62) | copy-start | bytes 4521988
  35.0 28.5 %collective-permute-start.6 = (f16[8,2,184,128]{3,2,1,0:T(8,128)(2,1)}, f16[8,2,184,128]{3,2,1,0:T(8,128)(2,1)S(1)}, u32[]{:S(2)}, u32[]{:S(2)}) collective-permute-start(f16[8,2,184,128]{3,2,1,0:T(8,128)(2,1)} %add_convert_fusion.1), channel_id=1, source_target_pairs={{0,96},{32,0},{64,32},{96,64},{1,97},{33,1},{65,33},{97,65},{2,98}... | collective-permute-start | bytes 2261000 | tf_op jit(solution)/shard_map/ppermute | solution.py:38
  35.8 28.0 %collective-permute-start.4 = (f16[8,2,184,128]{3,2,1,0:T(8,128)(2,1)}, f16[8,2,184,128]{3,2,1,0:T(8,128)(2,1)S(1)}, u32[]{:S(2)}, u32[]{:S(2)}) collective-permute-start(f16[8,2,184,128]{3,2,1,0:T(8,128)(2,1)} %add_convert_fusion.2), channel_id=1, source_target_pairs={{0,32},{32,64},{64,96},{96,0},{1,33},{33,65},{65,97},{97,1},{2,34}... | collective-permute-start | bytes 2261000 | tf_op jit(solution)/shard_map/ppermute | solution.py:38
  38.9 14.4 %collective-permute-start.7 = (f32[256,512]{1,0:T(8,128)}, f32[256,512]{1,0:T(8,128)S(1)}, u32[]{:S(2)}, u32[]{:S(2)}) collective-permute-start(f32[256,512]{1,0:T(8,128)} %pack.1), channel_id=1, source_target_pairs={{0,128},{128,0},{1,129},{129,1},{2,130},{130,2},{3,131},{131,3},{4... | collective-permute-start | bytes 1572872 | tf_op jit(solution)/shard_map/ppermute | solution.py:34
  43.2 0.5 copy-start.4
  53.3 14.9 %copy-start.3 = (f32[256,512]{1,0:T(8,128)}, f32[256,512]{1,0:T(8,128)S(1)}, u32[]{:S(2)}) copy-start(f32[256,512]{1,0:T(8,128)S(1)} %collective-permute-done.7.far) | copy-start | bytes 1572868
  63.5 1.0 copy-start.1
  63.8 0.9 copy-start.2
  68.2 29.9 %all-to-all-start.1 = ((f16[8,2,184,128]{3,2,1,0:T(8,128)(2,1)}), f16[8,2,184,128]{3,2,1,0:T(8,128)(2,1)S(1)}, u32[]{:S(2)}, u32[]{:S(2)}) async-start(f16[8,2,184,128]{3,2,1,0:T(8,128)(2,1)} %get-tuple-element.75), calls=%async_computation.1 | async-start | bytes 1507328 | tf_op jit(solution)/shard_map/all_to_all | solution.py:245
  76.7 4.2 %collective-permute-start.10 = (f16[2,72,128]{2,1,0:T(8,128)(2,1)S(1)}, f16[2,72,128]{2,1,0:T(8,128)(2,1)S(1)}, u32[]{:S(2)}, u32[]{:S(2)}) collective-permute-start(f16[2,72,128]{2,1,0:T(8,128)(2,1)S(1)} %get-tuple-element.79), channel_id=1, source_target_pairs={{0,96},{32,0},{64,32},{96,64},{1,97},{33,1},{65,33},{97,65},{2,98}... | collective-permute-start | bytes 110600 | tf_op jit(solution)/shard_map/ppermute | solution.py:38
  79.5 4.4 %collective-permute-start.9 = (f16[2,72,128]{2,1,0:T(8,128)(2,1)S(1)}, f16[2,72,128]{2,1,0:T(8,128)(2,1)S(1)}, u32[]{:S(2)}, u32[]{:S(2)}) collective-permute-start(f16[2,72,128]{2,1,0:T(8,128)(2,1)S(1)} %get-tuple-element.80), channel_id=1, source_target_pairs={{0,32},{32,64},{64,96},{96,0},{1,33},{33,65},{65,97},{97,1},{2,34}... | collective-permute-start | bytes 110600 | tf_op jit(solution)/shard_map/ppermute | solution.py:38
  79.5 5.0 %collective-permute-start.8 = (f16[2,72,128]{2,1,0:T(8,128)(2,1)S(1)}, f16[2,72,128]{2,1,0:T(8,128)(2,1)S(1)}, u32[]{:S(2)}, u32[]{:S(2)}) collective-permute-start(f16[2,72,128]{2,1,0:T(8,128)(2,1)S(1)} %get-tuple-element.81), channel_id=1, source_target_pairs={{0,64},{32,96},{64,0},{96,32},{1,65},{33,97},{65,1},{97,33},{2,66}... | collective-permute-start | bytes 110600 | tf_op jit(solution)/shard_map/ppermute | solution.py:38

commit v4 on v3

--- a/solution.py
+++ b/solution.py
@@ -8,6 +8,7 @@
 from jax.sharding import Mesh
 from jax.sharding import PartitionSpec as P
 
+
 FSDP = ("x", "z", "y", "c")
 FSDP_GROUP = ("x", "z", "y", "c", "group")
 NX, NZ, NY, NC, NG = 4, 8, 2, 2, 2
@@ -23,11 +24,12 @@
 WIRE = jnp.float16
 F32 = jnp.float32
 PEAK = 128.0
-ROWS_A = 184
+ROWS_A = 176
 LANES = 128
 BLOCK = 1024
 AHEAD = 4
 ORDER = (2, 1, 3, 0)
+FAR = (4, 3, 5, 2, 6, 1, 7)
 
 
 def swap(a, axis):
@@ -38,11 +40,7 @@
     return lax.ppermute(a, axis, [(i, (i + k) % size) for i in range(size)])
 
 
-def pick(a, i):
-    return lax.dynamic_index_in_dim(a, i, 0, False)
-
-
-def terms_kernel(scale, which, place, cot, acts, *refs):
+def terms_kernel(scale, which, place, layer, cot, acts, *refs):
     outs, out_b = refs[:NX], refs[NX]
     upstream, held, mine, arrived, ready, left = refs[NX + 1 :]
     outs = (*outs[:-1], mine)
@@ -75,6 +73,7 @@
         for j in range(BLOCK // LANES):
             z, y = divmod(j, NY)
             z += i % per * (NZ // per)
+            z = lax.rem(z + NZ - layer[0], NZ)
             piece = out[:, j * LANES : (j + 1) * LANES]
             outs[i // per][z, y] = piece[:ROWS_A]
             out_b[z, i // per, y] = piece[ROWS_A:]
@@ -83,14 +82,14 @@
     last.wait()
 
 
-def terms(inputs, upstream, which, x):
+def terms(inputs, upstream, which, x, z):
     tokens, width = inputs.shape
     half = upstream.shape[1] // NC
     steps = width // BLOCK
     vmem = pl.BlockSpec(memory_space=pltpu.VMEM)
     return pl.pallas_call(
         functools.partial(terms_kernel, PEAK / (tokens * NC)),
-        in_specs=[pl.BlockSpec(memory_space=pltpu.SMEM)] * 2
+        in_specs=[pl.BlockSpec(memory_space=pltpu.SMEM)] * 3
         + [pl.BlockSpec(memory_space=pl.ANY)] * 2,
         out_specs=[vmem] * (NX - 1) + [pl.BlockSpec(memory_space=pl.ANY), vmem],
         scratch_shapes=[
@@ -114,6 +113,7 @@
     )(
         which[None],
         x[None],
+        z[None],
         pltpu.with_memory_space_constraint(upstream, pltpu.HBM),
         pltpu.with_memory_space_constraint(inputs, pltpu.HBM),
     )
@@ -193,13 +193,13 @@
     half = upstream.shape[1] // NC
     rows = inner_params.shape[1]
 
-    *theirs_a, theirs_b = terms(inputs, upstream, 1 - core, x)
+    *theirs_a, theirs_b = terms(inputs, upstream, 1 - core, x, z)
     got_a = []
     for a in theirs_a:
         got_a.append(swap(a, "c"))
     got_b = swap(theirs_b, "c")
     inputs, upstream, _ = lax.optimization_barrier((inputs, upstream, theirs_b))
-    *own_a, own_b = terms(inputs, upstream, core, x)
+    *own_a, own_b = terms(inputs, upstream, core, x, z)
     counts = group_tokens.astype(F32)
     steps = inner_steps.astype(F32)
     facts = jnp.stack(
@@ -220,8 +220,11 @@
     wire = (own_a[0] + got_a[0]).astype(WIRE)
     sent_0 = send(wire, 0)
     _, own_b, got_b = lax.optimization_barrier((wire, own_b, got_b))
-    wire = (own_b + got_b).astype(WIRE)
-    back_b = lax.all_to_all(wire, "z", 0, 0, tiled=True)
+    wire = [(own_b[k] + got_b[k]).astype(WIRE) for k in FAR]
+    back_b = {}
+    for k, w in zip(FAR, wire):
+        back_b[k] = around(w, "z", k, NZ)
+    second = own_b[0] + got_b[0]
     sent = [sent_0]
     for n in range(1, NX - 1):
         _, own, got = lax.optimization_barrier((wire, own_a[n], got_a[n]))
@@ -237,13 +240,19 @@
     )(*gated)
     far = swap(packed, "group")
 
-    sent, back_b, far, facts = lax.optimization_barrier((sent, back_b, far, facts))
+    sent, far, facts = lax.optimization_barrier((sent, far, facts))
     first = own_a[-1] + got_a[-1]
     for w in sent:
         first = first + w.astype(F32)
     first = first * (1.0 / NX)
-    back_a = lax.all_to_all(first.astype(WIRE), "z", 0, 0, tiled=True)
-    second = back_b.astype(F32).sum(0) * (1.0 / NZ)
+    wire = [first[k].astype(WIRE) for k in FAR]
+    back_a = []
+    for k, w in zip(FAR, wire):
+        back_a.append(around(w, "z", k, NZ))
+    first = first[0]
+    for k in FAR:
+        second = second + back_b[k].astype(F32)
+    second = second * (1.0 / NZ)
     wires = [second[n].astype(WIRE) for n in range(NX - 1)]
     sent_b = [around(wires[n], "x", ORDER[n], NX) for n in range(NX - 1)]
     second = second[-1]
@@ -251,9 +260,9 @@
     for w in sent_b:
         second = second + w.astype(F32)
     second = second * (1.0 / NX)
-    place = lax.broadcasted_iota(jnp.int32, (NZ, 1, 1, 1), 0)
-    back_a = jnp.where(place == z, 0.0, back_a.astype(F32)).sum(0)
-    first = (back_a + pick(first, z)) * (1.0 / NZ)
+    for w in back_a:
+        first = first + w.astype(F32)
+    first = first * (1.0 / NZ)
 
     part = pl.pallas_call(
         turn_kernel,

time: 119 us -> 124 us (1.042)
  the two profiles are of different devices: /device:TPU:1 before, /device:TPU:0 now
where the time goes in v4:
time: 124 us; the launch traced here: 122 us
  starting transfers between devices  46.6 us (38%)
  waiting for transfers between devices  29.1 us (23%)
  Pallas kernels  17.6 us (14%)
  blocking collectives  14.9 us (12%)
  other arithmetic  11.3 us (9%)
  local copies, waits for them, and re-layouts  1.69 us (1%)
    ppermute x20, starting transfers between devices, around(): return lax.ppermute(a, axis, [(i, (i + k) % size) for i in range(size)])  42.1 us
    ppermute x20, waiting for transfers between devices, around(): return lax.ppermute(a, axis, [(i, (i + k) % size) for i in range(size)])  20 us
    all_to_all x1, blocking collectives, per_device(): got = lax.all_to_all(part, ('group', 'y', 'c'), 0, 0, tiled=True)  14.9 us
    pallas_call x2, Pallas kernels, terms(): pl.pallas_call(functools.partial(terms_kernel, PEAK / (tokens * NC)), in_...  11.5 us
    ppermute x6, waiting for transfers between devices, swap(): return lax.ppermute(a, axis, [(0, 1), (1, 0)])  9.09 us
    ppermute x6, starting transfers between devices, swap(): return lax.ppermute(a, axis, [(0, 1), (1, 0)])  4.46 us
    another operation x2, other arithmetic  4.04 us
  transfers between devices with their start and end apart: 26, of which 10 were waited for; matrix products, arithmetic and copies ran while one was open for 7% of the time, Pallas kernels for 6%

profile of v4, /device:TPU:0, one launch (start us, length us, event | category | flops | bytes accessed | tf_op | source)
XLA Modules:
  0.0 122.0 jit_solution(16211043315874051939)
XLA Ops:
  0.6 5.7 %terms.2 = (f32[8,2,176,128]{3,2,1,0:T(8,128)S(1)}, f32[8,2,176,128]{3,2,1,0:T(8,128)S(1)}, f32[8,2,176,128]{3,2,1,0:T(8,128)S(1)}, f32[8,2,176,128]{3,2,1,0:T(8,128)}, f32[8,4,2,80,128]{4,3,2,1,0:T(8,128)S(1)}) custom-call(s32[1]{0:T(128)} %bitcast.6.which, s32[1]{0:T(128)} %bitcast.2.place, s32[1]{0:T(128)} %bitcast.3.layer, bf16[512,512]{1,0:T(8,128)(2,1)} %bitcast.98, ...), custom_call_target="tpu_custom_call" | custom-call | flops 2147483648 | bytes 16777216 | tf_op jit(solution)/shard_map/terms/pallas_call | solution.py:90
  6.5 0.5 collective-permute-start
  7.1 0.4 collective-permute-start.5
  7.6 0.6 convert_reduce_fusion
  8.2 5.7 %terms.3 = (f32[8,2,176,128]{3,2,1,0:T(8,128)S(1)}, f32[8,2,176,128]{3,2,1,0:T(8,128)S(1)}, f32[8,2,176,128]{3,2,1,0:T(8,128)S(1)}, f32[8,2,176,128]{3,2,1,0:T(8,128)}, f32[8,4,2,80,128]{4,3,2,1,0:T(8,128)S(1)}) custom-call(s32[1]{0:T(128)} %bitcast.1.which, s32[1]{0:T(128)} %bitcast.2.place, s32[1]{0:T(128)} %bitcast.3.layer, bf16[512,512]{1,0:T(8,128)(2,1)} %bitcast.99, ...), custom_call_target="tpu_custom_call" | custom-call | flops 2147483648 | bytes 16777216 | tf_op jit(solution)/shard_map/terms/pallas_call | solution.py:90
  13.9 1.1 add_convert_fusion.2
  15.0 1.4 %fusion.21 = (f16[4,2,80,128]{3,2,1,0:T(8,128)(2,1)S(1)}, f16[4,2,80,128]{3,2,1,0:T(8,128)(2,1)S(1)}, f16[4,2,80,128]{3,2,1,0:T(8,128)(2,1)S(1)}, f16[4,2,80,128...) fusion(f32[8,4,2,80,128]{4,3,2,1,0:T(8,128)S(1)} %collective-pe, ...), kind=kLoop, calls=%fused_computation.34 | loop fusion | flops 1146880 | bytes 5734400 | tf_op jit(solution)/shard_map/convert_element_type | solution.py:223
  16.5 4.1 %collective-permute-start.15 = (f16[4,2,80,128]{3,2,1,0:T(8,128)(2,1)S(1)}, f16[4,2,80,128]{3,2,1,0:T(8,128)(2,1)S(1)}, u32[]{:S(2)}, u32[]{:S(2)}) collective-permute-start(f16[4,2,80,128]{3,2,1,0:T(8,128)(2,1)S(1)} %get-tuple-element.89), channel_id=1, source_target_pairs={{0,28},{4,0},{8,4},{12,8},{16,12},{20,16},{24,20},{28,24},{1,29},{... | collective-permute-start | bytes 491528 | tf_op jit(solution)/shard_map/ppermute | solution.py:40
  20.7 2.5 %collective-permute-start.13 = (f16[4,2,80,128]{3,2,1,0:T(8,128)(2,1)S(1)}, f16[4,2,80,128]{3,2,1,0:T(8,128)(2,1)S(1)}, u32[]{:S(2)}, u32[]{:S(2)}) collective-permute-start(f16[4,2,80,128]{3,2,1,0:T(8,128)(2,1)S(1)} %get-tuple-element.91), channel_id=1, source_target_pairs={{0,24},{4,28},{8,0},{12,4},{16,8},{20,12},{24,16},{28,20},{1,25},{... | collective-permute-start | bytes 491528 | tf_op jit(solution)/shard_map/ppermute | solution.py:40
  23.2 1.0 add_convert_fusion.1
  24.2 0.5 collective-permute-start.12
  24.6 1.3 %collective-permute-done.15 = f16[4,2,80,128]{3,2,1,0:T(8,128)(2,1)S(1)} collective-permute-done((f16[4,2,80,128]{3,2,1,0:T(8,128)(2,1)S(1)}, f16[4,2,80,128]{3,2,1,0:T(8,128)(2,1)S(1)}, u32[]{:S(2)}, u32[]{:S(2)}) %collective-permute-start.15) | collective-permute-done | bytes 163872 | tf_op jit(solution)/shard_map/ppermute | solution.py:40
  26.0 3.2 %collective-permute-start.11 = (f16[4,2,80,128]{3,2,1,0:T(8,128)(2,1)S(1)}, f16[4,2,80,128]{3,2,1,0:T(8,128)(2,1)}, u32[]{:S(2)}, u32[]{:S(2)}) collective-permute-start(f16[4,2,80,128]{3,2,1,0:T(8,128)(2,1)S(1)} %get-tuple-element.93), channel_id=1, source_target_pairs={{0,20},{4,24},{8,28},{12,0},{16,4},{20,8},{24,12},{28,16},{1,21},{... | collective-permute-start | bytes 491528 | tf_op jit(solution)/shard_map/ppermute | solution.py:40
  29.2 0.6 collective-permute-start.10
  29.8 1.0 add_convert_fusion
  30.8 2.9 %collective-permute-done.13 = f16[4,2,80,128]{3,2,1,0:T(8,128)(2,1)S(1)} collective-permute-done((f16[4,2,80,128]{3,2,1,0:T(8,128)(2,1)S(1)}, f16[4,2,80,128]{3,2,1,0:T(8,128)(2,1)S(1)}, u32[]{:S(2)}, u32[]{:S(2)}) %collective-permute-start.13) | collective-permute-done | bytes 163872 | tf_op jit(solution)/shard_map/ppermute | solution.py:40
  33.7 0.7 copy-done.3
  34.4 3.0 %collective-permute-start.1 = (f16[8,2,176,128]{3,2,1,0:T(8,128)(2,1)}, f16[8,2,176,128]{3,2,1,0:T(8,128)(2,1)S(1)}, u32[]{:S(2)}, u32[]{:S(2)}) collective-permute-start(f16[8,2,176,128]{3,2,1,0:T(8,128)(2,1)} %add_convert_fusion.2), channel_id=1, source_target_pairs={{0,64},{32,96},{64,0},{96,32},{1,65},{33,97},{65,1},{97,33},{2,66}... | collective-permute-start | bytes 2162696 | tf_op jit(solution)/shard_map/ppermute | solution.py:40
  37.4 3.6 %collective-permute-start.9 = (f16[4,2,80,128]{3,2,1,0:T(8,128)(2,1)}, f16[4,2,80,128]{3,2,1,0:T(8,128)(2,1)}, u32[]{:S(2)}, u32[]{:S(2)}) collective-permute-start(f16[4,2,80,128]{3,2,1,0:T(8,128)(2,1)} %get-tuple-element.95), channel_id=1, source_target_pairs={{0,16},{4,20},{8,24},{12,28},{16,0},{20,4},{24,8},{28,12},{1,17},{... | collective-permute-start | bytes 491528 | tf_op jit(solution)/shard_map/ppermute | solution.py:40
  41.0 0.6 collective-permute-done.11
  41.7 2.8 %collective-permute-start.4 = (f16[8,2,176,128]{3,2,1,0:T(8,128)(2,1)}, f16[8,2,176,128]{3,2,1,0:T(8,128)(2,1)}, u32[]{:S(2)}, u32[]{:S(2)}) collective-permute-start(f16[8,2,176,128]{3,2,1,0:T(8,128)(2,1)} %add_convert_fusion.1), channel_id=1, source_target_pairs={{0,32},{32,64},{64,96},{96,0},{1,33},{33,65},{65,97},{97,1},{2,34}... | collective-permute-start | bytes 2162696 | tf_op jit(solution)/shard_map/ppermute | solution.py:40
  44.4 2.4 %collective-permute-done.10 = f16[4,2,80,128]{3,2,1,0:T(8,128)(2,1)} collective-permute-done((f16[4,2,80,128]{3,2,1,0:T(8,128)(2,1)S(1)}, f16[4,2,80,128]{3,2,1,0:T(8,128)(2,1)}, u32[]{:S(2)}, u32[]{:S(2)}) %collective-permute-start.10) | collective-permute-done | bytes 163872 | tf_op jit(solution)/shard_map/ppermute | solution.py:40
  46.8 3.0 %collective-permute-start.6 = (f16[8,2,176,128]{3,2,1,0:T(8,128)(2,1)}, f16[8,2,176,128]{3,2,1,0:T(8,128)(2,1)}, u32[]{:S(2)}, u32[]{:S(2)}) collective-permute-start(f16[8,2,176,128]{3,2,1,0:T(8,128)(2,1)} %add_convert_fusion), channel_id=1, source_target_pairs={{0,96},{32,0},{64,32},{96,64},{1,97},{33,1},{65,33},{97,65},{2,98}... | collective-permute-start | bytes 2162696 | tf_op jit(solution)/shard_map/ppermute | solution.py:40
  49.9 0.7 subtract_bitcast_fusion.1
  50.5 1.9 %pack.1 = f32[256,512]{1,0:T(8,128)} custom-call(f32[64,512]{1,0:T(8,128)} %bitcast.100, f32[64,512]{1,0:T(8,128)} %bitcast.102, f32[64,512]{1,0:T(8,128)} %bitcast.104, f32[32,512]{1,0:T(8,128)} %a0.1, f32[32,512]{1,0:T(8,128)} %w0.1), custom_call_target="tpu_custom_call" | custom-call | tf_op jit(solution)/shard_map/pack/pallas_call | solution.py:234
  52.4 3.3 %collective-permute-start.7 = (f32[256,512]{1,0:T(8,128)}, f32[256,512]{1,0:T(8,128)}, u32[]{:S(2)}, u32[]{:S(2)}) collective-permute-start(f32[256,512]{1,0:T(8,128)} %pack.1), channel_id=1, source_target_pairs={{0,128},{128,0},{1,129},{129,1},{2,130},{130,2},{3,131},{131,3},{4... | collective-permute-start | bytes 1572872 | tf_op jit(solution)/shard_map/ppermute | solution.py:36
  55.9 0.6 reshape.34.facts
  56.5 1.7 %fusion.27 = (f16[4,2,80,128]{3,2,1,0:T(8,128)(2,1)S(1)}, f32[4,2,80,128]{3,2,1,0:T(8,128)S(1)}) fusion(f16[4,2,80,128]{3,2,1,0:T(8,128)(2,1)S(1)} %collective-permute-done.15, f16[4,2,80,128]{3,2,1,0:T(8,128)(2,1)} %copy-done.2, f16[4,2,80,128]{3,2,1,0:T(8,128)(2,1)} %copy-done.3, f16[4,2,80,128]{3,2,1,0:T(8,128)(2,1)} %collective-permute-done.12, ...), kind=kLoop, calls=%fused_computation.57 | loop fusion | flops 1392640 | bytes 2293760 | tf_op jit(solution)/shard_map/convert.9
  58.2 9.1 %collective-permute-done.7.far = f32[256,512]{1,0:T(8,128)} collective-permute-done((f32[256,512]{1,0:T(8,128)}, f32[256,512]{1,0:T(8,128)}, u32[]{:S(2)}, u32[]{:S(2)}) %collective-permute-start.7) | collective-permute-done | bytes 524320 | tf_op jit(solution)/shard_map/ppermute | solution.py:36
  67.3 2.1 %collective-permute-done.6 = f16[8,2,176,128]{3,2,1,0:T(8,128)(2,1)} collective-permute-done((f16[8,2,176,128]{3,2,1,0:T(8,128)(2,1)}, f16[8,2,176,128]{3,2,1,0:T(8,128)(2,1)}, u32[]{:S(2)}, u32[]{:S(2)}) %collective-permute-start.6) | collective-permute-done | bytes 720928 | tf_op jit(solution)/shard_map/ppermute | solution.py:40
  69.4 2.3 %fusion.26 = (f16[8,2,176,128]{3,2,1,0:T(8,128)(2,1)S(1)}, f32[8,2,176,128]{3,2,1,0:T(8,128)S(1)}) fusion(f16[8,2,176,128]{3,2,1,0:T(8,128)(2,1)} %collective-permute-done.6, f16[8,2,176,128]{3,2,1,0:T(8,128)(2,1)} %collective-permute-done.4, f16[8,2,176,128]{3,2,1,0:T(8,128)(2,1)S(1)} %collective-permute-done.1, f32[8,2,176,128]{3,2,1,0:T(8,128)S(1)} %copy-done.1, ...), kind=kLoop, calls=%fused_computation.56 | loop fusion | flops 3244032 | bytes 7208960 | tf_op jit(solution)/shard_map/convert.6
  71.9 4.3 %collective-permute-start.25 = (f16[2,176,128]{2,1,0:T(8,128)(2,1)S(1)}, f16[2,176,128]{2,1,0:T(8,128)(2,1)S(1)}, u32[]{:S(2)}, u32[]{:S(2)}) collective-permute-start(f16[2,176,128]{2,1,0:T(8,128)(2,1)S(1)} %get-tuple-element.96), channel_id=1, source_target_pairs={{0,28},{4,0},{8,4},{12,8},{16,12},{20,16},{24,20},{28,24},{1,29},{... | collective-permute-start | bytes 270344 | tf_op jit(solution)/shard_map/ppermute | solution.py:40
  76.2 2.7 %collective-permute-start.18 = (f16[2,80,128]{2,1,0:T(8,128)(2,1)S(1)}, f16[2,80,128]{2,1,0:T(8,128)(2,1)S(1)}, u32[]{:S(2)}, u32[]{:S(2)}) collective-permute-start(f16[2,80,128]{2,1,0:T(8,128)(2,1)S(1)} %get-tuple-element.103), channel_id=1, source_target_pairs={{0,96},{32,0},{64,32},{96,64},{1,97},{33,1},{65,33},{97,65},{2,98}... | collective-permute-start | bytes 122888 | tf_op jit(solution)/shard_map/ppermute | solution.py:40
  78.9 2.3 %collective-permute-start.16 = (f16[2,80,128]{2,1,0:T(8,128)(2,1)S(1)}, f16[2,80,128]{2,1,0:T(8,128)(2,1)S(1)}, u32[]{:S(2)}, u32[]{:S(2)}) collective-permute-start(f16[2,80,128]{2,1,0:T(8,128)(2,1)S(1)} %get-tuple-element.105), channel_id=1, source_target_pairs={{0,64},{32,96},{64,0},{96,32},{1,65},{33,97},{65,1},{97,33},{2,66}... | collective-permute-start | bytes 122888 | tf_op jit(solution)/shard_map/ppermute | solution.py:40
  81.2 1.5 %collective-permute-start.23 = (f16[2,176,128]{2,1,0:T(8,128)(2,1)S(1)}, f16[2,176,128]{2,1,0:T(8,128)(2,1)S(1)}, u32[]{:S(2)}, u32[]{:S(2)}) collective-permute-start(f16[2,176,128]{2,1,0:T(8,128)(2,1)S(1)} %get-tuple-element.98), channel_id=1, source_target_pairs={{0,24},{4,28},{8,0},{12,4},{16,8},{20,12},{24,16},{28,20},{1,25},{... | collective-permute-start | bytes 270344 | tf_op jit(solution)/shard_map/ppermute | solution.py:40
  82.8 1.8 %collective-permute-done.17 = f16[2,80,128]{2,1,0:T(8,128)(2,1)S(1)} collective-permute-done((f16[2,80,128]{2,1,0:T(8,128)(2,1)S(1)}, f16[2,80,128]{2,1,0:T(8,128)(2,1)S(1)}, u32[]{:S(2)}, u32[]{:S(2)}) %collective-permute-start.17) | collective-permute-done | bytes 40992 | tf_op jit(solution)/shard_map/ppermute | solution.py:40
  84.6 3.3 %collective-permute-start.22 = (f16[2,176,128]{2,1,0:T(8,128)(2,1)S(1)}, f16[2,176,128]{2,1,0:T(8,128)(2,1)S(1)}, u32[]{:S(2)}, u32[]{:S(2)}) collective-permute-start(f16[2,176,128]{2,1,0:T(8,128)(2,1)S(1)} %get-tuple-element.99), channel_id=1, source_target_pairs={{0,8},{4,12},{8,16},{12,20},{16,24},{20,28},{24,0},{28,4},{1,9},{5... | collective-permute-start | bytes 270344 | tf_op jit(solution)/shard_map/ppermute | solution.py:40
  87.9 2.3 %collective-permute-start.21 = (f16[2,176,128]{2,1,0:T(8,128)(2,1)S(1)}, f16[2,176,128]{2,1,0:T(8,128)(2,1)S(1)}, u32[]{:S(2)}, u32[]{:S(2)}) collective-permute-start(f16[2,176,128]{2,1,0:T(8,128)(2,1)S(1)} %get-tuple-element.100), channel_id=1, source_target_pairs={{0,20},{4,24},{8,28},{12,0},{16,4},{20,8},{24,12},{28,16},{1,21},{... | collective-permute-start | bytes 270344 | tf_op jit(solution)/shard_map/ppermute | solution.py:40
  90.2 1.5 %collective-permute-start.20 = (f16[2,176,128]{2,1,0:T(8,128)(2,1)S(1)}, f16[2,176,128]{2,1,0:T(8,128)(2,1)S(1)}, u32[]{:S(2)}, u32[]{:S(2)}) collective-permute-start(f16[2,176,128]{2,1,0:T(8,128)(2,1)S(1)} %get-tuple-element.101), channel_id=1, source_target_pairs={{0,12},{4,16},{8,20},{12,24},{16,28},{20,0},{24,4},{28,8},{1,13},{... | collective-permute-start | bytes 270344 | tf_op jit(solution)/shard_map/ppermute | solution.py:40
  91.7 0.8 collective-permute-start.19
  92.5 1.5 %collective-permute-done.22 = f16[2,176,128]{2,1,0:T(8,128)(2,1)S(1)} collective-permute-done((f16[2,176,128]{2,1,0:T(8,128)(2,1)S(1)}, f16[2,176,128]{2,1,0:T(8,128)(2,1)S(1)}, u32[]{:S(2)}, u32[]{:S(2)}) %collective-permute-start.22) | collective-permute-done | bytes 90144 | tf_op jit(solution)/shard_map/ppermute | solution.py:40
  94.1 5.3 %collective-permute-done.21 = f16[2,176,128]{2,1,0:T(8,128)(2,1)S(1)} collective-permute-done((f16[2,176,128]{2,1,0:T(8,128)(2,1)S(1)}, f16[2,176,128]{2,1,0:T(8,128)(2,1)S(1)}, u32[]{:S(2)}, u32[]{:S(2)}) %collective-permute-start.21) | collective-permute-done | bytes 90144 | tf_op jit(solution)/shard_map/ppermute | solution.py:40
  99.4 2.0 %collective-permute-done.19 = f16[2,176,128]{2,1,0:T(8,128)(2,1)S(1)} collective-permute-done((f16[2,176,128]{2,1,0:T(8,128)(2,1)S(1)}, f16[2,176,128]{2,1,0:T(8,128)(2,1)S(1)}, u32[]{:S(2)}, u32[]{:S(2)}) %collective-permute-start.19) | collective-permute-done | bytes 90144 | tf_op jit(solution)/shard_map/ppermute | solution.py:40
  101.4 0.7 fusion.25.second
  102.0 0.8 fusion.14.first
  102.8 1.9 %turn.1 = f32[8,64,256]{2,1,0:T(8,128)} custom-call(f32[2,176,128]{2,1,0:T(8,128)} %fusion.14.first, f32[2,80,128]{2,1,0:T(8,128)} %fusion.25.second), custom_call_target="tpu_custom_call" | custom-call | tf_op jit(solution)/shard_map/turn/pallas_call | solution.py:267
  104.7 14.9 %all_to_all.5.got = f32[8,64,256]{2,1,0:T(8,128)} all-to-all(f32[8,64,256]{2,1,0:T(8,128)} %turn.1), channel_id=1, replica_groups=mesh['group'=2,'x'=4,'z'=8,'y'=2,'c'=2] {'group','y','c'}, dimensions={0} | all-to-all | bytes 1048576 | tf_op jit(solution)/shard_map/all_to_all | solution.py:272
  119.6 2.4 %final.1 = (f32[32,512]{1,0:T(8,128)}, f32[32,512]{1,0:T(8,128)}, bf16[64,512]{1,0:T(8,128)(2,1)}) custom-call(s32[1]{0:T(128)} %bitcast.group, f32[6]{0:T(128)} %reshape.34.facts, f32[8,64,256]{2,1,0:T(8,128)} %all_to_all.5.got, f32[64,512]{1,0:T(8,128)} %bitcast.101, f32[64,512]{1,0:T(8,128)} %bitcast.103, f32[64,512]{1,0:T(8,128)} %bitcast.105, ...), custom_call_target="tpu_custom_call" | custom-call | tf_op jit(solution)/shard_map/final/pallas_call | solution.py:276
  (39 shorter events, 0.8 us)
Async XLA Ops:
  0.6 7.0 %copy-start.5 = (s32[2]{0:T(128)S(1)}, s32[2]{0:T(128)}, u32[]{:S(2)}) copy-start(s32[2]{0:T(128)} %param.15) | copy-start | bytes 28
  6.4 8.6 %collective-permute-start.2 = (f32[8,4,2,80,128]{4,3,2,1,0:T(8,128)S(1)}, f32[8,4,2,80,128]{4,3,2,1,0:T(8,128)S(1)}, u32[]{:S(2)}, u32[]{:S(2)}) collective-permute-start(f32[8,4,2,80,128]{4,3,2,1,0:T(8,128)S(1)} %get-tuple-element.44), channel_id=1, source_target_pairs={{0,1},{1,0},{2,3},{3,2},{4,5},{5,4},{6,7},{7,6},{8,9},{9,8},{10,11... | collective-permute-start | bytes 7864328 | tf_op jit(solution)/shard_map/ppermute | solution.py:36
  6.5 7.4 %collective-permute-start = (f32[8,2,176,128]{3,2,1,0:T(8,128)S(1)}, f32[8,2,176,128]{3,2,1,0:T(8,128)S(1)}, u32[]{:S(2)}, u32[]{:S(2)}) collective-permute-start(f32[8,2,176,128]{3,2,1,0:T(8,128)S(1)} %get-tuple-element.48), channel_id=1, source_target_pairs={{0,1},{1,0},{2,3},{3,2},{4,5},{5,4},{6,7},{7,6},{8,9},{9,8},{10,11... | collective-permute-start | bytes 4325384 | tf_op jit(solution)/shard_map/ppermute | solution.py:36
  7.0 13.7 %collective-permute-start.3 = (f32[8,2,176,128]{3,2,1,0:T(8,128)S(1)}, f32[8,2,176,128]{3,2,1,0:T(8,128)S(1)}, u32[]{:S(2)}, u32[]{:S(2)}) collective-permute-start(f32[8,2,176,128]{3,2,1,0:T(8,128)S(1)} %get-tuple-element.53), channel_id=1, source_target_pairs={{0,1},{1,0},{2,3},{3,2},{4,5},{5,4},{6,7},{7,6},{8,9},{9,8},{10,11... | collective-permute-start | bytes 4325384 | tf_op jit(solution)/shard_map/ppermute | solution.py:36
  7.1 17.1 %collective-permute-start.5 = (f32[8,2,176,128]{3,2,1,0:T(8,128)S(1)}, f32[8,2,176,128]{3,2,1,0:T(8,128)S(1)}, u32[]{:S(2)}, u32[]{:S(2)}) collective-permute-start(f32[8,2,176,128]{3,2,1,0:T(8,128)S(1)} %get-tuple-element.57), channel_id=1, source_target_pairs={{0,1},{1,0},{2,3},{3,2},{4,5},{5,4},{6,7},{7,6},{8,9},{9,8},{10,11... | collective-permute-start | bytes 4325384 | tf_op jit(solution)/shard_map/ppermute | solution.py:36
  7.5 61.9 %collective-permute-start.8 = (f32[8,2,176,128]{3,2,1,0:T(8,128)}, f32[8,2,176,128]{3,2,1,0:T(8,128)}, u32[]{:S(2)}, u32[]{:S(2)}) collective-permute-start(f32[8,2,176,128]{3,2,1,0:T(8,128)} %get-tuple-element.67), channel_id=1, source_target_pairs={{0,1},{1,0},{2,3},{3,2},{4,5},{5,4},{6,7},{7,6},{8,9},{9,8},{10,11... | collective-permute-start | bytes 4325384 | tf_op jit(solution)/shard_map/ppermute | solution.py:36
  15.0 1.5 %copy-start = (f32[8,4,2,80,128]{4,3,2,1,0:T(8,128)}, f32[8,4,2,80,128]{4,3,2,1,0:T(8,128)S(1)}, u32[]{:S(2)}) copy-start(f32[8,4,2,80,128]{4,3,2,1,0:T(8,128)S(1)} %collective-permute-done.2) | copy-start | bytes 7864324
  16.5 9.4 %collective-permute-start.15 = (f16[4,2,80,128]{3,2,1,0:T(8,128)(2,1)S(1)}, f16[4,2,80,128]{3,2,1,0:T(8,128)(2,1)S(1)}, u32[]{:S(2)}, u32[]{:S(2)}) collective-permute-start(f16[4,2,80,128]{3,2,1,0:T(8,128)(2,1)S(1)} %get-tuple-element.89), channel_id=1, source_target_pairs={{0,28},{4,0},{8,4},{12,8},{16,12},{20,16},{24,20},{28,24},{1,29},{... | collective-permute-start | bytes 491528 | tf_op jit(solution)/shard_map/ppermute | solution.py:40
  20.7 8.5 %collective-permute-start.14 = (f16[4,2,80,128]{3,2,1,0:T(8,128)(2,1)S(1)}, f16[4,2,80,128]{3,2,1,0:T(8,128)(2,1)S(1)}, u32[]{:S(2)}, u32[]{:S(2)}) collective-permute-start(f16[4,2,80,128]{3,2,1,0:T(8,128)(2,1)S(1)} %get-tuple-element.90), channel_id=1, source_target_pairs={{0,4},{4,8},{8,12},{12,16},{16,20},{20,24},{24,28},{28,0},{1,5},{5... | collective-permute-start | bytes 491528 | tf_op jit(solution)/shard_map/ppermute | solution.py:40
  20.7 13.0 %collective-permute-start.13 = (f16[4,2,80,128]{3,2,1,0:T(8,128)(2,1)S(1)}, f16[4,2,80,128]{3,2,1,0:T(8,128)(2,1)S(1)}, u32[]{:S(2)}, u32[]{:S(2)}) collective-permute-start(f16[4,2,80,128]{3,2,1,0:T(8,128)(2,1)S(1)} %get-tuple-element.91), channel_id=1, source_target_pairs={{0,24},{4,28},{8,0},{12,4},{16,8},{20,12},{24,16},{28,20},{1,25},{... | collective-permute-start | bytes 491528 | tf_op jit(solution)/shard_map/ppermute | solution.py:40
  24.2 13.2 %collective-permute-start.12 = (f16[4,2,80,128]{3,2,1,0:T(8,128)(2,1)S(1)}, f16[4,2,80,128]{3,2,1,0:T(8,128)(2,1)}, u32[]{:S(2)}, u32[]{:S(2)}) collective-permute-start(f16[4,2,80,128]{3,2,1,0:T(8,128)(2,1)S(1)} %get-tuple-element.92), channel_id=1, source_target_pairs={{0,8},{4,12},{8,16},{12,20},{16,24},{20,28},{24,0},{28,4},{1,9},{5... | collective-permute-start | bytes 491528 | tf_op jit(solution)/shard_map/ppermute | solution.py:40
  24.6 25.2 %copy-start.4 = (s32[2]{0:T(128)S(1)}, s32[2]{0:T(128)}, u32[]{:S(2)}) copy-start(s32[2]{0:T(128)} %param.14) | copy-start | bytes 28
  26.0 15.7 %collective-permute-start.11 = (f16[4,2,80,128]{3,2,1,0:T(8,128)(2,1)S(1)}, f16[4,2,80,128]{3,2,1,0:T(8,128)(2,1)}, u32[]{:S(2)}, u32[]{:S(2)}) collective-permute-start(f16[4,2,80,128]{3,2,1,0:T(8,128)(2,1)S(1)} %get-tuple-element.93), channel_id=1, source_target_pairs={{0,20},{4,24},{8,28},{12,0},{16,4},{20,8},{24,12},{28,16},{1,21},{... | collective-permute-start | bytes 491528 | tf_op jit(solution)/shard_map/ppermute | solution.py:40
  29.2 1.6 %copy-start.2 = (f16[4,2,80,128]{3,2,1,0:T(8,128)(2,1)}, f16[4,2,80,128]{3,2,1,0:T(8,128)(2,1)S(1)}, u32[]{:S(2)}) copy-start(f16[4,2,80,128]{3,2,1,0:T(8,128)(2,1)S(1)} %collective-permute-done.14) | copy-start | bytes 491524
  29.2 17.6 %collective-permute-start.10 = (f16[4,2,80,128]{3,2,1,0:T(8,128)(2,1)S(1)}, f16[4,2,80,128]{3,2,1,0:T(8,128)(2,1)}, u32[]{:S(2)}, u32[]{:S(2)}) collective-permute-start(f16[4,2,80,128]{3,2,1,0:T(8,128)(2,1)S(1)} %get-tuple-element.94), channel_id=1, source_target_pairs={{0,12},{4,16},{8,20},{12,24},{16,28},{20,0},{24,4},{28,8},{1,13},{... | collective-permute-start | bytes 491528 | tf_op jit(solution)/shard_map/ppermute | solution.py:40
  33.7 0.7 copy-start.3
  34.4 23.8 %collective-permute-start.1 = (f16[8,2,176,128]{3,2,1,0:T(8,128)(2,1)}, f16[8,2,176,128]{3,2,1,0:T(8,128)(2,1)S(1)}, u32[]{:S(2)}, u32[]{:S(2)}) collective-permute-start(f16[8,2,176,128]{3,2,1,0:T(8,128)(2,1)} %add_convert_fusion.2), channel_id=1, source_target_pairs={{0,64},{32,96},{64,0},{96,32},{1,65},{33,97},{65,1},{97,33},{2,66}... | collective-permute-start | bytes 2162696 | tf_op jit(solution)/shard_map/ppermute | solution.py:40
  37.4 15.0 %collective-permute-start.9 = (f16[4,2,80,128]{3,2,1,0:T(8,128)(2,1)}, f16[4,2,80,128]{3,2,1,0:T(8,128)(2,1)}, u32[]{:S(2)}, u32[]{:S(2)}) collective-permute-start(f16[4,2,80,128]{3,2,1,0:T(8,128)(2,1)} %get-tuple-element.95), channel_id=1, source_target_pairs={{0,16},{4,20},{8,24},{12,28},{16,0},{20,4},{24,8},{28,12},{1,17},{... | collective-permute-start | bytes 491528 | tf_op jit(solution)/shard_map/ppermute | solution.py:40
  41.7 27.7 %collective-permute-start.4 = (f16[8,2,176,128]{3,2,1,0:T(8,128)(2,1)}, f16[8,2,176,128]{3,2,1,0:T(8,128)(2,1)}, u32[]{:S(2)}, u32[]{:S(2)}) collective-permute-start(f16[8,2,176,128]{3,2,1,0:T(8,128)(2,1)} %add_convert_fusion.1), channel_id=1, source_target_pairs={{0,32},{32,64},{64,96},{96,0},{1,33},{33,65},{65,97},{97,1},{2,34}... | collective-permute-start | bytes 2162696 | tf_op jit(solution)/shard_map/ppermute | solution.py:40
  46.8 22.6 %collective-permute-start.6 = (f16[8,2,176,128]{3,2,1,0:T(8,128)(2,1)}, f16[8,2,176,128]{3,2,1,0:T(8,128)(2,1)}, u32[]{:S(2)}, u32[]{:S(2)}) collective-permute-start(f16[8,2,176,128]{3,2,1,0:T(8,128)(2,1)} %add_convert_fusion), channel_id=1, source_target_pairs={{0,96},{32,0},{64,32},{96,64},{1,97},{33,1},{65,33},{97,65},{2,98}... | collective-permute-start | bytes 2162696 | tf_op jit(solution)/shard_map/ppermute | solution.py:40
  52.4 14.9 %collective-permute-start.7 = (f32[256,512]{1,0:T(8,128)}, f32[256,512]{1,0:T(8,128)}, u32[]{:S(2)}, u32[]{:S(2)}) collective-permute-start(f32[256,512]{1,0:T(8,128)} %pack.1), channel_id=1, source_target_pairs={{0,128},{128,0},{1,129},{129,1},{2,130},{130,2},{3,131},{131,3},{4... | collective-permute-start | bytes 1572872 | tf_op jit(solution)/shard_map/ppermute | solution.py:36
  56.5 12.9 %copy-start.1 = (f32[8,2,176,128]{3,2,1,0:T(8,128)S(1)}, f32[8,2,176,128]{3,2,1,0:T(8,128)}, u32[]{:S(2)}) copy-start(f32[8,2,176,128]{3,2,1,0:T(8,128)} %get-tuple-element.66) | copy-start | bytes 4325380
  71.9 18.3 %collective-permute-start.25 = (f16[2,176,128]{2,1,0:T(8,128)(2,1)S(1)}, f16[2,176,128]{2,1,0:T(8,128)(2,1)S(1)}, u32[]{:S(2)}, u32[]{:S(2)}) collective-permute-start(f16[2,176,128]{2,1,0:T(8,128)(2,1)S(1)} %get-tuple-element.96), channel_id=1, source_target_pairs={{0,28},{4,0},{8,4},{12,8},{16,12},{20,16},{24,20},{28,24},{1,29},{... | collective-permute-start | bytes 270344 | tf_op jit(solution)/shard_map/ppermute | solution.py:40
  76.2 15.5 %collective-permute-start.24 = (f16[2,176,128]{2,1,0:T(8,128)(2,1)S(1)}, f16[2,176,128]{2,1,0:T(8,128)(2,1)S(1)}, u32[]{:S(2)}, u32[]{:S(2)}) collective-permute-start(f16[2,176,128]{2,1,0:T(8,128)(2,1)S(1)} %get-tuple-element.97), channel_id=1, source_target_pairs={{0,4},{4,8},{8,12},{12,16},{16,20},{20,24},{24,28},{28,0},{1,5},{5... | collective-permute-start | bytes 270344 | tf_op jit(solution)/shard_map/ppermute | solution.py:40
  76.2 5.0 %collective-permute-start.18 = (f16[2,80,128]{2,1,0:T(8,128)(2,1)S(1)}, f16[2,80,128]{2,1,0:T(8,128)(2,1)S(1)}, u32[]{:S(2)}, u32[]{:S(2)}) collective-permute-start(f16[2,80,128]{2,1,0:T(8,128)(2,1)S(1)} %get-tuple-element.103), channel_id=1, source_target_pairs={{0,96},{32,0},{64,32},{96,64},{1,97},{33,1},{65,33},{97,65},{2,98}... | collective-permute-start | bytes 122888 | tf_op jit(solution)/shard_map/ppermute | solution.py:40
  78.9 5.7 %collective-permute-start.17 = (f16[2,80,128]{2,1,0:T(8,128)(2,1)S(1)}, f16[2,80,128]{2,1,0:T(8,128)(2,1)S(1)}, u32[]{:S(2)}, u32[]{:S(2)}) collective-permute-start(f16[2,80,128]{2,1,0:T(8,128)(2,1)S(1)} %get-tuple-element.104), channel_id=1, source_target_pairs={{0,32},{32,64},{64,96},{96,0},{1,33},{33,65},{65,97},{97,1},{2,34}... | collective-permute-start | bytes 122888 | tf_op jit(solution)/shard_map/ppermute | solution.py:40
  78.9 9.0 %collective-permute-start.16 = (f16[2,80,128]{2,1,0:T(8,128)(2,1)S(1)}, f16[2,80,128]{2,1,0:T(8,128)(2,1)S(1)}, u32[]{:S(2)}, u32[]{:S(2)}) collective-permute-start(f16[2,80,128]{2,1,0:T(8,128)(2,1)S(1)} %get-tuple-element.105), channel_id=1, source_target_pairs={{0,64},{32,96},{64,0},{96,32},{1,65},{33,97},{65,1},{97,33},{2,66}... | collective-permute-start | bytes 122888 | tf_op jit(solution)/shard_map/ppermute | solution.py:40
  81.2 11.3 %collective-permute-start.23 = (f16[2,176,128]{2,1,0:T(8,128)(2,1)S(1)}, f16[2,176,128]{2,1,0:T(8,128)(2,1)S(1)}, u32[]{:S(2)}, u32[]{:S(2)}) collective-permute-start(f16[2,176,128]{2,1,0:T(8,128)(2,1)S(1)} %get-tuple-element.98), channel_id=1, source_target_pairs={{0,24},{4,28},{8,0},{12,4},{16,8},{20,12},{24,16},{28,20},{1,25},{... | collective-permute-start | bytes 270344 | tf_op jit(solution)/shard_map/ppermute | solution.py:40
  84.6 9.5 %collective-permute-start.22 = (f16[2,176,128]{2,1,0:T(8,128)(2,1)S(1)}, f16[2,176,128]{2,1,0:T(8,128)(2,1)S(1)}, u32[]{:S(2)}, u32[]{:S(2)}) collective-permute-start(f16[2,176,128]{2,1,0:T(8,128)(2,1)S(1)} %get-tuple-element.99), channel_id=1, source_target_pairs={{0,8},{4,12},{8,16},{12,20},{16,24},{20,28},{24,0},{28,4},{1,9},{5... | collective-permute-start | bytes 270344 | tf_op jit(solution)/shard_map/ppermute | solution.py:40
  87.9 11.5 %collective-permute-start.21 = (f16[2,176,128]{2,1,0:T(8,128)(2,1)S(1)}, f16[2,176,128]{2,1,0:T(8,128)(2,1)S(1)}, u32[]{:S(2)}, u32[]{:S(2)}) collective-permute-start(f16[2,176,128]{2,1,0:T(8,128)(2,1)S(1)} %get-tuple-element.100), channel_id=1, source_target_pairs={{0,20},{4,24},{8,28},{12,0},{16,4},{20,8},{24,12},{28,16},{1,21},{... | collective-permute-start | bytes 270344 | tf_op jit(solution)/shard_map/ppermute | solution.py:40
  90.2 9.2 %collective-permute-start.20 = (f16[2,176,128]{2,1,0:T(8,128)(2,1)S(1)}, f16[2,176,128]{2,1,0:T(8,128)(2,1)S(1)}, u32[]{:S(2)}, u32[]{:S(2)}) collective-permute-start(f16[2,176,128]{2,1,0:T(8,128)(2,1)S(1)} %get-tuple-element.101), channel_id=1, source_target_pairs={{0,12},{4,16},{8,20},{12,24},{16,28},{20,0},{24,4},{28,8},{1,13},{... | collective-permute-start | bytes 270344 | tf_op jit(solution)/shard_map/ppermute | solution.py:40
  91.7 9.6 %collective-permute-start.19 = (f16[2,176,128]{2,1,0:T(8,128)(2,1)S(1)}, f16[2,176,128]{2,1,0:T(8,128)(2,1)S(1)}, u32[]{:S(2)}, u32[]{:S(2)}) collective-permute-start(f16[2,176,128]{2,1,0:T(8,128)(2,1)S(1)} %get-tuple-element.102), channel_id=1, source_target_pairs={{0,16},{4,20},{8,24},{12,28},{16,0},{20,4},{24,8},{28,12},{1,17},{... | collective-permute-start | bytes 270344 | tf_op jit(solution)/shard_map/ppermute | solution.py:40

commit v5 on v4

--- a/solution.py
+++ b/solution.py
@@ -24,10 +24,11 @@
 WIRE = jnp.float16
 F32 = jnp.float32
 PEAK = 128.0
-ROWS_A = 176
+ROWS_A = 192
 LANES = 128
 BLOCK = 1024
 AHEAD = 4
+LIMIT = 28
 ORDER = (2, 1, 3, 0)
 FAR = (4, 3, 5, 2, 6, 1, 7)
 
@@ -40,16 +41,19 @@
     return lax.ppermute(a, axis, [(i, (i + k) % size) for i in range(size)])
 
 
-def terms_kernel(scale, which, place, layer, cot, acts, *refs):
-    outs, out_b = refs[:NX], refs[NX]
-    upstream, held, mine, arrived, ready, left = refs[NX + 1 :]
-    outs = (*outs[:-1], mine)
-    last = pltpu.make_async_copy(mine, refs[NX - 1], left)
+def terms_kernel(scale, core, place, layer, cot, acts, *refs):
+    theirs, own = refs[: NX + 1], refs[NX + 1 : 2 * NX + 2]
+    upstream, turned, held, kept, arrived, ready, left = refs[2 * NX + 2 :]
     steps = acts.shape[1] // BLOCK
     per = steps // NX
-    half = upstream.shape[1]
-
+    half = upstream.shape[1] // NC
     turns = [n * per + i for n in (0, NX - 1, *range(1, NX - 1)) for i in range(per)]
+    last = [
+        pltpu.make_async_copy(kept.at[side], refs[NX - 1], left.at[side])
+        if side == 0
+        else pltpu.make_async_copy(kept.at[side], refs[2 * NX], left.at[side])
+        for side in range(NC)
+    ]
 
     def copy(i):
         x = lax.rem(place[0] + ORDER[i // per], NX)
@@ -58,65 +62,80 @@
             acts.at[:, pl.ds(start, BLOCK)], held.at[i], arrived.at[i]
         )
 
-    first = pl.multiple_of(which[0] * half, half)
-    whole = pltpu.make_async_copy(cot.at[:, pl.ds(first, half)], upstream, ready)
+    whole = pltpu.make_async_copy(cot, upstream, ready)
     whole.start()
     for i in turns[:AHEAD]:
         copy(i).start()
     whole.wait()
-    turned = upstream[...].astype(F32).T.astype(upstream.dtype)
+    for side in range(NC):
+        which = lax.rem(core[0] + 1 + side, NC)
+        part = upstream[:, pl.ds(pl.multiple_of(which * half, half), half)]
+        turned[side * half : (side + 1) * half] = part.astype(F32).T.astype(part.dtype)
     for turn, i in enumerate(turns):
         copy(i).wait()
         if turn + AHEAD < steps:
             copy(turns[turn + AHEAD]).start()
-        out = jnp.dot(turned, held[i], preferred_element_type=F32) * scale
-        for j in range(BLOCK // LANES):
-            z, y = divmod(j, NY)
-            z += i % per * (NZ // per)
-            z = lax.rem(z + NZ - layer[0], NZ)
-            piece = out[:, j * LANES : (j + 1) * LANES]
-            outs[i // per][z, y] = piece[:ROWS_A]
-            out_b[z, i // per, y] = piece[ROWS_A:]
+        out = jnp.dot(turned[...], held[i], preferred_element_type=F32) * scale
+        n = i // per
+        for side, into in enumerate((theirs, own)):
+            rows_a = kept.at[side] if n == NX - 1 else into[n]
+            for j in range(BLOCK // LANES):
+                z, y = divmod(j, NY)
+                z += i % per * (NZ // per)
+                piece = out[
+                    side * half : (side + 1) * half, j * LANES : (j + 1) * LANES
+                ]
+                rows_a[lax.rem(z + NZ - layer[0], NZ), y] = piece[:ROWS_A]
+                into[NX][z, n, y] = piece[ROWS_A:]
         if turn == 2 * per - 1:
-            last.start()
-    last.wait()
-
-
-def terms(inputs, upstream, which, x, z):
+            for c in last:
+                c.start()
+    for c in last:
+        c.wait()
+
+
+def terms(inputs, upstream, core, x, z):
     tokens, width = inputs.shape
-    half = upstream.shape[1] // NC
+    keys = upstream.shape[1]
+    half = keys // NC
     steps = width // BLOCK
     vmem = pl.BlockSpec(memory_space=pltpu.VMEM)
-    return pl.pallas_call(
+    block_a = (NZ, NY, ROWS_A, LANES)
+    out = pl.pallas_call(
         functools.partial(terms_kernel, PEAK / (tokens * NC)),
         in_specs=[pl.BlockSpec(memory_space=pltpu.SMEM)] * 3
         + [pl.BlockSpec(memory_space=pl.ANY)] * 2,
-        out_specs=[vmem] * (NX - 1) + [pl.BlockSpec(memory_space=pl.ANY), vmem],
+        out_specs=([vmem] * (NX - 1) + [pl.BlockSpec(memory_space=pl.ANY), vmem]) * NC,
         scratch_shapes=[
-            pltpu.VMEM((tokens, half), inputs.dtype),
+            pltpu.VMEM((tokens, keys), inputs.dtype),
+            pltpu.VMEM((keys, tokens), inputs.dtype),
             pltpu.VMEM((steps, tokens, BLOCK), inputs.dtype),
-            pltpu.VMEM((NZ, NY, ROWS_A, LANES), F32),
+            pltpu.VMEM((NC,) + block_a, F32),
             pltpu.SemaphoreType.DMA((steps,)),
             pltpu.SemaphoreType.DMA,
-            pltpu.SemaphoreType.DMA,
+            pltpu.SemaphoreType.DMA((NC,)),
         ],
-        out_shape=[pltpu.VMEM((NZ, NY, ROWS_A, LANES), F32)] * (NX - 1)
-        + [pltpu.HBM((NZ, NY, ROWS_A, LANES), F32)]
-        + [pltpu.VMEM((NZ, NX, NY, half - ROWS_A, LANES), F32)],
-        compiler_params=pltpu.CompilerParams(vmem_limit_bytes=18 * 2**20),
+        out_shape=(
+            [pltpu.VMEM(block_a, F32)] * (NX - 1)
+            + [pltpu.HBM(block_a, F32)]
+            + [pltpu.VMEM((NZ, NX, NY, half - ROWS_A, LANES), F32)]
+        )
+        * NC,
+        compiler_params=pltpu.CompilerParams(vmem_limit_bytes=LIMIT * 2**20),
         cost_estimate=pl.CostEstimate(
-            flops=2 * tokens * half * width,
-            bytes_accessed=2 * tokens * width + 4 * half * width,
+            flops=2 * tokens * keys * width,
+            bytes_accessed=2 * tokens * width + 4 * keys * width,
             transcendentals=0,
         ),
         name="terms",
     )(
-        which[None],
+        core[None],
         x[None],
         z[None],
         pltpu.with_memory_space_constraint(upstream, pltpu.HBM),
         pltpu.with_memory_space_constraint(inputs, pltpu.HBM),
     )
+    return out[:NX], out[NX], out[NX + 1 : 2 * NX + 1], out[2 * NX + 1]
 
 
 def turn_kernel(first, second, out):
@@ -193,13 +212,11 @@
     half = upstream.shape[1] // NC
     rows = inner_params.shape[1]
 
-    *theirs_a, theirs_b = terms(inputs, upstream, 1 - core, x, z)
+    theirs_a, theirs_b, own_a, own_b = terms(inputs, upstream, core, x, z)
     got_a = []
     for a in theirs_a:
         got_a.append(swap(a, "c"))
     got_b = swap(theirs_b, "c")
-    inputs, upstream, _ = lax.optimization_barrier((inputs, upstream, theirs_b))
-    *own_a, own_b = terms(inputs, upstream, core, x, z)
     counts = group_tokens.astype(F32)
     steps = inner_steps.astype(F32)
     facts = jnp.stack(
@@ -220,11 +237,8 @@
     wire = (own_a[0] + got_a[0]).astype(WIRE)
     sent_0 = send(wire, 0)
     _, own_b, got_b = lax.optimization_barrier((wire, own_b, got_b))
-    wire = [(own_b[k] + got_b[k]).astype(WIRE) for k in FAR]
-    back_b = {}
-    for k, w in zip(FAR, wire):
-        back_b[k] = around(w, "z", k, NZ)
-    second = own_b[0] + got_b[0]
+    wire = (own_b + got_b).astype(WIRE)
+    back_b = lax.all_to_all(wire, "z", 0, 0, tiled=True)
     sent = [sent_0]
     for n in range(1, NX - 1):
         _, own, got = lax.optimization_barrier((wire, own_a[n], got_a[n]))
@@ -240,7 +254,9 @@
     )(*gated)
     far = swap(packed, "group")
 
-    sent, far, facts = lax.optimization_barrier((sent, far, facts))
+    sent, back_b, far, facts = lax.optimization_barrier(
+        (sent, back_b, far, facts)
+    )
     first = own_a[-1] + got_a[-1]
     for w in sent:
         first = first + w.astype(F32)
@@ -250,9 +266,7 @@
     for k, w in zip(FAR, wire):
         back_a.append(around(w, "z", k, NZ))
     first = first[0]
-    for k in FAR:
-        second = second + back_b[k].astype(F32)
-    second = second * (1.0 / NZ)
+    second = back_b.astype(F32).sum(0) * (1.0 / NZ)
     wires = [second[n].astype(WIRE) for n in range(NX - 1)]
     sent_b = [around(wires[n], "x", ORDER[n], NX) for n in range(NX - 1)]
     second = second[-1]

time: 124 us -> 120 us (0.968)
  the two profiles are of different devices: /device:TPU:0 before, /device:TPU:1 now
where the time goes in v5:
time: 120 us
  starting transfers between devices  39.1 us (33%)
  waiting for transfers between devices  33.7 us (28%)
  Pallas kernels  15.9 us (13%)
  blocking collectives  14.9 us (12%)
  other arithmetic  14.2 us (12%)
    ppermute x13, starting transfers between devices, around(): return lax.ppermute(a, axis, [(i, (i + k) % size) for i in range(size)])  25.1 us
    ppermute x13, waiting for transfers between devices, around(): return lax.ppermute(a, axis, [(i, (i + k) % size) for i in range(size)])  23 us
    all_to_all x1, blocking collectives, per_device(): got = lax.all_to_all(part, ('group', 'y', 'c'), 0, 0, tiled=True)  14.9 us
    ppermute x6, waiting for transfers between devices, swap(): return lax.ppermute(a, axis, [(0, 1), (1, 0)])  10.7 us
    pallas_call x1, Pallas kernels, terms(): pl.pallas_call(functools.partial(terms_kernel, PEAK / (tokens * NC)), in_...  9.79 us
    ppermute x6, starting transfers between devices, swap(): return lax.ppermute(a, axis, [(0, 1), (1, 0)])  7.46 us
    all_to_all x1, starting transfers between devices, per_device(): back_b = lax.all_to_all(wire, 'z', 0, 0, tiled=True)  6.48 us
    convert_element_type x2, other arithmetic, per_device(): wire = (own + got).astype(WIRE)  5.08 us
  transfers between devices with their start and end apart: 20, of which 9 were waited for; matrix products, arithmetic and copies ran while one was open for 9% of the time, Pallas kernels for 2%

profile of v5, /device:TPU:1, one launch (start us, length us, event | category | flops | bytes accessed | tf_op | source)
XLA Modules:
  0.0 119.6 jit_solution(11955168799073976201)
XLA Ops:
  0.6 9.8 %terms.1 = (f32[8,2,192,128]{3,2,1,0:T(8,128)S(1)}, f32[8,2,192,128]{3,2,1,0:T(8,128)}, f32[8,2,192,128]{3,2,1,0:T(8,128)}, f32[8,2,192,128]{3,2,1,0:T(8,128)}, ...) custom-call(s32[1]{0:T(128)} %bitcast.1.core, ...), custom_call_target="tpu_custom_call" | custom-call | flops 4294967296 | bytes 25165824 | tf_op jit(solution)/shard_map/terms/pallas_call | solution.py:104
  10.4 3.3 %collective-permute-start.2 = (f32[8,4,2,64,128]{4,3,2,1,0:T(8,128)S(1)}, f32[8,4,2,64,128]{4,3,2,1,0:T(8,128)S(1)}, u32[]{:S(2)}, u32[]{:S(2)}) collective-permute-start(f32[8,4,2,64,128]{4,3,2,1,0:T(8,128)S(1)} %get-tuple-element.46), channel_id=1, source_target_pairs={{0,1},{1,0},{2,3},{3,2},{4,5},{5,4},{6,7},{7,6},{8,9},{9,8},{10,11... | collective-permute-start | bytes 6291464 | tf_op jit(solution)/shard_map/ppermute | solution.py:37
  13.7 0.1 collective-permute-start
  13.8 0.4 collective-permute-start.3
  14.2 0.1 collective-permute-start.5
  14.3 5.4 %collective-permute-done = f32[8,2,192,128]{3,2,1,0:T(8,128)S(1)} collective-permute-done((f32[8,2,192,128]{3,2,1,0:T(8,128)S(1)}, f32[8,2,192,128]{3,2,1,0:T(8,128)S(1)}, u32[]{:S(2)}, u32[]{:S(2)}) %collective-permute-start) | collective-permute-done | bytes 1572896 | tf_op jit(solution)/shard_map/ppermute | solution.py:37
  19.8 1.1 add_convert_fusion.3
  20.9 1.5 %add_convert_fusion = f16[8,4,2,64,128]{4,3,2,1,0:T(8,128)(2,1)} fusion(f32[8,4,2,64,128]{4,3,2,1,0:T(8,128)S(1)} %get-tuple-element.47, f32[8,4,2,64,128]{4,3,2,1,0:T(8,128)S(1)} %collective-permute-done.2), kind=kLoop, calls=%fused_computation.1 | loop fusion | flops 1048576 | bytes 5242880 | tf_op jit(solution)/shard_map/convert_element_type | solution.py:240
  22.4 6.5 %all-to-all-start = ((f16[8,4,2,64,128]{4,3,2,1,0:T(8,128)(2,1)}), f16[8,4,2,64,128]{4,3,2,1,0:T(8,128)(2,1)}, u32[]{:S(2)}, u32[]{:S(2)}) async-start(f16[8,4,2,64,128]{4,3,2,1,0:T(8,128)(2,1)} %add_convert_fusion), calls=%async_computation | async-start | bytes 2097152 | tf_op jit(solution)/shard_map/all_to_all | solution.py:241
  28.9 0.7 collective-permute-start.8
  29.5 2.7 %collective-permute-start.1 = (f16[8,2,192,128]{3,2,1,0:T(8,128)(2,1)}, f16[8,2,192,128]{3,2,1,0:T(8,128)(2,1)}, u32[]{:S(2)}, u32[]{:S(2)}) collective-permute-start(f16[8,2,192,128]{3,2,1,0:T(8,128)(2,1)} %add_convert_fusion.3), channel_id=1, source_target_pairs={{0,64},{32,96},{64,0},{96,32},{1,65},{33,97},{65,1},{97,33},{2,66}... | collective-permute-start | bytes 2359304 | tf_op jit(solution)/shard_map/ppermute | solution.py:41
  32.3 2.5 %add_convert_fusion.2 = f16[8,2,192,128]{3,2,1,0:T(8,128)(2,1)} fusion(f32[8,2,192,128]{3,2,1,0:T(8,128)S(1)} %get-tuple-element.51, f32[8,2,192,128]{3,2,1,0:T(8,128)} %collective-permute-done.3), kind=kLoop, calls=%fused_computation.4 | loop fusion | flops 786432 | bytes 3932160 | tf_op jit(solution)/shard_map/convert_element_type | solution.py:245
  34.8 2.6 %add_convert_fusion.1 = f16[8,2,192,128]{3,2,1,0:T(8,128)(2,1)} fusion(f32[8,2,192,128]{3,2,1,0:T(8,128)S(1)} %get-tuple-element.55, f32[8,2,192,128]{3,2,1,0:T(8,128)} %collective-permute-done.5), kind=kLoop, calls=%fused_computation.3 | loop fusion | flops 786432 | bytes 3932160 | tf_op jit(solution)/shard_map/convert_element_type | solution.py:245
  37.4 0.9 collective-permute-start.6
  38.2 0.6 collective-permute-start.4
  38.8 0.6 convert_reduce_fusion.1
  39.4 1.9 %pack.1 = f32[256,512]{1,0:T(8,128)} custom-call(f32[64,512]{1,0:T(8,128)} %bitcast.64, f32[64,512]{1,0:T(8,128)} %bitcast.66, f32[64,512]{1,0:T(8,128)} %bitcast.68, f32[32,512]{1,0:T(8,128)} %a0.1, f32[32,512]{1,0:T(8,128)} %w0.1), custom_call_target="tpu_custom_call" | custom-call | tf_op jit(solution)/shard_map/pack/pallas_call | solution.py:248
  41.3 2.9 %collective-permute-start.7 = (f32[256,512]{1,0:T(8,128)}, f32[256,512]{1,0:T(8,128)}, u32[]{:S(2)}, u32[]{:S(2)}) collective-permute-start(f32[256,512]{1,0:T(8,128)} %pack.1), channel_id=1, source_target_pairs={{0,128},{128,0},{1,129},{129,1},{2,130},{130,2},{3,131},{131,3},{4... | collective-permute-start | bytes 1572872 | tf_op jit(solution)/shard_map/ppermute | solution.py:37
  44.2 0.7 subtract_bitcast_fusion.1
  44.9 0.1 rev.3
  45.0 0.1 copy.12
  45.1 0.7 reshape.19.facts
  45.8 4.6 %collective-permute-done.1 = f16[8,2,192,128]{3,2,1,0:T(8,128)(2,1)} collective-permute-done((f16[8,2,192,128]{3,2,1,0:T(8,128)(2,1)}, f16[8,2,192,128]{3,2,1,0:T(8,128)(2,1)}, u32[]{:S(2)}, u32[]{:S(2)}) %collective-permute-start.1) | collective-permute-done | bytes 786464 | tf_op jit(solution)/shard_map/ppermute | solution.py:41
  50.4 5.3 %collective-permute-done.7.far = f32[256,512]{1,0:T(8,128)} collective-permute-done((f32[256,512]{1,0:T(8,128)}, f32[256,512]{1,0:T(8,128)}, u32[]{:S(2)}, u32[]{:S(2)}) %collective-permute-start.7) | collective-permute-done | bytes 524320 | tf_op jit(solution)/shard_map/ppermute | solution.py:37
  55.7 11.5 %collective-permute-done.6 = f16[8,2,192,128]{3,2,1,0:T(8,128)(2,1)S(1)} collective-permute-done((f16[8,2,192,128]{3,2,1,0:T(8,128)(2,1)}, f16[8,2,192,128]{3,2,1,0:T(8,128)(2,1)S(1)}, u32[]{:S(2)}, u32[]{:S(2)}) %collective-permute-start.6) | collective-permute-done | bytes 786464 | tf_op jit(solution)/shard_map/ppermute | solution.py:41
  67.2 0.3 collective-permute-done.4
  67.6 2.2 %fusion.13 = (f16[8,2,192,128]{3,2,1,0:T(8,128)(2,1)S(1)}, f32[8,2,192,128]{3,2,1,0:T(8,128)S(1)}) fusion(f16[8,2,192,128]{3,2,1,0:T(8,128)(2,1)S(1)} %collective-permute-done.6, f16[8,2,192,128]{3,2,1,0:T(8,128)(2,1)S(1)} %collective-permute-done.4, f16[8,2,192,128]{3,2,1,0:T(8,128)(2,1)} %collective-permute-done.1, f32[8,2,192,128]{3,2,1,0:T(8,128)S(1)} %copy-done, ...), kind=kLoop, calls=%fused_computation.38 | loop fusion | flops 3538944 | bytes 7864320 | tf_op jit(solution)/shard_map/convert.6
  69.8 0.2 slice_bitcast_fusion.1
  70.0 5.9 %collective-permute-start.12 = (f16[2,192,128]{2,1,0:T(8,128)(2,1)S(1)}, f16[2,192,128]{2,1,0:T(8,128)(2,1)S(1)}, u32[]{:S(2)}, u32[]{:S(2)}) collective-permute-start(f16[2,192,128]{2,1,0:T(8,128)(2,1)S(1)} %get-tuple-element.91), channel_id=1, source_target_pairs={{0,16},{4,20},{8,24},{12,28},{16,0},{20,4},{24,8},{28,12},{1,17},{... | collective-permute-start | bytes 294920 | tf_op jit(solution)/shard_map/ppermute | solution.py:41
  75.9 0.3 collective-permute-start.13
  76.2 1.5 %convert_reduce_fusion = f32[4,2,64,128]{3,2,1,0:T(8,128)S(1)} fusion(f16[8,4,2,64,128]{4,3,2,1,0:T(8,128)(2,1)} %all-to-all-done), kind=kLoop, calls=%fused_computation | loop fusion | flops 983040 | bytes 1310720 | tf_op jit(solution)/shard_map/reduce_sum | solution.py:269
  77.7 1.3 %collective-permute-start.10 = (f16[2,64,128]{2,1,0:T(8,128)(2,1)S(1)}, f16[2,64,128]{2,1,0:T(8,128)(2,1)S(1)}, u32[]{:S(2)}, u32[]{:S(2)}) collective-permute-start(f16[2,64,128]{2,1,0:T(8,128)(2,1)S(1)} %get-tuple-element.95), channel_id=1, source_target_pairs={{0,32},{32,64},{64,96},{96,0},{1,33},{33,65},{65,97},{97,1},{2,34}... | collective-permute-start | bytes 98312 | tf_op jit(solution)/shard_map/ppermute | solution.py:41
  79.1 1.4 %collective-permute-start.11 = (f16[2,64,128]{2,1,0:T(8,128)(2,1)S(1)}, f16[2,64,128]{2,1,0:T(8,128)(2,1)S(1)}, u32[]{:S(2)}, u32[]{:S(2)}) collective-permute-start(f16[2,64,128]{2,1,0:T(8,128)(2,1)S(1)} %get-tuple-element.94), channel_id=1, source_target_pairs={{0,96},{32,0},{64,32},{96,64},{1,97},{33,1},{65,33},{97,65},{2,98}... | collective-permute-start | bytes 98312 | tf_op jit(solution)/shard_map/ppermute | solution.py:41
  80.5 1.5 %collective-permute-start.9 = (f16[2,64,128]{2,1,0:T(8,128)(2,1)S(1)}, f16[2,64,128]{2,1,0:T(8,128)(2,1)S(1)}, u32[]{:S(2)}, u32[]{:S(2)}) collective-permute-start(f16[2,64,128]{2,1,0:T(8,128)(2,1)S(1)} %get-tuple-element.96), channel_id=1, source_target_pairs={{0,64},{32,96},{64,0},{96,32},{1,65},{33,97},{65,1},{97,33},{2,66}... | collective-permute-start | bytes 98312 | tf_op jit(solution)/shard_map/ppermute | solution.py:41
  82.0 4.2 %collective-permute-start.14 = (f16[2,192,128]{2,1,0:T(8,128)(2,1)S(1)}, f16[2,192,128]{2,1,0:T(8,128)(2,1)S(1)}, u32[]{:S(2)}, u32[]{:S(2)}) collective-permute-start(f16[2,192,128]{2,1,0:T(8,128)(2,1)S(1)} %get-tuple-element.89), channel_id=1, source_target_pairs={{0,20},{4,24},{8,28},{12,0},{16,4},{20,8},{24,12},{28,16},{1,21},{... | collective-permute-start | bytes 294920 | tf_op jit(solution)/shard_map/ppermute | solution.py:41
  86.2 0.3 collective-permute-start.15
  86.5 3.3 %collective-permute-start.16 = (f16[2,192,128]{2,1,0:T(8,128)(2,1)S(1)}, f16[2,192,128]{2,1,0:T(8,128)(2,1)S(1)}, u32[]{:S(2)}, u32[]{:S(2)}) collective-permute-start(f16[2,192,128]{2,1,0:T(8,128)(2,1)S(1)} %get-tuple-element.87), channel_id=1, source_target_pairs={{0,24},{4,28},{8,0},{12,4},{16,8},{20,12},{24,16},{28,20},{1,25},{... | collective-permute-start | bytes 294920 | tf_op jit(solution)/shard_map/ppermute | solution.py:41
  89.8 0.3 collective-permute-start.17
  90.1 2.3 %collective-permute-start.18 = (f16[2,192,128]{2,1,0:T(8,128)(2,1)S(1)}, f16[2,192,128]{2,1,0:T(8,128)(2,1)S(1)}, u32[]{:S(2)}, u32[]{:S(2)}) collective-permute-start(f16[2,192,128]{2,1,0:T(8,128)(2,1)S(1)} %get-tuple-element.85), channel_id=1, source_target_pairs={{0,28},{4,0},{8,4},{12,8},{16,12},{20,16},{24,20},{28,24},{1,29},{... | collective-permute-start | bytes 294920 | tf_op jit(solution)/shard_map/ppermute | solution.py:41
  92.5 0.6 collective-permute-done.15
  93.1 3.0 %collective-permute-done.16 = f16[2,192,128]{2,1,0:T(8,128)(2,1)S(1)} collective-permute-done((f16[2,192,128]{2,1,0:T(8,128)(2,1)S(1)}, f16[2,192,128]{2,1,0:T(8,128)(2,1)S(1)}, u32[]{:S(2)}, u32[]{:S(2)}) %collective-permute-start.16) | collective-permute-done | bytes 98336 | tf_op jit(solution)/shard_map/ppermute | solution.py:41
  96.1 0.1 collective-permute-done.17
  96.2 2.8 %collective-permute-done.18 = f16[2,192,128]{2,1,0:T(8,128)(2,1)S(1)} collective-permute-done((f16[2,192,128]{2,1,0:T(8,128)(2,1)S(1)}, f16[2,192,128]{2,1,0:T(8,128)(2,1)S(1)}, u32[]{:S(2)}, u32[]{:S(2)}) %collective-permute-start.18) | collective-permute-done | bytes 98336 | tf_op jit(solution)/shard_map/ppermute | solution.py:41
  99.0 0.6 fusion.11.second
  99.6 0.8 fusion.7.first
  100.4 1.9 %turn.1 = f32[8,64,256]{2,1,0:T(8,128)} custom-call(f32[2,192,128]{2,1,0:T(8,128)} %fusion.7.first, f32[2,64,128]{2,1,0:T(8,128)} %fusion.11.second), custom_call_target="tpu_custom_call" | custom-call | tf_op jit(solution)/shard_map/turn/pallas_call | solution.py:281
  102.3 14.9 %all_to_all.10.got = f32[8,64,256]{2,1,0:T(8,128)} all-to-all(f32[8,64,256]{2,1,0:T(8,128)} %turn.1), channel_id=1, replica_groups=mesh['group'=2,'x'=4,'z'=8,'y'=2,'c'=2] {'group','y','c'}, dimensions={0} | all-to-all | bytes 1048576 | tf_op jit(solution)/shard_map/all_to_all | solution.py:286
  117.2 2.4 %final.1 = (f32[32,512]{1,0:T(8,128)}, f32[32,512]{1,0:T(8,128)}, bf16[64,512]{1,0:T(8,128)(2,1)}) custom-call(s32[1]{0:T(128)} %bitcast.group, f32[6]{0:T(128)} %reshape.19.facts, f32[8,64,256]{2,1,0:T(8,128)} %all_to_all.10.got, f32[64,512]{1,0:T(8,128)} %bitcast.65, f32[64,512]{1,0:T(8,128)} %bitcast.67, f32[64,512]{1,0:T(8,128)} %bitcast.69, ...), custom_call_target="tpu_custom_call" | custom-call | tf_op jit(solution)/shard_map/final/pallas_call | solution.py:290
  (21 shorter events, 0.1 us)
Async XLA Ops:
  10.4 10.5 %collective-permute-start.2 = (f32[8,4,2,64,128]{4,3,2,1,0:T(8,128)S(1)}, f32[8,4,2,64,128]{4,3,2,1,0:T(8,128)S(1)}, u32[]{:S(2)}, u32[]{:S(2)}) collective-permute-start(f32[8,4,2,64,128]{4,3,2,1,0:T(8,128)S(1)} %get-tuple-element.46), channel_id=1, source_target_pairs={{0,1},{1,0},{2,3},{3,2},{4,5},{5,4},{6,7},{7,6},{8,9},{9,8},{10,11... | collective-permute-start | bytes 6291464 | tf_op jit(solution)/shard_map/ppermute | solution.py:37
  13.7 6.0 %collective-permute-start = (f32[8,2,192,128]{3,2,1,0:T(8,128)S(1)}, f32[8,2,192,128]{3,2,1,0:T(8,128)S(1)}, u32[]{:S(2)}, u32[]{:S(2)}) collective-permute-start(f32[8,2,192,128]{3,2,1,0:T(8,128)S(1)} %get-tuple-element.44), channel_id=1, source_target_pairs={{0,1},{1,0},{2,3},{3,2},{4,5},{5,4},{6,7},{7,6},{8,9},{9,8},{10,11... | collective-permute-start | bytes 4718600 | tf_op jit(solution)/shard_map/ppermute | solution.py:37
  13.8 18.4 %collective-permute-start.3 = (f32[8,2,192,128]{3,2,1,0:T(8,128)}, f32[8,2,192,128]{3,2,1,0:T(8,128)}, u32[]{:S(2)}, u32[]{:S(2)}) collective-permute-start(f32[8,2,192,128]{3,2,1,0:T(8,128)} %get-tuple-element.50), channel_id=1, source_target_pairs={{0,1},{1,0},{2,3},{3,2},{4,5},{5,4},{6,7},{7,6},{8,9},{9,8},{10,11... | collective-permute-start | bytes 4718600 | tf_op jit(solution)/shard_map/ppermute | solution.py:37
  14.2 20.5 %collective-permute-start.5 = (f32[8,2,192,128]{3,2,1,0:T(8,128)}, f32[8,2,192,128]{3,2,1,0:T(8,128)}, u32[]{:S(2)}, u32[]{:S(2)}) collective-permute-start(f32[8,2,192,128]{3,2,1,0:T(8,128)} %get-tuple-element.54), channel_id=1, source_target_pairs={{0,1},{1,0},{2,3},{3,2},{4,5},{5,4},{6,7},{7,6},{8,9},{9,8},{10,11... | collective-permute-start | bytes 4718600 | tf_op jit(solution)/shard_map/ppermute | solution.py:37
  22.4 45.2 %all-to-all-start = ((f16[8,4,2,64,128]{4,3,2,1,0:T(8,128)(2,1)}), f16[8,4,2,64,128]{4,3,2,1,0:T(8,128)(2,1)}, u32[]{:S(2)}, u32[]{:S(2)}) async-start(f16[8,4,2,64,128]{4,3,2,1,0:T(8,128)(2,1)} %add_convert_fusion), calls=%async_computation | async-start | bytes 2097152 | tf_op jit(solution)/shard_map/all_to_all | solution.py:241
  28.9 38.7 %collective-permute-start.8 = (f32[8,2,192,128]{3,2,1,0:T(8,128)}, f32[8,2,192,128]{3,2,1,0:T(8,128)}, u32[]{:S(2)}, u32[]{:S(2)}) collective-permute-start(f32[8,2,192,128]{3,2,1,0:T(8,128)} %get-tuple-element.64), channel_id=1, source_target_pairs={{0,1},{1,0},{2,3},{3,2},{4,5},{5,4},{6,7},{7,6},{8,9},{9,8},{10,11... | collective-permute-start | bytes 4718600 | tf_op jit(solution)/shard_map/ppermute | solution.py:37
  29.5 20.9 %collective-permute-start.1 = (f16[8,2,192,128]{3,2,1,0:T(8,128)(2,1)}, f16[8,2,192,128]{3,2,1,0:T(8,128)(2,1)}, u32[]{:S(2)}, u32[]{:S(2)}) collective-permute-start(f16[8,2,192,128]{3,2,1,0:T(8,128)(2,1)} %add_convert_fusion.3), channel_id=1, source_target_pairs={{0,64},{32,96},{64,0},{96,32},{1,65},{33,97},{65,1},{97,33},{2,66}... | collective-permute-start | bytes 2359304 | tf_op jit(solution)/shard_map/ppermute | solution.py:41
  34.8 4.1 %copy-start.2 = (s32[2]{0:T(128)S(1)}, s32[2]{0:T(128)}, u32[]{:S(2)}) copy-start(s32[2]{0:T(128)} %param.15) | copy-start | bytes 28
  34.8 9.5 %copy-start.1 = (s32[2]{0:T(128)S(1)}, s32[2]{0:T(128)}, u32[]{:S(2)}) copy-start(s32[2]{0:T(128)} %param.14) | copy-start | bytes 28
  34.8 32.8 %copy-start = (f32[8,2,192,128]{3,2,1,0:T(8,128)S(1)}, f32[8,2,192,128]{3,2,1,0:T(8,128)}, u32[]{:S(2)}) copy-start(f32[8,2,192,128]{3,2,1,0:T(8,128)} %get-tuple-element.63) | copy-start | bytes 4718596
  37.4 29.9 %collective-permute-start.6 = (f16[8,2,192,128]{3,2,1,0:T(8,128)(2,1)}, f16[8,2,192,128]{3,2,1,0:T(8,128)(2,1)S(1)}, u32[]{:S(2)}, u32[]{:S(2)}) collective-permute-start(f16[8,2,192,128]{3,2,1,0:T(8,128)(2,1)} %add_convert_fusion.1), channel_id=1, source_target_pairs={{0,96},{32,0},{64,32},{96,64},{1,97},{33,1},{65,33},{97,65},{2,98}... | collective-permute-start | bytes 2359304 | tf_op jit(solution)/shard_map/ppermute | solution.py:41
  38.2 29.3 %collective-permute-start.4 = (f16[8,2,192,128]{3,2,1,0:T(8,128)(2,1)}, f16[8,2,192,128]{3,2,1,0:T(8,128)(2,1)S(1)}, u32[]{:S(2)}, u32[]{:S(2)}) collective-permute-start(f16[8,2,192,128]{3,2,1,0:T(8,128)(2,1)} %add_convert_fusion.2), channel_id=1, source_target_pairs={{0,32},{32,64},{64,96},{96,0},{1,33},{33,65},{65,97},{97,1},{2,34}... | collective-permute-start | bytes 2359304 | tf_op jit(solution)/shard_map/ppermute | solution.py:41
  41.3 14.4 %collective-permute-start.7 = (f32[256,512]{1,0:T(8,128)}, f32[256,512]{1,0:T(8,128)}, u32[]{:S(2)}, u32[]{:S(2)}) collective-permute-start(f32[256,512]{1,0:T(8,128)} %pack.1), channel_id=1, source_target_pairs={{0,128},{128,0},{1,129},{129,1},{2,130},{130,2},{3,131},{131,3},{4... | collective-permute-start | bytes 1572872 | tf_op jit(solution)/shard_map/ppermute | solution.py:37
  70.0 19.8 %collective-permute-start.12 = (f16[2,192,128]{2,1,0:T(8,128)(2,1)S(1)}, f16[2,192,128]{2,1,0:T(8,128)(2,1)S(1)}, u32[]{:S(2)}, u32[]{:S(2)}) collective-permute-start(f16[2,192,128]{2,1,0:T(8,128)(2,1)S(1)} %get-tuple-element.91), channel_id=1, source_target_pairs={{0,16},{4,20},{8,24},{12,28},{16,0},{20,4},{24,8},{28,12},{1,17},{... | collective-permute-start | bytes 294920 | tf_op jit(solution)/shard_map/ppermute | solution.py:41
  75.9 14.2 %collective-permute-start.13 = (f16[2,192,128]{2,1,0:T(8,128)(2,1)S(1)}, f16[2,192,128]{2,1,0:T(8,128)(2,1)S(1)}, u32[]{:S(2)}, u32[]{:S(2)}) collective-permute-start(f16[2,192,128]{2,1,0:T(8,128)(2,1)S(1)} %get-tuple-element.90), channel_id=1, source_target_pairs={{0,12},{4,16},{8,20},{12,24},{16,28},{20,0},{24,4},{28,8},{1,13},{... | collective-permute-start | bytes 294920 | tf_op jit(solution)/shard_map/ppermute | solution.py:41
  77.7 4.3 %collective-permute-start.10 = (f16[2,64,128]{2,1,0:T(8,128)(2,1)S(1)}, f16[2,64,128]{2,1,0:T(8,128)(2,1)S(1)}, u32[]{:S(2)}, u32[]{:S(2)}) collective-permute-start(f16[2,64,128]{2,1,0:T(8,128)(2,1)S(1)} %get-tuple-element.95), channel_id=1, source_target_pairs={{0,32},{32,64},{64,96},{96,0},{1,33},{33,65},{65,97},{97,1},{2,34}... | collective-permute-start | bytes 98312 | tf_op jit(solution)/shard_map/ppermute | solution.py:41
  79.1 7.2 %collective-permute-start.11 = (f16[2,64,128]{2,1,0:T(8,128)(2,1)S(1)}, f16[2,64,128]{2,1,0:T(8,128)(2,1)S(1)}, u32[]{:S(2)}, u32[]{:S(2)}) collective-permute-start(f16[2,64,128]{2,1,0:T(8,128)(2,1)S(1)} %get-tuple-element.94), channel_id=1, source_target_pairs={{0,96},{32,0},{64,32},{96,64},{1,97},{33,1},{65,33},{97,65},{2,98}... | collective-permute-start | bytes 98312 | tf_op jit(solution)/shard_map/ppermute | solution.py:41
  80.5 6.0 %collective-permute-start.9 = (f16[2,64,128]{2,1,0:T(8,128)(2,1)S(1)}, f16[2,64,128]{2,1,0:T(8,128)(2,1)S(1)}, u32[]{:S(2)}, u32[]{:S(2)}) collective-permute-start(f16[2,64,128]{2,1,0:T(8,128)(2,1)S(1)} %get-tuple-element.96), channel_id=1, source_target_pairs={{0,64},{32,96},{64,0},{96,32},{1,65},{33,97},{65,1},{97,33},{2,66}... | collective-permute-start | bytes 98312 | tf_op jit(solution)/shard_map/ppermute | solution.py:41
  82.0 10.5 %collective-permute-start.14 = (f16[2,192,128]{2,1,0:T(8,128)(2,1)S(1)}, f16[2,192,128]{2,1,0:T(8,128)(2,1)S(1)}, u32[]{:S(2)}, u32[]{:S(2)}) collective-permute-start(f16[2,192,128]{2,1,0:T(8,128)(2,1)S(1)} %get-tuple-element.89), channel_id=1, source_target_pairs={{0,20},{4,24},{8,28},{12,0},{16,4},{20,8},{24,12},{28,16},{1,21},{... | collective-permute-start | bytes 294920 | tf_op jit(solution)/shard_map/ppermute | solution.py:41
  86.2 6.9 %collective-permute-start.15 = (f16[2,192,128]{2,1,0:T(8,128)(2,1)S(1)}, f16[2,192,128]{2,1,0:T(8,128)(2,1)S(1)}, u32[]{:S(2)}, u32[]{:S(2)}) collective-permute-start(f16[2,192,128]{2,1,0:T(8,128)(2,1)S(1)} %get-tuple-element.88), channel_id=1, source_target_pairs={{0,8},{4,12},{8,16},{12,20},{16,24},{20,28},{24,0},{28,4},{1,9},{5... | collective-permute-start | bytes 294920 | tf_op jit(solution)/shard_map/ppermute | solution.py:41
  86.5 9.6 %collective-permute-start.16 = (f16[2,192,128]{2,1,0:T(8,128)(2,1)S(1)}, f16[2,192,128]{2,1,0:T(8,128)(2,1)S(1)}, u32[]{:S(2)}, u32[]{:S(2)}) collective-permute-start(f16[2,192,128]{2,1,0:T(8,128)(2,1)S(1)} %get-tuple-element.87), channel_id=1, source_target_pairs={{0,24},{4,28},{8,0},{12,4},{16,8},{20,12},{24,16},{28,20},{1,25},{... | collective-permute-start | bytes 294920 | tf_op jit(solution)/shard_map/ppermute | solution.py:41
  89.8 6.4 %collective-permute-start.17 = (f16[2,192,128]{2,1,0:T(8,128)(2,1)S(1)}, f16[2,192,128]{2,1,0:T(8,128)(2,1)S(1)}, u32[]{:S(2)}, u32[]{:S(2)}) collective-permute-start(f16[2,192,128]{2,1,0:T(8,128)(2,1)S(1)} %get-tuple-element.86), channel_id=1, source_target_pairs={{0,4},{4,8},{8,12},{12,16},{16,20},{20,24},{24,28},{28,0},{1,5},{5... | collective-permute-start | bytes 294920 | tf_op jit(solution)/shard_map/ppermute | solution.py:41
  90.1 8.8 %collective-permute-start.18 = (f16[2,192,128]{2,1,0:T(8,128)(2,1)S(1)}, f16[2,192,128]{2,1,0:T(8,128)(2,1)S(1)}, u32[]{:S(2)}, u32[]{:S(2)}) collective-permute-start(f16[2,192,128]{2,1,0:T(8,128)(2,1)S(1)} %get-tuple-element.85), channel_id=1, source_target_pairs={{0,28},{4,0},{8,4},{12,8},{16,12},{20,16},{24,20},{28,24},{1,29},{... | collective-permute-start | bytes 294920 | tf_op jit(solution)/shard_map/ppermute | solution.py:41

commit v6 on v5

--- a/solution.py
+++ b/solution.py
@@ -31,6 +31,10 @@
 LIMIT = 28
 ORDER = (2, 1, 3, 0)
 FAR = (4, 3, 5, 2, 6, 1, 7)
+
+
+def on_chip(*arrays):
+    return [pltpu.with_memory_space_constraint(a, pltpu.VMEM) for a in arrays]
 
 
 def swap(a, axis):
@@ -280,9 +284,11 @@
 
     part = pl.pallas_call(
         turn_kernel,
-        out_shape=jax.ShapeDtypeStruct((NG * NY * NC, rows, half), F32),
+        in_specs=[pl.BlockSpec(memory_space=pltpu.VMEM)] * 2,
+        out_specs=pl.BlockSpec(memory_space=pltpu.VMEM),
+        out_shape=pltpu.VMEM((NG * NY * NC, rows, half), F32),
         name="turn",
-    )(first, second)
+    )(*on_chip(first, second))
     got = lax.all_to_all(part, ("group", "y", "c"), 0, 0, tiled=True)
 
     vmem = pl.BlockSpec(memory_space=pltpu.VMEM)
@@ -297,7 +303,7 @@
             jax.ShapeDtypeStruct((rows, anchor.shape[1]), jnp.bfloat16),
         ],
         name="final",
-    )(group[None], facts, got, *near, far)
+    )(group[None], facts, *on_chip(got, *near, far))
     return new_anchor, new_momentum, weights[None]
 
 

time: 120 us -> 116 us (0.967)
  Pallas kernels: 15.9 us -> 13.5 us
    pallas_call x1, Pallas kernels: 1.87 us -> 0.13 us  [per_device(): pl.pallas_call(turn_kernel, in_specs=[pl.BlockSpec(memory_space=pltpu.VME...]
  transfers between devices with their start and end apart: 20 -> 20, of which waited for: 9 -> 9; matrix products, arithmetic and copies ran while one was open for 9% -> 10% of each run, Pallas kernels for 2% -> 2%
where the time goes in v6:
time: 116 us
  starting transfers between devices  39.1 us (34%)
  waiting for transfers between devices  33.8 us (29%)
  blocking collectives  14.6 us (13%)
  Pallas kernels  13.5 us (12%)
  other arithmetic  13.1 us (11%)
    ppermute x13, starting transfers between devices, around(): return lax.ppermute(a, axis, [(i, (i + k) % size) for i in range(size)])  25.1 us
    ppermute x13, waiting for transfers between devices, around(): return lax.ppermute(a, axis, [(i, (i + k) % size) for i in range(size)])  23.1 us
    all_to_all x1, blocking collectives, per_device(): got = lax.all_to_all(part, ('group', 'y', 'c'), 0, 0, tiled=True)  14.6 us
    ppermute x6, waiting for transfers between devices, swap(): return lax.ppermute(a, axis, [(0, 1), (1, 0)])  10.8 us
    pallas_call x1, Pallas kernels, terms(): pl.pallas_call(functools.partial(terms_kernel, PEAK / (tokens * NC)), in_...  9.83 us
    ppermute x6, starting transfers between devices, swap(): return lax.ppermute(a, axis, [(0, 1), (1, 0)])  7.46 us
    all_to_all x1, starting transfers between devices, per_device(): back_b = lax.all_to_all(wire, 'z', 0, 0, tiled=True)  6.48 us
    convert_element_type x2, other arithmetic, per_device(): wire = (own + got).astype(WIRE)  5.09 us
  transfers between devices with their start and end apart: 20, of which 9 were waited for; matrix products, arithmetic and copies ran while one was open for 10% of the time, Pallas kernels for 2%

profile of v6, /device:TPU:1, one launch (start us, length us, event | category | flops | bytes accessed | tf_op | source)
XLA Modules:
  0.0 116.0 jit_solution(7822544567178962643)
XLA Ops:
  0.6 9.8 %terms.1 = (f32[8,2,192,128]{3,2,1,0:T(8,128)S(1)}, f32[8,2,192,128]{3,2,1,0:T(8,128)}, f32[8,2,192,128]{3,2,1,0:T(8,128)}, f32[8,2,192,128]{3,2,1,0:T(8,128)}, ...) custom-call(s32[1]{0:T(128)} %bitcast.1.core, ...), custom_call_target="tpu_custom_call" | custom-call | flops 4294967296 | bytes 25165824 | tf_op jit(solution)/shard_map/terms/pallas_call | solution.py:108
  10.5 3.3 %collective-permute-start.2 = (f32[8,4,2,64,128]{4,3,2,1,0:T(8,128)S(1)}, f32[8,4,2,64,128]{4,3,2,1,0:T(8,128)S(1)}, u32[]{:S(2)}, u32[]{:S(2)}) collective-permute-start(f32[8,4,2,64,128]{4,3,2,1,0:T(8,128)S(1)} %get-tuple-element.46), channel_id=1, source_target_pairs={{0,1},{1,0},{2,3},{3,2},{4,5},{5,4},{6,7},{7,6},{8,9},{9,8},{10,11... | collective-permute-start | bytes 6291464 | tf_op jit(solution)/shard_map/ppermute | solution.py:41
  13.8 0.1 collective-permute-start
  13.9 0.4 collective-permute-start.3
  14.3 0.1 collective-permute-start.5
  14.4 5.4 %collective-permute-done = f32[8,2,192,128]{3,2,1,0:T(8,128)S(1)} collective-permute-done((f32[8,2,192,128]{3,2,1,0:T(8,128)S(1)}, f32[8,2,192,128]{3,2,1,0:T(8,128)S(1)}, u32[]{:S(2)}, u32[]{:S(2)}) %collective-permute-start) | collective-permute-done | bytes 1572896 | tf_op jit(solution)/shard_map/ppermute | solution.py:41
  19.8 1.1 add_convert_fusion.3
  20.9 1.5 %add_convert_fusion = f16[8,4,2,64,128]{4,3,2,1,0:T(8,128)(2,1)} fusion(f32[8,4,2,64,128]{4,3,2,1,0:T(8,128)S(1)} %get-tuple-element.47, f32[8,4,2,64,128]{4,3,2,1,0:T(8,128)S(1)} %collective-permute-done.2), kind=kLoop, calls=%fused_computation.1 | loop fusion | flops 1048576 | bytes 5242880 | tf_op jit(solution)/shard_map/convert_element_type | solution.py:244
  22.4 6.5 %all-to-all-start = ((f16[8,4,2,64,128]{4,3,2,1,0:T(8,128)(2,1)}), f16[8,4,2,64,128]{4,3,2,1,0:T(8,128)(2,1)}, u32[]{:S(2)}, u32[]{:S(2)}) async-start(f16[8,4,2,64,128]{4,3,2,1,0:T(8,128)(2,1)} %add_convert_fusion), calls=%async_computation | async-start | bytes 2097152 | tf_op jit(solution)/shard_map/all_to_all | solution.py:245
  28.9 0.7 collective-permute-start.8
  29.6 2.7 %collective-permute-start.1 = (f16[8,2,192,128]{3,2,1,0:T(8,128)(2,1)}, f16[8,2,192,128]{3,2,1,0:T(8,128)(2,1)}, u32[]{:S(2)}, u32[]{:S(2)}) collective-permute-start(f16[8,2,192,128]{3,2,1,0:T(8,128)(2,1)} %add_convert_fusion.3), channel_id=1, source_target_pairs={{0,64},{32,96},{64,0},{96,32},{1,65},{33,97},{65,1},{97,33},{2,66}... | collective-permute-start | bytes 2359304 | tf_op jit(solution)/shard_map/ppermute | solution.py:45
  32.3 2.5 %add_convert_fusion.2 = f16[8,2,192,128]{3,2,1,0:T(8,128)(2,1)} fusion(f32[8,2,192,128]{3,2,1,0:T(8,128)S(1)} %get-tuple-element.51, f32[8,2,192,128]{3,2,1,0:T(8,128)} %collective-permute-done.3), kind=kLoop, calls=%fused_computation.4 | loop fusion | flops 786432 | bytes 3932160 | tf_op jit(solution)/shard_map/convert_element_type | solution.py:249
  34.8 2.6 %add_convert_fusion.1 = f16[8,2,192,128]{3,2,1,0:T(8,128)(2,1)} fusion(f32[8,2,192,128]{3,2,1,0:T(8,128)S(1)} %get-tuple-element.55, f32[8,2,192,128]{3,2,1,0:T(8,128)} %collective-permute-done.5), kind=kLoop, calls=%fused_computation.3 | loop fusion | flops 786432 | bytes 3932160 | tf_op jit(solution)/shard_map/convert_element_type | solution.py:249
  37.4 0.9 collective-permute-start.6
  38.3 0.6 collective-permute-start.4
  38.9 0.6 convert_reduce_fusion.1
  39.5 1.9 %pack.1 = f32[256,512]{1,0:T(8,128)} custom-call(f32[64,512]{1,0:T(8,128)} %bitcast.64, f32[64,512]{1,0:T(8,128)} %bitcast.66, f32[64,512]{1,0:T(8,128)} %bitcast.68, f32[32,512]{1,0:T(8,128)} %a0.1, f32[32,512]{1,0:T(8,128)} %w0.1), custom_call_target="tpu_custom_call" | custom-call | tf_op jit(solution)/shard_map/pack/pallas_call | solution.py:252
  41.4 2.9 %collective-permute-start.7 = (f32[256,512]{1,0:T(8,128)}, f32[256,512]{1,0:T(8,128)S(1)}, u32[]{:S(2)}, u32[]{:S(2)}) collective-permute-start(f32[256,512]{1,0:T(8,128)} %pack.1), channel_id=1, source_target_pairs={{0,128},{128,0},{1,129},{129,1},{2,130},{130,2},{3,131},{131,3},{4... | collective-permute-start | bytes 1572872 | tf_op jit(solution)/shard_map/ppermute | solution.py:41
  44.3 0.7 subtract_bitcast_fusion.1
  45.0 0.1 rev.3
  45.1 0.1 copy.12
  45.2 0.7 reshape.19.facts
  45.8 4.6 %collective-permute-done.1 = f16[8,2,192,128]{3,2,1,0:T(8,128)(2,1)} collective-permute-done((f16[8,2,192,128]{3,2,1,0:T(8,128)(2,1)}, f16[8,2,192,128]{3,2,1,0:T(8,128)(2,1)}, u32[]{:S(2)}, u32[]{:S(2)}) %collective-permute-start.1) | collective-permute-done | bytes 786464 | tf_op jit(solution)/shard_map/ppermute | solution.py:45
  50.4 5.3 %collective-permute-done.7.far = f32[256,512]{1,0:T(8,128)S(1)} collective-permute-done((f32[256,512]{1,0:T(8,128)}, f32[256,512]{1,0:T(8,128)S(1)}, u32[]{:S(2)}, u32[]{:S(2)}) %collective-permute-start.7) | collective-permute-done | bytes 524320 | tf_op jit(solution)/shard_map/ppermute | solution.py:41
  55.8 11.6 %collective-permute-done.6 = f16[8,2,192,128]{3,2,1,0:T(8,128)(2,1)S(1)} collective-permute-done((f16[8,2,192,128]{3,2,1,0:T(8,128)(2,1)}, f16[8,2,192,128]{3,2,1,0:T(8,128)(2,1)S(1)}, u32[]{:S(2)}, u32[]{:S(2)}) %collective-permute-start.6) | collective-permute-done | bytes 786464 | tf_op jit(solution)/shard_map/ppermute | solution.py:45
  67.4 0.3 collective-permute-done.4
  67.7 2.5 %fusion.13 = (f16[8,2,192,128]{3,2,1,0:T(8,128)(2,1)S(1)}, f32[8,2,192,128]{3,2,1,0:T(8,128)S(1)}) fusion(f16[8,2,192,128]{3,2,1,0:T(8,128)(2,1)S(1)} %collective-permute-done.6, f16[8,2,192,128]{3,2,1,0:T(8,128)(2,1)} %collective-permute-done.4, f16[8,2,192,128]{3,2,1,0:T(8,128)(2,1)} %collective-permute-done.1, f32[8,2,192,128]{3,2,1,0:T(8,128)S(1)} %copy-done.5, ...), kind=kLoop, calls=%fused_computation.38 | loop fusion | flops 3538944 | bytes 7864320 | tf_op jit(solution)/shard_map/convert.6
  70.2 0.2 slice_bitcast_fusion.1
  70.4 5.9 %collective-permute-start.12 = (f16[2,192,128]{2,1,0:T(8,128)(2,1)S(1)}, f16[2,192,128]{2,1,0:T(8,128)(2,1)S(1)}, u32[]{:S(2)}, u32[]{:S(2)}) collective-permute-start(f16[2,192,128]{2,1,0:T(8,128)(2,1)S(1)} %get-tuple-element.91), channel_id=1, source_target_pairs={{0,16},{4,20},{8,24},{12,28},{16,0},{20,4},{24,8},{28,12},{1,17},{... | collective-permute-start | bytes 294920 | tf_op jit(solution)/shard_map/ppermute | solution.py:45
  76.3 0.3 collective-permute-start.13
  76.6 1.5 %convert_reduce_fusion = f32[4,2,64,128]{3,2,1,0:T(8,128)S(1)} fusion(f16[8,4,2,64,128]{4,3,2,1,0:T(8,128)(2,1)} %all-to-all-done), kind=kLoop, calls=%fused_computation | loop fusion | flops 983040 | bytes 1310720 | tf_op jit(solution)/shard_map/reduce_sum | solution.py:273
  78.1 1.3 %collective-permute-start.10 = (f16[2,64,128]{2,1,0:T(8,128)(2,1)S(1)}, f16[2,64,128]{2,1,0:T(8,128)(2,1)S(1)}, u32[]{:S(2)}, u32[]{:S(2)}) collective-permute-start(f16[2,64,128]{2,1,0:T(8,128)(2,1)S(1)} %get-tuple-element.95), channel_id=1, source_target_pairs={{0,32},{32,64},{64,96},{96,0},{1,33},{33,65},{65,97},{97,1},{2,34}... | collective-permute-start | bytes 98312 | tf_op jit(solution)/shard_map/ppermute | solution.py:45
  79.5 1.4 %collective-permute-start.11 = (f16[2,64,128]{2,1,0:T(8,128)(2,1)S(1)}, f16[2,64,128]{2,1,0:T(8,128)(2,1)S(1)}, u32[]{:S(2)}, u32[]{:S(2)}) collective-permute-start(f16[2,64,128]{2,1,0:T(8,128)(2,1)S(1)} %get-tuple-element.94), channel_id=1, source_target_pairs={{0,96},{32,0},{64,32},{96,64},{1,97},{33,1},{65,33},{97,65},{2,98}... | collective-permute-start | bytes 98312 | tf_op jit(solution)/shard_map/ppermute | solution.py:45
  80.9 1.5 %collective-permute-start.9 = (f16[2,64,128]{2,1,0:T(8,128)(2,1)S(1)}, f16[2,64,128]{2,1,0:T(8,128)(2,1)S(1)}, u32[]{:S(2)}, u32[]{:S(2)}) collective-permute-start(f16[2,64,128]{2,1,0:T(8,128)(2,1)S(1)} %get-tuple-element.96), channel_id=1, source_target_pairs={{0,64},{32,96},{64,0},{96,32},{1,65},{33,97},{65,1},{97,33},{2,66}... | collective-permute-start | bytes 98312 | tf_op jit(solution)/shard_map/ppermute | solution.py:45
  82.4 4.2 %collective-permute-start.14 = (f16[2,192,128]{2,1,0:T(8,128)(2,1)S(1)}, f16[2,192,128]{2,1,0:T(8,128)(2,1)S(1)}, u32[]{:S(2)}, u32[]{:S(2)}) collective-permute-start(f16[2,192,128]{2,1,0:T(8,128)(2,1)S(1)} %get-tuple-element.89), channel_id=1, source_target_pairs={{0,20},{4,24},{8,28},{12,0},{16,4},{20,8},{24,12},{28,16},{1,21},{... | collective-permute-start | bytes 294920 | tf_op jit(solution)/shard_map/ppermute | solution.py:45
  86.6 0.3 collective-permute-start.15
  86.9 3.3 %collective-permute-start.16 = (f16[2,192,128]{2,1,0:T(8,128)(2,1)S(1)}, f16[2,192,128]{2,1,0:T(8,128)(2,1)S(1)}, u32[]{:S(2)}, u32[]{:S(2)}) collective-permute-start(f16[2,192,128]{2,1,0:T(8,128)(2,1)S(1)} %get-tuple-element.87), channel_id=1, source_target_pairs={{0,24},{4,28},{8,0},{12,4},{16,8},{20,12},{24,16},{28,20},{1,25},{... | collective-permute-start | bytes 294920 | tf_op jit(solution)/shard_map/ppermute | solution.py:45
  90.2 0.3 collective-permute-start.17
  90.5 2.3 %collective-permute-start.18 = (f16[2,192,128]{2,1,0:T(8,128)(2,1)S(1)}, f16[2,192,128]{2,1,0:T(8,128)(2,1)S(1)}, u32[]{:S(2)}, u32[]{:S(2)}) collective-permute-start(f16[2,192,128]{2,1,0:T(8,128)(2,1)S(1)} %get-tuple-element.85), channel_id=1, source_target_pairs={{0,28},{4,0},{8,4},{12,8},{16,12},{20,16},{24,20},{28,24},{1,29},{... | collective-permute-start | bytes 294920 | tf_op jit(solution)/shard_map/ppermute | solution.py:45
  92.9 0.6 collective-permute-done.15
  93.5 3.0 %collective-permute-done.16 = f16[2,192,128]{2,1,0:T(8,128)(2,1)S(1)} collective-permute-done((f16[2,192,128]{2,1,0:T(8,128)(2,1)S(1)}, f16[2,192,128]{2,1,0:T(8,128)(2,1)S(1)}, u32[]{:S(2)}, u32[]{:S(2)}) %collective-permute-start.16) | collective-permute-done | bytes 98336 | tf_op jit(solution)/shard_map/ppermute | solution.py:45
  96.5 0.1 collective-permute-done.17
  96.6 2.8 %collective-permute-done.18 = f16[2,192,128]{2,1,0:T(8,128)(2,1)S(1)} collective-permute-done((f16[2,192,128]{2,1,0:T(8,128)(2,1)S(1)}, f16[2,192,128]{2,1,0:T(8,128)(2,1)S(1)}, u32[]{:S(2)}, u32[]{:S(2)}) %collective-permute-start.18) | collective-permute-done | bytes 98336 | tf_op jit(solution)/shard_map/ppermute | solution.py:45
  99.4 0.0 copy-start.4
  99.4 0.1 fusion.7.first
  99.6 0.1 turn.1
  99.7 14.6 %all_to_all.10.got = f32[8,64,256]{2,1,0:T(8,128)S(1)} all-to-all(f32[8,64,256]{2,1,0:T(8,128)S(1)} %turn.1), channel_id=1, replica_groups=mesh['group'=2,'x'=4,'z'=8,'y'=2,'c'=2] {'group','y','c'}, dimensions={0} | all-to-all | bytes 1048576 | tf_op jit(solution)/shard_map/all_to_all | solution.py:292
  114.3 1.6 %final.1 = (f32[32,512]{1,0:T(8,128)}, f32[32,512]{1,0:T(8,128)}, bf16[64,512]{1,0:T(8,128)(2,1)}) custom-call(s32[1]{0:T(128)} %bitcast.group, f32[6]{0:T(128)} %reshape.19.facts, f32[8,64,256]{2,1,0:T(8,128)S(1)} %all_to_all.10.got, f32[64,512]{1,0:T(8,128)S(1)} %bitcast.65, f32[64,512]{1,0:T(8,128)S(1)} %bitcast.67, f32[64,512]{1,0:T(8,128)S(1)} %bitcast.69, ...), custom_call_target="tpu_custom_call" | custom-call | tf_op jit(solution)/shard_map/final/pallas_call | solution.py:296
  (31 shorter events, 0.2 us)
Async XLA Ops:
  10.5 10.5 %collective-permute-start.2 = (f32[8,4,2,64,128]{4,3,2,1,0:T(8,128)S(1)}, f32[8,4,2,64,128]{4,3,2,1,0:T(8,128)S(1)}, u32[]{:S(2)}, u32[]{:S(2)}) collective-permute-start(f32[8,4,2,64,128]{4,3,2,1,0:T(8,128)S(1)} %get-tuple-element.46), channel_id=1, source_target_pairs={{0,1},{1,0},{2,3},{3,2},{4,5},{5,4},{6,7},{7,6},{8,9},{9,8},{10,11... | collective-permute-start | bytes 6291464 | tf_op jit(solution)/shard_map/ppermute | solution.py:41
  13.8 6.0 %collective-permute-start = (f32[8,2,192,128]{3,2,1,0:T(8,128)S(1)}, f32[8,2,192,128]{3,2,1,0:T(8,128)S(1)}, u32[]{:S(2)}, u32[]{:S(2)}) collective-permute-start(f32[8,2,192,128]{3,2,1,0:T(8,128)S(1)} %get-tuple-element.44), channel_id=1, source_target_pairs={{0,1},{1,0},{2,3},{3,2},{4,5},{5,4},{6,7},{7,6},{8,9},{9,8},{10,11... | collective-permute-start | bytes 4718600 | tf_op jit(solution)/shard_map/ppermute | solution.py:41
  13.9 18.5 %collective-permute-start.3 = (f32[8,2,192,128]{3,2,1,0:T(8,128)}, f32[8,2,192,128]{3,2,1,0:T(8,128)}, u32[]{:S(2)}, u32[]{:S(2)}) collective-permute-start(f32[8,2,192,128]{3,2,1,0:T(8,128)} %get-tuple-element.50), channel_id=1, source_target_pairs={{0,1},{1,0},{2,3},{3,2},{4,5},{5,4},{6,7},{7,6},{8,9},{9,8},{10,11... | collective-permute-start | bytes 4718600 | tf_op jit(solution)/shard_map/ppermute | solution.py:41
  14.3 20.5 %collective-permute-start.5 = (f32[8,2,192,128]{3,2,1,0:T(8,128)}, f32[8,2,192,128]{3,2,1,0:T(8,128)}, u32[]{:S(2)}, u32[]{:S(2)}) collective-permute-start(f32[8,2,192,128]{3,2,1,0:T(8,128)} %get-tuple-element.54), channel_id=1, source_target_pairs={{0,1},{1,0},{2,3},{3,2},{4,5},{5,4},{6,7},{7,6},{8,9},{9,8},{10,11... | collective-permute-start | bytes 4718600 | tf_op jit(solution)/shard_map/ppermute | solution.py:41
  22.4 45.3 %all-to-all-start = ((f16[8,4,2,64,128]{4,3,2,1,0:T(8,128)(2,1)}), f16[8,4,2,64,128]{4,3,2,1,0:T(8,128)(2,1)}, u32[]{:S(2)}, u32[]{:S(2)}) async-start(f16[8,4,2,64,128]{4,3,2,1,0:T(8,128)(2,1)} %add_convert_fusion), calls=%async_computation | async-start | bytes 2097152 | tf_op jit(solution)/shard_map/all_to_all | solution.py:245
  28.9 38.8 %collective-permute-start.8 = (f32[8,2,192,128]{3,2,1,0:T(8,128)}, f32[8,2,192,128]{3,2,1,0:T(8,128)}, u32[]{:S(2)}, u32[]{:S(2)}) collective-permute-start(f32[8,2,192,128]{3,2,1,0:T(8,128)} %get-tuple-element.64), channel_id=1, source_target_pairs={{0,1},{1,0},{2,3},{3,2},{4,5},{5,4},{6,7},{7,6},{8,9},{9,8},{10,11... | collective-permute-start | bytes 4718600 | tf_op jit(solution)/shard_map/ppermute | solution.py:41
  29.6 20.9 %collective-permute-start.1 = (f16[8,2,192,128]{3,2,1,0:T(8,128)(2,1)}, f16[8,2,192,128]{3,2,1,0:T(8,128)(2,1)}, u32[]{:S(2)}, u32[]{:S(2)}) collective-permute-start(f16[8,2,192,128]{3,2,1,0:T(8,128)(2,1)} %add_convert_fusion.3), channel_id=1, source_target_pairs={{0,64},{32,96},{64,0},{96,32},{1,65},{33,97},{65,1},{97,33},{2,66}... | collective-permute-start | bytes 2359304 | tf_op jit(solution)/shard_map/ppermute | solution.py:45
  34.8 4.1 %copy-start.7 = (s32[2]{0:T(128)S(1)}, s32[2]{0:T(128)}, u32[]{:S(2)}) copy-start(s32[2]{0:T(128)} %param.15) | copy-start | bytes 28
  34.8 9.5 %copy-start.6 = (s32[2]{0:T(128)S(1)}, s32[2]{0:T(128)}, u32[]{:S(2)}) copy-start(s32[2]{0:T(128)} %param.14) | copy-start | bytes 28
  34.8 32.9 %copy-start.5 = (f32[8,2,192,128]{3,2,1,0:T(8,128)S(1)}, f32[8,2,192,128]{3,2,1,0:T(8,128)}, u32[]{:S(2)}) copy-start(f32[8,2,192,128]{3,2,1,0:T(8,128)} %get-tuple-element.63) | copy-start | bytes 4718596
  37.4 30.0 %collective-permute-start.6 = (f16[8,2,192,128]{3,2,1,0:T(8,128)(2,1)}, f16[8,2,192,128]{3,2,1,0:T(8,128)(2,1)S(1)}, u32[]{:S(2)}, u32[]{:S(2)}) collective-permute-start(f16[8,2,192,128]{3,2,1,0:T(8,128)(2,1)} %add_convert_fusion.1), channel_id=1, source_target_pairs={{0,96},{32,0},{64,32},{96,64},{1,97},{33,1},{65,33},{97,65},{2,98}... | collective-permute-start | bytes 2359304 | tf_op jit(solution)/shard_map/ppermute | solution.py:45
  38.3 29.4 %collective-permute-start.4 = (f16[8,2,192,128]{3,2,1,0:T(8,128)(2,1)}, f16[8,2,192,128]{3,2,1,0:T(8,128)(2,1)}, u32[]{:S(2)}, u32[]{:S(2)}) collective-permute-start(f16[8,2,192,128]{3,2,1,0:T(8,128)(2,1)} %add_convert_fusion.2), channel_id=1, source_target_pairs={{0,32},{32,64},{64,96},{96,0},{1,33},{33,65},{65,97},{97,1},{2,34}... | collective-permute-start | bytes 2359304 | tf_op jit(solution)/shard_map/ppermute | solution.py:45
  41.4 14.4 %collective-permute-start.7 = (f32[256,512]{1,0:T(8,128)}, f32[256,512]{1,0:T(8,128)S(1)}, u32[]{:S(2)}, u32[]{:S(2)}) collective-permute-start(f32[256,512]{1,0:T(8,128)} %pack.1), channel_id=1, source_target_pairs={{0,128},{128,0},{1,129},{129,1},{2,130},{130,2},{3,131},{131,3},{4... | collective-permute-start | bytes 1572872 | tf_op jit(solution)/shard_map/ppermute | solution.py:41
  70.4 19.8 %collective-permute-start.12 = (f16[2,192,128]{2,1,0:T(8,128)(2,1)S(1)}, f16[2,192,128]{2,1,0:T(8,128)(2,1)S(1)}, u32[]{:S(2)}, u32[]{:S(2)}) collective-permute-start(f16[2,192,128]{2,1,0:T(8,128)(2,1)S(1)} %get-tuple-element.91), channel_id=1, source_target_pairs={{0,16},{4,20},{8,24},{12,28},{16,0},{20,4},{24,8},{28,12},{1,17},{... | collective-permute-start | bytes 294920 | tf_op jit(solution)/shard_map/ppermute | solution.py:45
  76.3 14.2 %collective-permute-start.13 = (f16[2,192,128]{2,1,0:T(8,128)(2,1)S(1)}, f16[2,192,128]{2,1,0:T(8,128)(2,1)S(1)}, u32[]{:S(2)}, u32[]{:S(2)}) collective-permute-start(f16[2,192,128]{2,1,0:T(8,128)(2,1)S(1)} %get-tuple-element.90), channel_id=1, source_target_pairs={{0,12},{4,16},{8,20},{12,24},{16,28},{20,0},{24,4},{28,8},{1,13},{... | collective-permute-start | bytes 294920 | tf_op jit(solution)/shard_map/ppermute | solution.py:45
  78.1 4.3 %collective-permute-start.10 = (f16[2,64,128]{2,1,0:T(8,128)(2,1)S(1)}, f16[2,64,128]{2,1,0:T(8,128)(2,1)S(1)}, u32[]{:S(2)}, u32[]{:S(2)}) collective-permute-start(f16[2,64,128]{2,1,0:T(8,128)(2,1)S(1)} %get-tuple-element.95), channel_id=1, source_target_pairs={{0,32},{32,64},{64,96},{96,0},{1,33},{33,65},{65,97},{97,1},{2,34}... | collective-permute-start | bytes 98312 | tf_op jit(solution)/shard_map/ppermute | solution.py:45
  79.5 7.2 %collective-permute-start.11 = (f16[2,64,128]{2,1,0:T(8,128)(2,1)S(1)}, f16[2,64,128]{2,1,0:T(8,128)(2,1)S(1)}, u32[]{:S(2)}, u32[]{:S(2)}) collective-permute-start(f16[2,64,128]{2,1,0:T(8,128)(2,1)S(1)} %get-tuple-element.94), channel_id=1, source_target_pairs={{0,96},{32,0},{64,32},{96,64},{1,97},{33,1},{65,33},{97,65},{2,98}... | collective-permute-start | bytes 98312 | tf_op jit(solution)/shard_map/ppermute | solution.py:45
  80.9 6.0 %collective-permute-start.9 = (f16[2,64,128]{2,1,0:T(8,128)(2,1)S(1)}, f16[2,64,128]{2,1,0:T(8,128)(2,1)S(1)}, u32[]{:S(2)}, u32[]{:S(2)}) collective-permute-start(f16[2,64,128]{2,1,0:T(8,128)(2,1)S(1)} %get-tuple-element.96), channel_id=1, source_target_pairs={{0,64},{32,96},{64,0},{96,32},{1,65},{33,97},{65,1},{97,33},{2,66}... | collective-permute-start | bytes 98312 | tf_op jit(solution)/shard_map/ppermute | solution.py:45
  82.4 10.5 %collective-permute-start.14 = (f16[2,192,128]{2,1,0:T(8,128)(2,1)S(1)}, f16[2,192,128]{2,1,0:T(8,128)(2,1)S(1)}, u32[]{:S(2)}, u32[]{:S(2)}) collective-permute-start(f16[2,192,128]{2,1,0:T(8,128)(2,1)S(1)} %get-tuple-element.89), channel_id=1, source_target_pairs={{0,20},{4,24},{8,28},{12,0},{16,4},{20,8},{24,12},{28,16},{1,21},{... | collective-permute-start | bytes 294920 | tf_op jit(solution)/shard_map/ppermute | solution.py:45
  86.6 6.9 %collective-permute-start.15 = (f16[2,192,128]{2,1,0:T(8,128)(2,1)S(1)}, f16[2,192,128]{2,1,0:T(8,128)(2,1)S(1)}, u32[]{:S(2)}, u32[]{:S(2)}) collective-permute-start(f16[2,192,128]{2,1,0:T(8,128)(2,1)S(1)} %get-tuple-element.88), channel_id=1, source_target_pairs={{0,8},{4,12},{8,16},{12,20},{16,24},{20,28},{24,0},{28,4},{1,9},{5... | collective-permute-start | bytes 294920 | tf_op jit(solution)/shard_map/ppermute | solution.py:45
  86.9 9.6 %collective-permute-start.16 = (f16[2,192,128]{2,1,0:T(8,128)(2,1)S(1)}, f16[2,192,128]{2,1,0:T(8,128)(2,1)S(1)}, u32[]{:S(2)}, u32[]{:S(2)}) collective-permute-start(f16[2,192,128]{2,1,0:T(8,128)(2,1)S(1)} %get-tuple-element.87), channel_id=1, source_target_pairs={{0,24},{4,28},{8,0},{12,4},{16,8},{20,12},{24,16},{28,20},{1,25},{... | collective-permute-start | bytes 294920 | tf_op jit(solution)/shard_map/ppermute | solution.py:45
  90.2 6.4 %collective-permute-start.17 = (f16[2,192,128]{2,1,0:T(8,128)(2,1)S(1)}, f16[2,192,128]{2,1,0:T(8,128)(2,1)S(1)}, u32[]{:S(2)}, u32[]{:S(2)}) collective-permute-start(f16[2,192,128]{2,1,0:T(8,128)(2,1)S(1)} %get-tuple-element.86), channel_id=1, source_target_pairs={{0,4},{4,8},{8,12},{12,16},{16,20},{20,24},{24,28},{28,0},{1,5},{5... | collective-permute-start | bytes 294920 | tf_op jit(solution)/shard_map/ppermute | solution.py:45
  90.5 8.9 %collective-permute-start.18 = (f16[2,192,128]{2,1,0:T(8,128)(2,1)S(1)}, f16[2,192,128]{2,1,0:T(8,128)(2,1)S(1)}, u32[]{:S(2)}, u32[]{:S(2)}) collective-permute-start(f16[2,192,128]{2,1,0:T(8,128)(2,1)S(1)} %get-tuple-element.85), channel_id=1, source_target_pairs={{0,28},{4,0},{8,4},{12,8},{16,12},{20,16},{24,20},{28,24},{1,29},{... | collective-permute-start | bytes 294920 | tf_op jit(solution)/shard_map/ppermute | solution.py:45
  99.4 14.9 %copy-start = (f32[1,64,512]{2,1,0:T(8,128)S(1)}, f32[1,64,512]{2,1,0:T(8,128)}, u32[]{:S(2)}) copy-start(f32[1,64,512]{2,1,0:T(8,128)} %param.11) | copy-start | bytes 393220
  99.4 14.9 %copy-start.1 = (f32[1,64,512]{2,1,0:T(8,128)S(1)}, f32[1,64,512]{2,1,0:T(8,128)}, u32[]{:S(2)}) copy-start(f32[1,64,512]{2,1,0:T(8,128)} %param.12) | copy-start | bytes 393220
  99.4 14.9 %copy-start.2 = (f32[1,64,512]{2,1,0:T(8,128)S(1)}, f32[1,64,512]{2,1,0:T(8,128)}, u32[]{:S(2)}) copy-start(f32[1,64,512]{2,1,0:T(8,128)} %param.13) | copy-start | bytes 393220
  99.4 14.9 %copy-start.3 = (f32[32,512]{1,0:T(8,128)S(1)}, f32[32,512]{1,0:T(8,128)}, u32[]{:S(2)}) copy-start(f32[32,512]{1,0:T(8,128)} %a0.1) | copy-start | bytes 196612
  99.4 14.9 %copy-start.4 = (f32[32,512]{1,0:T(8,128)S(1)}, f32[32,512]{1,0:T(8,128)}, u32[]{:S(2)}) copy-start(f32[32,512]{1,0:T(8,128)} %w0.1) | copy-start | bytes 196612

commit v7 on v6

--- a/solution.py
+++ b/solution.py
@@ -27,7 +27,6 @@
 ROWS_A = 192
 LANES = 128
 BLOCK = 1024
-AHEAD = 4
 LIMIT = 28
 ORDER = (2, 1, 3, 0)
 FAR = (4, 3, 5, 2, 6, 1, 7)
@@ -51,7 +50,7 @@
     steps = acts.shape[1] // BLOCK
     per = steps // NX
     half = upstream.shape[1] // NC
-    turns = [n * per + i for n in (0, NX - 1, *range(1, NX - 1)) for i in range(per)]
+    turns = (0, NX - 1, *range(1, NX - 1))
     last = [
         pltpu.make_async_copy(kept.at[side], refs[NX - 1], left.at[side])
         if side == 0
@@ -59,39 +58,46 @@
         for side in range(NC)
     ]
 
-    def copy(i):
-        x = lax.rem(place[0] + ORDER[i // per], NX)
-        start = pl.multiple_of((x * per + i % per) * BLOCK, BLOCK)
+    def copy(n, b):
+        x = lax.rem(place[0] + ORDER[n], NX)
+        start = pl.multiple_of((x * per + b) * BLOCK, BLOCK)
         return pltpu.make_async_copy(
-            acts.at[:, pl.ds(start, BLOCK)], held.at[i], arrived.at[i]
+            acts.at[:, pl.ds(start, BLOCK)],
+            held.at[n * per + b],
+            arrived.at[n * per + b],
         )
 
     whole = pltpu.make_async_copy(cot, upstream, ready)
     whole.start()
-    for i in turns[:AHEAD]:
-        copy(i).start()
+    for b in range(per):
+        copy(turns[0], b).start()
     whole.wait()
     for side in range(NC):
         which = lax.rem(core[0] + 1 + side, NC)
         part = upstream[:, pl.ds(pl.multiple_of(which * half, half), half)]
         turned[side * half : (side + 1) * half] = part.astype(F32).T.astype(part.dtype)
-    for turn, i in enumerate(turns):
-        copy(i).wait()
-        if turn + AHEAD < steps:
-            copy(turns[turn + AHEAD]).start()
-        out = jnp.dot(turned[...], held[i], preferred_element_type=F32) * scale
-        n = i // per
-        for side, into in enumerate((theirs, own)):
-            rows_a = kept.at[side] if n == NX - 1 else into[n]
-            for j in range(BLOCK // LANES):
-                z, y = divmod(j, NY)
-                z += i % per * (NZ // per)
-                piece = out[
-                    side * half : (side + 1) * half, j * LANES : (j + 1) * LANES
-                ]
-                rows_a[lax.rem(z + NZ - layer[0], NZ), y] = piece[:ROWS_A]
-                into[NX][z, n, y] = piece[ROWS_A:]
-        if turn == 2 * per - 1:
+    for n in turns[1:]:
+        for b in range(per):
+            copy(n, b).start()
+    for n in turns:
+
+        @pl.loop(0, per)
+        def _(b):
+            copy(n, b).wait()
+            block = held[n * per + b]
+            out = jnp.dot(turned[...], block, preferred_element_type=F32) * scale
+            for side, into in enumerate((theirs, own)):
+                rows_a = kept.at[side] if n == NX - 1 else into[n]
+                for j in range(BLOCK // LANES):
+                    z, y = divmod(j, NY)
+                    z += b * (NZ // per)
+                    piece = out[
+                        side * half : (side + 1) * half, j * LANES : (j + 1) * LANES
+                    ]
+                    rows_a[lax.rem(z + NZ - layer[0], NZ), y] = piece[:ROWS_A]
+                    into[NX][z, n, y] = piece[ROWS_A:]
+
+        if n == NX - 1:
             for c in last:
                 c.start()
     for c in last:

time: 116 us -> 116 us (level)
  no operation moved by 1% of the time
where the time goes in v7:
time: 116 us; the launch traced here: 115 us
  starting transfers between devices  39.1 us (34%)
  waiting for transfers between devices  33.8 us (29%)
  blocking collectives  14.6 us (13%)
  other arithmetic  13.1 us (11%)
  Pallas kernels  12.9 us (11%)
    ppermute x13, starting transfers between devices, around(): return lax.ppermute(a, axis, [(i, (i + k) % size) for i in range(size)])  25.1 us
    ppermute x13, waiting for transfers between devices, around(): return lax.ppermute(a, axis, [(i, (i + k) % size) for i in range(size)])  23.1 us
    all_to_all x1, blocking collectives, per_device(): got = lax.all_to_all(part, ('group', 'y', 'c'), 0, 0, tiled=True)  14.6 us
    ppermute x6, waiting for transfers between devices, swap(): return lax.ppermute(a, axis, [(0, 1), (1, 0)])  10.8 us
    pallas_call x1, Pallas kernels, terms(): pl.pallas_call(functools.partial(terms_kernel, PEAK / (tokens * NC)), in_...  9.26 us
    ppermute x6, starting transfers between devices, swap(): return lax.ppermute(a, axis, [(0, 1), (1, 0)])  7.47 us
    all_to_all x1, starting transfers between devices, per_device(): back_b = lax.all_to_all(wire, 'z', 0, 0, tiled=True)  6.48 us
    convert_element_type x2, other arithmetic, per_device(): wire = (own + got).astype(WIRE)  5.09 us
  transfers between devices with their start and end apart: 20, of which 9 were waited for; matrix products, arithmetic and copies ran while one was open for 10% of the time, Pallas kernels for 2%

profile of v7, /device:TPU:1, one launch (start us, length us, event | category | flops | bytes accessed | tf_op | source)
XLA Modules:
  0.0 115.4 jit_solution(15847483533592523)
XLA Ops:
  0.6 9.3 %terms.1 = (f32[8,2,192,128]{3,2,1,0:T(8,128)S(1)}, f32[8,2,192,128]{3,2,1,0:T(8,128)}, f32[8,2,192,128]{3,2,1,0:T(8,128)}, f32[8,2,192,128]{3,2,1,0:T(8,128)}, ...) custom-call(s32[1]{0:T(128)} %bitcast.1.core, ...), custom_call_target="tpu_custom_call" | custom-call | flops 4294967296 | bytes 25165824 | tf_op jit(solution)/shard_map/terms/pallas_call | solution.py:114
  9.9 3.3 %collective-permute-start.2 = (f32[8,4,2,64,128]{4,3,2,1,0:T(8,128)S(1)}, f32[8,4,2,64,128]{4,3,2,1,0:T(8,128)S(1)}, u32[]{:S(2)}, u32[]{:S(2)}) collective-permute-start(f32[8,4,2,64,128]{4,3,2,1,0:T(8,128)S(1)} %get-tuple-element.46), channel_id=1, source_target_pairs={{0,1},{1,0},{2,3},{3,2},{4,5},{5,4},{6,7},{7,6},{8,9},{9,8},{10,11... | collective-permute-start | bytes 6291464 | tf_op jit(solution)/shard_map/ppermute | solution.py:40
  13.2 0.1 collective-permute-start
  13.3 0.4 collective-permute-start.3
  13.7 0.1 collective-permute-start.5
  13.8 5.4 %collective-permute-done = f32[8,2,192,128]{3,2,1,0:T(8,128)S(1)} collective-permute-done((f32[8,2,192,128]{3,2,1,0:T(8,128)S(1)}, f32[8,2,192,128]{3,2,1,0:T(8,128)S(1)}, u32[]{:S(2)}, u32[]{:S(2)}) %collective-permute-start) | collective-permute-done | bytes 1572896 | tf_op jit(solution)/shard_map/ppermute | solution.py:40
  19.2 1.1 add_convert_fusion.3
  20.4 1.5 %add_convert_fusion = f16[8,4,2,64,128]{4,3,2,1,0:T(8,128)(2,1)} fusion(f32[8,4,2,64,128]{4,3,2,1,0:T(8,128)S(1)} %get-tuple-element.47, f32[8,4,2,64,128]{4,3,2,1,0:T(8,128)S(1)} %collective-permute-done.2), kind=kLoop, calls=%fused_computation.1 | loop fusion | flops 1048576 | bytes 5242880 | tf_op jit(solution)/shard_map/convert_element_type | solution.py:250
  21.9 6.5 %all-to-all-start = ((f16[8,4,2,64,128]{4,3,2,1,0:T(8,128)(2,1)}), f16[8,4,2,64,128]{4,3,2,1,0:T(8,128)(2,1)}, u32[]{:S(2)}, u32[]{:S(2)}) async-start(f16[8,4,2,64,128]{4,3,2,1,0:T(8,128)(2,1)} %add_convert_fusion), calls=%async_computation | async-start | bytes 2097152 | tf_op jit(solution)/shard_map/all_to_all | solution.py:251
  28.3 0.7 collective-permute-start.8
  29.0 2.7 %collective-permute-start.1 = (f16[8,2,192,128]{3,2,1,0:T(8,128)(2,1)}, f16[8,2,192,128]{3,2,1,0:T(8,128)(2,1)}, u32[]{:S(2)}, u32[]{:S(2)}) collective-permute-start(f16[8,2,192,128]{3,2,1,0:T(8,128)(2,1)} %add_convert_fusion.3), channel_id=1, source_target_pairs={{0,64},{32,96},{64,0},{96,32},{1,65},{33,97},{65,1},{97,33},{2,66}... | collective-permute-start | bytes 2359304 | tf_op jit(solution)/shard_map/ppermute | solution.py:44
  31.7 2.5 %add_convert_fusion.2 = f16[8,2,192,128]{3,2,1,0:T(8,128)(2,1)} fusion(f32[8,2,192,128]{3,2,1,0:T(8,128)S(1)} %get-tuple-element.51, f32[8,2,192,128]{3,2,1,0:T(8,128)} %collective-permute-done.3), kind=kLoop, calls=%fused_computation.4 | loop fusion | flops 786432 | bytes 3932160 | tf_op jit(solution)/shard_map/convert_element_type | solution.py:255
  34.2 2.6 %add_convert_fusion.1 = f16[8,2,192,128]{3,2,1,0:T(8,128)(2,1)} fusion(f32[8,2,192,128]{3,2,1,0:T(8,128)S(1)} %get-tuple-element.55, f32[8,2,192,128]{3,2,1,0:T(8,128)} %collective-permute-done.5), kind=kLoop, calls=%fused_computation.3 | loop fusion | flops 786432 | bytes 3932160 | tf_op jit(solution)/shard_map/convert_element_type | solution.py:255
  36.8 0.9 collective-permute-start.6
  37.7 0.6 collective-permute-start.4
  38.3 0.6 convert_reduce_fusion.1
  38.9 1.9 %pack.1 = f32[256,512]{1,0:T(8,128)} custom-call(f32[64,512]{1,0:T(8,128)} %bitcast.64, f32[64,512]{1,0:T(8,128)} %bitcast.66, f32[64,512]{1,0:T(8,128)} %bitcast.68, f32[32,512]{1,0:T(8,128)} %a0.1, f32[32,512]{1,0:T(8,128)} %w0.1), custom_call_target="tpu_custom_call" | custom-call | tf_op jit(solution)/shard_map/pack/pallas_call | solution.py:258
  40.8 2.9 %collective-permute-start.7 = (f32[256,512]{1,0:T(8,128)}, f32[256,512]{1,0:T(8,128)S(1)}, u32[]{:S(2)}, u32[]{:S(2)}) collective-permute-start(f32[256,512]{1,0:T(8,128)} %pack.1), channel_id=1, source_target_pairs={{0,128},{128,0},{1,129},{129,1},{2,130},{130,2},{3,131},{131,3},{4... | collective-permute-start | bytes 1572872 | tf_op jit(solution)/shard_map/ppermute | solution.py:40
  43.7 0.7 subtract_bitcast_fusion.1
  44.4 0.1 rev.3
  44.5 0.1 copy.12
  44.6 0.7 reshape.19.facts
  45.3 4.6 %collective-permute-done.1 = f16[8,2,192,128]{3,2,1,0:T(8,128)(2,1)} collective-permute-done((f16[8,2,192,128]{3,2,1,0:T(8,128)(2,1)}, f16[8,2,192,128]{3,2,1,0:T(8,128)(2,1)}, u32[]{:S(2)}, u32[]{:S(2)}) %collective-permute-start.1) | collective-permute-done | bytes 786464 | tf_op jit(solution)/shard_map/ppermute | solution.py:44
  49.9 5.3 %collective-permute-done.7.far = f32[256,512]{1,0:T(8,128)S(1)} collective-permute-done((f32[256,512]{1,0:T(8,128)}, f32[256,512]{1,0:T(8,128)S(1)}, u32[]{:S(2)}, u32[]{:S(2)}) %collective-permute-start.7) | collective-permute-done | bytes 524320 | tf_op jit(solution)/shard_map/ppermute | solution.py:40
  55.2 11.6 %collective-permute-done.6 = f16[8,2,192,128]{3,2,1,0:T(8,128)(2,1)S(1)} collective-permute-done((f16[8,2,192,128]{3,2,1,0:T(8,128)(2,1)}, f16[8,2,192,128]{3,2,1,0:T(8,128)(2,1)S(1)}, u32[]{:S(2)}, u32[]{:S(2)}) %collective-permute-start.6) | collective-permute-done | bytes 786464 | tf_op jit(solution)/shard_map/ppermute | solution.py:44
  66.8 0.3 collective-permute-done.4
  67.2 2.5 %fusion.13 = (f16[8,2,192,128]{3,2,1,0:T(8,128)(2,1)S(1)}, f32[8,2,192,128]{3,2,1,0:T(8,128)S(1)}) fusion(f16[8,2,192,128]{3,2,1,0:T(8,128)(2,1)S(1)} %collective-permute-done.6, f16[8,2,192,128]{3,2,1,0:T(8,128)(2,1)} %collective-permute-done.4, f16[8,2,192,128]{3,2,1,0:T(8,128)(2,1)} %collective-permute-done.1, f32[8,2,192,128]{3,2,1,0:T(8,128)S(1)} %copy-done.5, ...), kind=kLoop, calls=%fused_computation.38 | loop fusion | flops 3538944 | bytes 7864320 | tf_op jit(solution)/shard_map/convert.6
  69.6 0.2 slice_bitcast_fusion.1
  69.8 5.7 %collective-permute-start.12 = (f16[2,192,128]{2,1,0:T(8,128)(2,1)S(1)}, f16[2,192,128]{2,1,0:T(8,128)(2,1)S(1)}, u32[]{:S(2)}, u32[]{:S(2)}) collective-permute-start(f16[2,192,128]{2,1,0:T(8,128)(2,1)S(1)} %get-tuple-element.91), channel_id=1, source_target_pairs={{0,16},{4,20},{8,24},{12,28},{16,0},{20,4},{24,8},{28,12},{1,17},{... | collective-permute-start | bytes 294920 | tf_op jit(solution)/shard_map/ppermute | solution.py:44
  75.6 0.3 collective-permute-start.13
  75.8 1.5 %convert_reduce_fusion = f32[4,2,64,128]{3,2,1,0:T(8,128)S(1)} fusion(f16[8,4,2,64,128]{4,3,2,1,0:T(8,128)(2,1)} %all-to-all-done), kind=kLoop, calls=%fused_computation | loop fusion | flops 983040 | bytes 1310720 | tf_op jit(solution)/shard_map/reduce_sum | solution.py:279
  77.4 1.5 %collective-permute-start.10 = (f16[2,64,128]{2,1,0:T(8,128)(2,1)S(1)}, f16[2,64,128]{2,1,0:T(8,128)(2,1)S(1)}, u32[]{:S(2)}, u32[]{:S(2)}) collective-permute-start(f16[2,64,128]{2,1,0:T(8,128)(2,1)S(1)} %get-tuple-element.95), channel_id=1, source_target_pairs={{0,32},{32,64},{64,96},{96,0},{1,33},{33,65},{65,97},{97,1},{2,34}... | collective-permute-start | bytes 98312 | tf_op jit(solution)/shard_map/ppermute | solution.py:44
  78.9 1.4 %collective-permute-start.11 = (f16[2,64,128]{2,1,0:T(8,128)(2,1)S(1)}, f16[2,64,128]{2,1,0:T(8,128)(2,1)S(1)}, u32[]{:S(2)}, u32[]{:S(2)}) collective-permute-start(f16[2,64,128]{2,1,0:T(8,128)(2,1)S(1)} %get-tuple-element.94), channel_id=1, source_target_pairs={{0,96},{32,0},{64,32},{96,64},{1,97},{33,1},{65,33},{97,65},{2,98}... | collective-permute-start | bytes 98312 | tf_op jit(solution)/shard_map/ppermute | solution.py:44
  80.3 1.5 %collective-permute-start.9 = (f16[2,64,128]{2,1,0:T(8,128)(2,1)S(1)}, f16[2,64,128]{2,1,0:T(8,128)(2,1)S(1)}, u32[]{:S(2)}, u32[]{:S(2)}) collective-permute-start(f16[2,64,128]{2,1,0:T(8,128)(2,1)S(1)} %get-tuple-element.96), channel_id=1, source_target_pairs={{0,64},{32,96},{64,0},{96,32},{1,65},{33,97},{65,1},{97,33},{2,66}... | collective-permute-start | bytes 98312 | tf_op jit(solution)/shard_map/ppermute | solution.py:44
  81.8 4.2 %collective-permute-start.14 = (f16[2,192,128]{2,1,0:T(8,128)(2,1)S(1)}, f16[2,192,128]{2,1,0:T(8,128)(2,1)S(1)}, u32[]{:S(2)}, u32[]{:S(2)}) collective-permute-start(f16[2,192,128]{2,1,0:T(8,128)(2,1)S(1)} %get-tuple-element.89), channel_id=1, source_target_pairs={{0,20},{4,24},{8,28},{12,0},{16,4},{20,8},{24,12},{28,16},{1,21},{... | collective-permute-start | bytes 294920 | tf_op jit(solution)/shard_map/ppermute | solution.py:44
  86.0 0.3 collective-permute-start.15
  86.3 3.3 %collective-permute-start.16 = (f16[2,192,128]{2,1,0:T(8,128)(2,1)S(1)}, f16[2,192,128]{2,1,0:T(8,128)(2,1)S(1)}, u32[]{:S(2)}, u32[]{:S(2)}) collective-permute-start(f16[2,192,128]{2,1,0:T(8,128)(2,1)S(1)} %get-tuple-element.87), channel_id=1, source_target_pairs={{0,24},{4,28},{8,0},{12,4},{16,8},{20,12},{24,16},{28,20},{1,25},{... | collective-permute-start | bytes 294920 | tf_op jit(solution)/shard_map/ppermute | solution.py:44
  89.6 0.3 collective-permute-start.17
  90.0 2.3 %collective-permute-start.18 = (f16[2,192,128]{2,1,0:T(8,128)(2,1)S(1)}, f16[2,192,128]{2,1,0:T(8,128)(2,1)S(1)}, u32[]{:S(2)}, u32[]{:S(2)}) collective-permute-start(f16[2,192,128]{2,1,0:T(8,128)(2,1)S(1)} %get-tuple-element.85), channel_id=1, source_target_pairs={{0,28},{4,0},{8,4},{12,8},{16,12},{20,16},{24,20},{28,24},{1,29},{... | collective-permute-start | bytes 294920 | tf_op jit(solution)/shard_map/ppermute | solution.py:44
  92.3 0.6 collective-permute-done.15
  92.9 3.0 %collective-permute-done.16 = f16[2,192,128]{2,1,0:T(8,128)(2,1)S(1)} collective-permute-done((f16[2,192,128]{2,1,0:T(8,128)(2,1)S(1)}, f16[2,192,128]{2,1,0:T(8,128)(2,1)S(1)}, u32[]{:S(2)}, u32[]{:S(2)}) %collective-permute-start.16) | collective-permute-done | bytes 98336 | tf_op jit(solution)/shard_map/ppermute | solution.py:44
  95.9 0.1 collective-permute-done.17
  96.0 2.8 %collective-permute-done.18 = f16[2,192,128]{2,1,0:T(8,128)(2,1)S(1)} collective-permute-done((f16[2,192,128]{2,1,0:T(8,128)(2,1)S(1)}, f16[2,192,128]{2,1,0:T(8,128)(2,1)S(1)}, u32[]{:S(2)}, u32[]{:S(2)}) %collective-permute-start.18) | collective-permute-done | bytes 98336 | tf_op jit(solution)/shard_map/ppermute | solution.py:44
  98.8 0.0 copy-start.4
  98.9 0.1 fusion.7.first
  99.0 0.1 turn.1
  99.1 14.6 %all_to_all.10.got = f32[8,64,256]{2,1,0:T(8,128)S(1)} all-to-all(f32[8,64,256]{2,1,0:T(8,128)S(1)} %turn.1), channel_id=1, replica_groups=mesh['group'=2,'x'=4,'z'=8,'y'=2,'c'=2] {'group','y','c'}, dimensions={0} | all-to-all | bytes 1048576 | tf_op jit(solution)/shard_map/all_to_all | solution.py:298
  113.8 1.6 %final.1 = (f32[32,512]{1,0:T(8,128)}, f32[32,512]{1,0:T(8,128)}, bf16[64,512]{1,0:T(8,128)(2,1)}) custom-call(s32[1]{0:T(128)} %bitcast.group, f32[6]{0:T(128)} %reshape.19.facts, f32[8,64,256]{2,1,0:T(8,128)S(1)} %all_to_all.10.got, f32[64,512]{1,0:T(8,128)S(1)} %bitcast.65, f32[64,512]{1,0:T(8,128)S(1)} %bitcast.67, f32[64,512]{1,0:T(8,128)S(1)} %bitcast.69, ...), custom_call_target="tpu_custom_call" | custom-call | tf_op jit(solution)/shard_map/final/pallas_call | solution.py:302
  (31 shorter events, 0.2 us)
Async XLA Ops:
  9.9 10.5 %collective-permute-start.2 = (f32[8,4,2,64,128]{4,3,2,1,0:T(8,128)S(1)}, f32[8,4,2,64,128]{4,3,2,1,0:T(8,128)S(1)}, u32[]{:S(2)}, u32[]{:S(2)}) collective-permute-start(f32[8,4,2,64,128]{4,3,2,1,0:T(8,128)S(1)} %get-tuple-element.46), channel_id=1, source_target_pairs={{0,1},{1,0},{2,3},{3,2},{4,5},{5,4},{6,7},{7,6},{8,9},{9,8},{10,11... | collective-permute-start | bytes 6291464 | tf_op jit(solution)/shard_map/ppermute | solution.py:40
  13.2 6.0 %collective-permute-start = (f32[8,2,192,128]{3,2,1,0:T(8,128)S(1)}, f32[8,2,192,128]{3,2,1,0:T(8,128)S(1)}, u32[]{:S(2)}, u32[]{:S(2)}) collective-permute-start(f32[8,2,192,128]{3,2,1,0:T(8,128)S(1)} %get-tuple-element.44), channel_id=1, source_target_pairs={{0,1},{1,0},{2,3},{3,2},{4,5},{5,4},{6,7},{7,6},{8,9},{9,8},{10,11... | collective-permute-start | bytes 4718600 | tf_op jit(solution)/shard_map/ppermute | solution.py:40
  13.3 18.5 %collective-permute-start.3 = (f32[8,2,192,128]{3,2,1,0:T(8,128)}, f32[8,2,192,128]{3,2,1,0:T(8,128)}, u32[]{:S(2)}, u32[]{:S(2)}) collective-permute-start(f32[8,2,192,128]{3,2,1,0:T(8,128)} %get-tuple-element.50), channel_id=1, source_target_pairs={{0,1},{1,0},{2,3},{3,2},{4,5},{5,4},{6,7},{7,6},{8,9},{9,8},{10,11... | collective-permute-start | bytes 4718600 | tf_op jit(solution)/shard_map/ppermute | solution.py:40
  13.7 20.5 %collective-permute-start.5 = (f32[8,2,192,128]{3,2,1,0:T(8,128)}, f32[8,2,192,128]{3,2,1,0:T(8,128)}, u32[]{:S(2)}, u32[]{:S(2)}) collective-permute-start(f32[8,2,192,128]{3,2,1,0:T(8,128)} %get-tuple-element.54), channel_id=1, source_target_pairs={{0,1},{1,0},{2,3},{3,2},{4,5},{5,4},{6,7},{7,6},{8,9},{9,8},{10,11... | collective-permute-start | bytes 4718600 | tf_op jit(solution)/shard_map/ppermute | solution.py:40
  21.9 45.3 %all-to-all-start = ((f16[8,4,2,64,128]{4,3,2,1,0:T(8,128)(2,1)}), f16[8,4,2,64,128]{4,3,2,1,0:T(8,128)(2,1)}, u32[]{:S(2)}, u32[]{:S(2)}) async-start(f16[8,4,2,64,128]{4,3,2,1,0:T(8,128)(2,1)} %add_convert_fusion), calls=%async_computation | async-start | bytes 2097152 | tf_op jit(solution)/shard_map/all_to_all | solution.py:251
  28.3 38.8 %collective-permute-start.8 = (f32[8,2,192,128]{3,2,1,0:T(8,128)}, f32[8,2,192,128]{3,2,1,0:T(8,128)}, u32[]{:S(2)}, u32[]{:S(2)}) collective-permute-start(f32[8,2,192,128]{3,2,1,0:T(8,128)} %get-tuple-element.64), channel_id=1, source_target_pairs={{0,1},{1,0},{2,3},{3,2},{4,5},{5,4},{6,7},{7,6},{8,9},{9,8},{10,11... | collective-permute-start | bytes 4718600 | tf_op jit(solution)/shard_map/ppermute | solution.py:40
  29.0 20.9 %collective-permute-start.1 = (f16[8,2,192,128]{3,2,1,0:T(8,128)(2,1)}, f16[8,2,192,128]{3,2,1,0:T(8,128)(2,1)}, u32[]{:S(2)}, u32[]{:S(2)}) collective-permute-start(f16[8,2,192,128]{3,2,1,0:T(8,128)(2,1)} %add_convert_fusion.3), channel_id=1, source_target_pairs={{0,64},{32,96},{64,0},{96,32},{1,65},{33,97},{65,1},{97,33},{2,66}... | collective-permute-start | bytes 2359304 | tf_op jit(solution)/shard_map/ppermute | solution.py:44
  34.2 4.1 %copy-start.7 = (s32[2]{0:T(128)S(1)}, s32[2]{0:T(128)}, u32[]{:S(2)}) copy-start(s32[2]{0:T(128)} %param.15) | copy-start | bytes 28
  34.2 9.5 %copy-start.6 = (s32[2]{0:T(128)S(1)}, s32[2]{0:T(128)}, u32[]{:S(2)}) copy-start(s32[2]{0:T(128)} %param.14) | copy-start | bytes 28
  34.2 32.9 %copy-start.5 = (f32[8,2,192,128]{3,2,1,0:T(8,128)S(1)}, f32[8,2,192,128]{3,2,1,0:T(8,128)}, u32[]{:S(2)}) copy-start(f32[8,2,192,128]{3,2,1,0:T(8,128)} %get-tuple-element.63) | copy-start | bytes 4718596
  36.8 30.0 %collective-permute-start.6 = (f16[8,2,192,128]{3,2,1,0:T(8,128)(2,1)}, f16[8,2,192,128]{3,2,1,0:T(8,128)(2,1)S(1)}, u32[]{:S(2)}, u32[]{:S(2)}) collective-permute-start(f16[8,2,192,128]{3,2,1,0:T(8,128)(2,1)} %add_convert_fusion.1), channel_id=1, source_target_pairs={{0,96},{32,0},{64,32},{96,64},{1,97},{33,1},{65,33},{97,65},{2,98}... | collective-permute-start | bytes 2359304 | tf_op jit(solution)/shard_map/ppermute | solution.py:44
  37.7 29.4 %collective-permute-start.4 = (f16[8,2,192,128]{3,2,1,0:T(8,128)(2,1)}, f16[8,2,192,128]{3,2,1,0:T(8,128)(2,1)}, u32[]{:S(2)}, u32[]{:S(2)}) collective-permute-start(f16[8,2,192,128]{3,2,1,0:T(8,128)(2,1)} %add_convert_fusion.2), channel_id=1, source_target_pairs={{0,32},{32,64},{64,96},{96,0},{1,33},{33,65},{65,97},{97,1},{2,34}... | collective-permute-start | bytes 2359304 | tf_op jit(solution)/shard_map/ppermute | solution.py:44
  40.8 14.4 %collective-permute-start.7 = (f32[256,512]{1,0:T(8,128)}, f32[256,512]{1,0:T(8,128)S(1)}, u32[]{:S(2)}, u32[]{:S(2)}) collective-permute-start(f32[256,512]{1,0:T(8,128)} %pack.1), channel_id=1, source_target_pairs={{0,128},{128,0},{1,129},{129,1},{2,130},{130,2},{3,131},{131,3},{4... | collective-permute-start | bytes 1572872 | tf_op jit(solution)/shard_map/ppermute | solution.py:40
  69.8 19.8 %collective-permute-start.12 = (f16[2,192,128]{2,1,0:T(8,128)(2,1)S(1)}, f16[2,192,128]{2,1,0:T(8,128)(2,1)S(1)}, u32[]{:S(2)}, u32[]{:S(2)}) collective-permute-start(f16[2,192,128]{2,1,0:T(8,128)(2,1)S(1)} %get-tuple-element.91), channel_id=1, source_target_pairs={{0,16},{4,20},{8,24},{12,28},{16,0},{20,4},{24,8},{28,12},{1,17},{... | collective-permute-start | bytes 294920 | tf_op jit(solution)/shard_map/ppermute | solution.py:44
  75.6 14.4 %collective-permute-start.13 = (f16[2,192,128]{2,1,0:T(8,128)(2,1)S(1)}, f16[2,192,128]{2,1,0:T(8,128)(2,1)S(1)}, u32[]{:S(2)}, u32[]{:S(2)}) collective-permute-start(f16[2,192,128]{2,1,0:T(8,128)(2,1)S(1)} %get-tuple-element.90), channel_id=1, source_target_pairs={{0,12},{4,16},{8,20},{12,24},{16,28},{20,0},{24,4},{28,8},{1,13},{... | collective-permute-start | bytes 294920 | tf_op jit(solution)/shard_map/ppermute | solution.py:44
  77.4 4.5 %collective-permute-start.10 = (f16[2,64,128]{2,1,0:T(8,128)(2,1)S(1)}, f16[2,64,128]{2,1,0:T(8,128)(2,1)S(1)}, u32[]{:S(2)}, u32[]{:S(2)}) collective-permute-start(f16[2,64,128]{2,1,0:T(8,128)(2,1)S(1)} %get-tuple-element.95), channel_id=1, source_target_pairs={{0,32},{32,64},{64,96},{96,0},{1,33},{33,65},{65,97},{97,1},{2,34}... | collective-permute-start | bytes 98312 | tf_op jit(solution)/shard_map/ppermute | solution.py:44
  78.9 7.2 %collective-permute-start.11 = (f16[2,64,128]{2,1,0:T(8,128)(2,1)S(1)}, f16[2,64,128]{2,1,0:T(8,128)(2,1)S(1)}, u32[]{:S(2)}, u32[]{:S(2)}) collective-permute-start(f16[2,64,128]{2,1,0:T(8,128)(2,1)S(1)} %get-tuple-element.94), channel_id=1, source_target_pairs={{0,96},{32,0},{64,32},{96,64},{1,97},{33,1},{65,33},{97,65},{2,98}... | collective-permute-start | bytes 98312 | tf_op jit(solution)/shard_map/ppermute | solution.py:44
  80.3 6.0 %collective-permute-start.9 = (f16[2,64,128]{2,1,0:T(8,128)(2,1)S(1)}, f16[2,64,128]{2,1,0:T(8,128)(2,1)S(1)}, u32[]{:S(2)}, u32[]{:S(2)}) collective-permute-start(f16[2,64,128]{2,1,0:T(8,128)(2,1)S(1)} %get-tuple-element.96), channel_id=1, source_target_pairs={{0,64},{32,96},{64,0},{96,32},{1,65},{33,97},{65,1},{97,33},{2,66}... | collective-permute-start | bytes 98312 | tf_op jit(solution)/shard_map/ppermute | solution.py:44
  81.8 10.5 %collective-permute-start.14 = (f16[2,192,128]{2,1,0:T(8,128)(2,1)S(1)}, f16[2,192,128]{2,1,0:T(8,128)(2,1)S(1)}, u32[]{:S(2)}, u32[]{:S(2)}) collective-permute-start(f16[2,192,128]{2,1,0:T(8,128)(2,1)S(1)} %get-tuple-element.89), channel_id=1, source_target_pairs={{0,20},{4,24},{8,28},{12,0},{16,4},{20,8},{24,12},{28,16},{1,21},{... | collective-permute-start | bytes 294920 | tf_op jit(solution)/shard_map/ppermute | solution.py:44
  86.0 6.9 %collective-permute-start.15 = (f16[2,192,128]{2,1,0:T(8,128)(2,1)S(1)}, f16[2,192,128]{2,1,0:T(8,128)(2,1)S(1)}, u32[]{:S(2)}, u32[]{:S(2)}) collective-permute-start(f16[2,192,128]{2,1,0:T(8,128)(2,1)S(1)} %get-tuple-element.88), channel_id=1, source_target_pairs={{0,8},{4,12},{8,16},{12,20},{16,24},{20,28},{24,0},{28,4},{1,9},{5... | collective-permute-start | bytes 294920 | tf_op jit(solution)/shard_map/ppermute | solution.py:44
  86.3 9.6 %collective-permute-start.16 = (f16[2,192,128]{2,1,0:T(8,128)(2,1)S(1)}, f16[2,192,128]{2,1,0:T(8,128)(2,1)S(1)}, u32[]{:S(2)}, u32[]{:S(2)}) collective-permute-start(f16[2,192,128]{2,1,0:T(8,128)(2,1)S(1)} %get-tuple-element.87), channel_id=1, source_target_pairs={{0,24},{4,28},{8,0},{12,4},{16,8},{20,12},{24,16},{28,20},{1,25},{... | collective-permute-start | bytes 294920 | tf_op jit(solution)/shard_map/ppermute | solution.py:44
  89.6 6.4 %collective-permute-start.17 = (f16[2,192,128]{2,1,0:T(8,128)(2,1)S(1)}, f16[2,192,128]{2,1,0:T(8,128)(2,1)S(1)}, u32[]{:S(2)}, u32[]{:S(2)}) collective-permute-start(f16[2,192,128]{2,1,0:T(8,128)(2,1)S(1)} %get-tuple-element.86), channel_id=1, source_target_pairs={{0,4},{4,8},{8,12},{12,16},{16,20},{20,24},{24,28},{28,0},{1,5},{5... | collective-permute-start | bytes 294920 | tf_op jit(solution)/shard_map/ppermute | solution.py:44
  90.0 8.8 %collective-permute-start.18 = (f16[2,192,128]{2,1,0:T(8,128)(2,1)S(1)}, f16[2,192,128]{2,1,0:T(8,128)(2,1)S(1)}, u32[]{:S(2)}, u32[]{:S(2)}) collective-permute-start(f16[2,192,128]{2,1,0:T(8,128)(2,1)S(1)} %get-tuple-element.85), channel_id=1, source_target_pairs={{0,28},{4,0},{8,4},{12,8},{16,12},{20,16},{24,20},{28,24},{1,29},{... | collective-permute-start | bytes 294920 | tf_op jit(solution)/shard_map/ppermute | solution.py:44
  98.8 14.9 %copy-start = (f32[1,64,512]{2,1,0:T(8,128)S(1)}, f32[1,64,512]{2,1,0:T(8,128)}, u32[]{:S(2)}) copy-start(f32[1,64,512]{2,1,0:T(8,128)} %param.11) | copy-start | bytes 393220
  98.8 14.9 %copy-start.1 = (f32[1,64,512]{2,1,0:T(8,128)S(1)}, f32[1,64,512]{2,1,0:T(8,128)}, u32[]{:S(2)}) copy-start(f32[1,64,512]{2,1,0:T(8,128)} %param.12) | copy-start | bytes 393220
  98.8 14.9 %copy-start.2 = (f32[1,64,512]{2,1,0:T(8,128)S(1)}, f32[1,64,512]{2,1,0:T(8,128)}, u32[]{:S(2)}) copy-start(f32[1,64,512]{2,1,0:T(8,128)} %param.13) | copy-start | bytes 393220
  98.8 14.9 %copy-start.3 = (f32[32,512]{1,0:T(8,128)S(1)}, f32[32,512]{1,0:T(8,128)}, u32[]{:S(2)}) copy-start(f32[32,512]{1,0:T(8,128)} %a0.1) | copy-start | bytes 196612
  98.8 14.9 %copy-start.4 = (f32[32,512]{1,0:T(8,128)S(1)}, f32[32,512]{1,0:T(8,128)}, u32[]{:S(2)}) copy-start(f32[32,512]{1,0:T(8,128)} %w0.1) | copy-start | bytes 196612
